TPU v7x, 256 devices: a whole 4x4x8 slice. The times are simulated.
256 devices in a mesh: seq: 32 (over y, x, core), tp: 8 (over z).
Axes of the slice: x: 4, y: 4, z: 8, core: 2. Of those that a mesh axis runs over, the one named last changes fastest.
Arguments:
- hidden_in: bfloat16 [2, 16384, 2560], P(None, 'seq'), may hold values from -6 to 6
- gate_proj: bfloat16 [2560, 5120], P(None, 'tp'), may hold values from -0.125 to 0.125
- value_proj: bfloat16 [2560, 5120], P(None, 'tp'), may hold values from -0.125 to 0.125
- bc_proj: bfloat16 [2560, 256], P(None, 'tp'), may hold values from -0.125 to 0.125
- step_proj: bfloat16 [2560, 80], P(None, 'tp'), may hold values from -0.125 to 0.125
- value_conv: float32 [4, 5120], P(None, 'tp'), may hold values from -3 to 3
- bc_conv: float32 [4, 256], replicated, may hold values from -3 to 3
- step_bias: float32 [80], P('tp'), may hold values from -1.5 to 0
- log_rate: float32 [80], P('tp'), as said below
- norm_gain: float32 [5120], P('tp'), may hold values from 0.25 to 1.75
Outputs:
- mixer_out: bfloat16 [2, 16384, 5120], P(None, 'seq', 'tp')
Inputs may be any that keep to these rules, and one draw needn't show every extreme that they name: log_rate lies between -1.5 - ln(16384) and 1.0 - ln(16384).
All inputs are finite; a program needn't handle non-finite values.
Results may differ from a plain program's by a relative error of at most 0.0095.
Values may be sent and summed in bfloat16 or wider, within the bound.
No kernel may reach another device: no remote copies, remote signals or barrier semaphores. Data moves between devices by JAX's collectives and lax.ppermute only.
A program may use at most 128 MiB of HBM per device.

v0:
```python
import jax
import jax.numpy as jnp
from jax import lax
from jax.sharding import Mesh
from jax.sharding import PartitionSpec as P

DI = 5120
HEAD_DIM = 64
STATE = 128
CONV = 4
BLOCK = 64
SEQ = ("seq_0", "seq_1", "seq_2")


epsilon = 1e-05


def passed_along(block, axis, distance):
    devices = range(lax.axis_size(axis))
    route = [(i - distance, i) for i in devices if i - distance in devices]
    return lax.ppermute(block, axis, route)


def filled_with(x, identity):
    return jax.tree.map(
        lambda part, zero: jnp.zeros_like(part) + jnp.asarray(zero, part.dtype), x, identity
    )


def entering(x, axes, combine, identity, reverse):
    before = start = filled_with(x, identity)
    so_far = x
    for axis in reversed(axes):
        length, index = lax.axis_size(axis), lax.axis_index(axis)
        pieces = jax.tree.map(lambda part: lax.all_gather(part, axis), so_far)
        inside, so_far = start, start
        for k in reversed(range(length)) if reverse else range(length):
            passed = k > index if reverse else k < index
            so_far = combine(so_far, jax.tree.map(lambda part: part[k], pieces))
            inside = jax.tree.map(lambda new, old: jnp.where(passed, new, old), so_far, inside)
        before = combine(inside, before)
    return before


def conv_silu(padded, kernel, length):
    running = jnp.zeros((padded.shape[0], length, padded.shape[2]), jnp.float32)
    for tap_index in range(kernel.shape[0]):
        running = running + kernel[tap_index] * padded[:, tap_index : tap_index + length, :]
    return jax.nn.silu(running)


def block_step(carried, inputs):
    values, log_decay, step_sizes, b_rows, c_rows = inputs
    length = log_decay.shape[1]
    cumulative = jnp.cumsum(log_decay, axis=1)
    log_gap = cumulative[:, :, None, :] - cumulative[:, None, :, :]
    causal = jnp.arange(length)[:, None] >= jnp.arange(length)[None, :]
    weights_in = jnp.exp(jnp.where(causal[None, :, :, None], log_gap, -jnp.inf))
    scores = jnp.einsum("bin,bjn->bij", c_rows, b_rows, precision=lax.Precision.HIGHEST)
    mixing = scores[:, :, :, None] * weights_in * step_sizes[:, None, :, :]
    within = jnp.einsum("bijh,bjhp->bihp", mixing, values, precision=lax.Precision.HIGHEST)
    earlier = jnp.einsum("bin,bhpn->bihp", c_rows, carried, precision=lax.Precision.HIGHEST)
    earlier = earlier * jnp.exp(cumulative)[..., None]
    remain = jnp.exp(cumulative[:, -1:, :] - cumulative) * step_sizes
    added_state = jnp.einsum(
        "bjh,bjhp,bjn->bhpn", remain, values, b_rows, precision=lax.Precision.HIGHEST
    )
    updated = jnp.exp(cumulative[:, -1, :])[:, :, None, None] * carried + added_state
    return (updated, within + earlier)


def to_blocks(series, batch_size, blocks):
    return jnp.moveaxis(series.reshape((batch_size, blocks, BLOCK) + series.shape[2:]), 1, 0)


def combine(earlier, latter):
    return (earlier[0] * latter[0], latter[0][:, :, None, None] * earlier[1] + latter[1])


def on_device(
    hidden_in,
    gate_proj,
    value_proj,
    bc_proj,
    step_proj,
    value_conv,
    bc_conv,
    step_bias,
    log_rate,
    norm_gain,
):
    batch_size, length, model_width = hidden_in.shape
    heads_here = step_proj.shape[1]
    inner_here = value_proj.shape[1]
    flat_rows = hidden_in.reshape(-1, model_width)
    gate_pre = jnp.dot(flat_rows, gate_proj, preferred_element_type=jnp.float32).astype(
        jnp.bfloat16
    )
    value_pre = jnp.dot(flat_rows, value_proj, preferred_element_type=jnp.float32).astype(
        jnp.bfloat16
    )
    step_pre = jnp.dot(flat_rows, step_proj, preferred_element_type=jnp.float32)
    bc_part = jnp.dot(flat_rows, bc_proj, preferred_element_type=jnp.float32).astype(jnp.bfloat16)
    bc_pre = lax.all_gather(bc_part, "tp", axis=1, tiled=True)
    joined = jnp.concatenate([value_pre, bc_pre], axis=1).reshape(batch_size, length, -1)
    tail_rows = joined[:, length - (CONV - 1) :, :]
    before = passed_along(tail_rows, SEQ, 1)
    padded = jnp.concatenate([before, joined], axis=1).astype(jnp.float32)
    kernel = jnp.concatenate([value_conv, bc_conv], axis=1)
    mixed_in = conv_silu(padded, kernel, length)
    values = mixed_in[..., :inner_here].reshape(batch_size, length, heads_here, HEAD_DIM)
    b_rows = mixed_in[..., inner_here : inner_here + STATE]
    c_rows = mixed_in[..., inner_here + STATE :]
    step_sizes = jax.nn.softplus(step_pre.reshape(batch_size, length, heads_here) + step_bias)
    log_decay = -step_sizes * jnp.exp(log_rate)
    blocks = length // BLOCK
    initial = jnp.zeros((batch_size, heads_here, HEAD_DIM, STATE), jnp.float32)
    local_state, outputs = lax.scan(
        block_step,
        initial,
        (
            to_blocks(values, batch_size, blocks),
            to_blocks(log_decay, batch_size, blocks),
            to_blocks(step_sizes, batch_size, blocks),
            to_blocks(b_rows, batch_size, blocks),
            to_blocks(c_rows, batch_size, blocks),
        ),
    )
    within = jnp.moveaxis(outputs, 0, 1).reshape(batch_size, length, heads_here, HEAD_DIM)
    cumulative = jnp.cumsum(log_decay, axis=1)
    decays = jnp.exp(cumulative[:, -1, :])
    arrived = entering(
        (decays, local_state),
        SEQ,
        combine,
        (jnp.ones_like(decays), jnp.zeros_like(local_state)),
        False,
    )[1]
    correction = jnp.einsum("btn,bhpn->bthp", c_rows, arrived, precision=lax.Precision.HIGHEST)
    correction = correction * jnp.exp(cumulative)[..., None]
    mixed_out = (within + correction).reshape(batch_size, length, inner_here)
    gated_out = mixed_out * jax.nn.silu(
        gate_pre.reshape(batch_size, length, inner_here).astype(jnp.float32)
    )
    squares = jnp.sum(gated_out * gated_out, axis=-1, keepdims=True)
    whole_sq = lax.psum(squares, "tp")
    return (gated_out * lax.rsqrt(whole_sq / DI + epsilon) * norm_gain).astype(jnp.bfloat16)


def solution(mesh):
    split = Mesh(mesh.devices.reshape(4, 4, 2, mesh.shape["tp"]), ("seq_0", "seq_1", "seq_2", "tp"))
    placed = (
        P(None, SEQ, None),
        P(None, "tp"),
        P(None, "tp"),
        P(None, "tp"),
        P(None, "tp"),
        P(None, "tp"),
        P(),
        P("tp"),
        P("tp"),
        P("tp"),
    )
    return jax.shard_map(
        on_device, mesh=split, in_specs=placed, out_specs=P(None, SEQ, "tp"), check_vma=False
    )
```

profile of v0, /device:TPU:1, one launch (start us, length us, event | category | flops | bytes accessed | tf_op | source)
XLA Modules:
  0.0 266.5 jit_solution(15965139563152484885)
XLA Ops:
  6.5 1.9 copy-done
  8.5 6.2 %convolution_convert_fusion.1 = bf16[1024,640]{0,1:T(8,128)(2,1)S(1)} fusion(bf16[1024,2560]{1,0:T(8,128)(2,1)} %bitcast.229, bf16[2560,640]{1,0:T(8,128)(2,1)S(1)} %copy-done), kind=kOutput, calls=%fused_computation.57 | convolution fusion | flops 3356098560 | bytes 9830400 | tf_op jit(solution)/shard_map/dot_general | solution.py:99
  14.7 1.6 convolution_convert_fusion.2
  16.3 23.7 %all_gather.29 = bf16[1024,256]{0,1:T(8,128)(2,1)S(1)} all-gather(bf16[1024,32]{0,1:T(8,128)(2,1)S(1)} %convolution_convert_fusion.2), channel_id=1, replica_groups=mesh['seq_0'=4,'seq_1'=4,'seq_2'=2,'tp'=8] {'tp'}, dimensions={1}, use_global_device_ids=true | all-gather | bytes 589824 | tf_op jit(solution)/shard_map/all_gather | solution.py:104
  40.1 1.4 pad_maximum_fusion
  41.5 3.1 %copy.121 = bf16[1024,896]{1,0:T(8,128)(2,1)S(1)} copy(bf16[1024,896]{0,1:T(8,128)(2,1)} %pad_maximum_fusion) | data formatting | bytes 3670016 | tf_op jit(solution)/shard_map/reshape | solution.py:105
  44.6 10.1 %collective-permute-start = (bf16[2,3,896]{2,1,0:T(4,128)(2,1)S(1)}, bf16[2,3,896]{2,1,0:T(4,128)(2,1)S(1)}, u32[]{:S(2)}, u32[]{:S(2)}) collective-permute-start(bf16[2,3,896]{2,1,0:T(4,128)(2,1)S(1)} %slice.155), channel_id=1, source_target_pairs={{0,8},{8,16},{16,24},{24,32},{32,40},{40,48},{48,56},{56,64},{64,7... | collective-permute-start | bytes 32264 | tf_op jit(solution)/shard_map/ppermute | solution.py:21
  54.7 4.0 %fusion.102 = (f32[2,10,512]{2,1,0:T(8,128)S(1)}, f32[2,512,10]{1,2,0:T(8,128)S(1)}) fusion(f32[10]{0:T(128)S(1)} %exp.58, f32[10]{0:T(128)S(1)} %copy-done.14, bf16[2,512,2560]{2,1,0:T(8,128)(2,1)} %param.12, bf16[2560,10]{0,1:T(8,128)(2,1)S(1)} %copy-done.10), kind=kOutput, calls=%fused_computation.135 | convolution fusion | flops 52520960 | bytes 5376080 | tf_op jit(solution)/shard_map/dot_general | solution.py:102
  59.5 2.2 divide_multiply_fusion
  61.7 1.2 fusion.111
  62.9 1.0 copy-done.4
  64.1 2.1 copy.96
  66.2 4.9 %reshape_reshape.3 = f32[2,8,64,10,64]{2,1,4,3,0:T(8,128)} reshape(f32[2,512,640]{1,2,0:T(8,128)} %copy.96) | data formatting | bytes 5242880 | tf_op jit(solution)/shard_map/reshape;reshape | solution.py:73
  71.2 62.0 %while.13 = (s32[]{:T(128)}, f32[2,10,64,128]{3,2,1,0:T(8,128)S(1)}, f32[8,2,64,10,64]{2,4,3,1,0:T(8,128)}, f32[8,2,64,10]{2,0,1,3:T(8,128)S(1)}, f32[8,2,64,10]...) while((s32[]{:T(128)}, ...), condition=%wide.region_2.3_spmd.clone, body=%wide.region_0.2_spmd.clone.sunk | while | flops 328471808 | bytes 6140956 | solution.py:118
  72.7 3.1 %constant_dynamic-slice_fusion.5 = f32[1,2,64,10,64]{2,0,4,3,1:T(1,128)S(1)} fusion(f32[8,2,64,10,64]{2,0,4,3,1:T(8,128)} %get-tuple-element.235, s32[]{:T(128)} %get-tuple-element.219), kind=kLoop, calls=%fused_computation.37.clone.1 | loop fusion | bytes 655364 | tf_op jit(solution)/shard_map/while/body/jit(dynamic_index_in_dim)/dynamic_slice | solution.py:118
  75.8 2.2 fusion.141
  78.2 0.9 convolution_add_fusion.3
  80.5 3.1 %constant_dynamic-slice_fusion.5 = f32[1,2,64,10,64]{2,0,4,3,1:T(1,128)S(1)} fusion(f32[8,2,64,10,64]{2,0,4,3,1:T(8,128)} %get-tuple-element.235, s32[]{:T(128)} %get-tuple-element.219), kind=kLoop, calls=%fused_computation.37.clone.1 | loop fusion | bytes 655364 | tf_op jit(solution)/shard_map/while/body/jit(dynamic_index_in_dim)/dynamic_slice | solution.py:118
  83.6 2.2 fusion.141
  88.2 3.1 %constant_dynamic-slice_fusion.5 = f32[1,2,64,10,64]{2,0,4,3,1:T(1,128)S(1)} fusion(f32[8,2,64,10,64]{2,0,4,3,1:T(8,128)} %get-tuple-element.235, s32[]{:T(128)} %get-tuple-element.219), kind=kLoop, calls=%fused_computation.37.clone.1 | loop fusion | bytes 655364 | tf_op jit(solution)/shard_map/while/body/jit(dynamic_index_in_dim)/dynamic_slice | solution.py:118
  91.4 2.2 fusion.141
  96.0 3.1 %constant_dynamic-slice_fusion.5 = f32[1,2,64,10,64]{2,0,4,3,1:T(1,128)S(1)} fusion(f32[8,2,64,10,64]{2,0,4,3,1:T(8,128)} %get-tuple-element.235, s32[]{:T(128)} %get-tuple-element.219), kind=kLoop, calls=%fused_computation.37.clone.1 | loop fusion | bytes 655364 | tf_op jit(solution)/shard_map/while/body/jit(dynamic_index_in_dim)/dynamic_slice | solution.py:118
  99.1 2.2 fusion.141
  103.7 3.1 %constant_dynamic-slice_fusion.5 = f32[1,2,64,10,64]{2,0,4,3,1:T(1,128)S(1)} fusion(f32[8,2,64,10,64]{2,0,4,3,1:T(8,128)} %get-tuple-element.235, s32[]{:T(128)} %get-tuple-element.219), kind=kLoop, calls=%fused_computation.37.clone.1 | loop fusion | bytes 655364 | tf_op jit(solution)/shard_map/while/body/jit(dynamic_index_in_dim)/dynamic_slice | solution.py:118
  106.8 2.2 fusion.141
  111.5 3.1 %constant_dynamic-slice_fusion.5 = f32[1,2,64,10,64]{2,0,4,3,1:T(1,128)S(1)} fusion(f32[8,2,64,10,64]{2,0,4,3,1:T(8,128)} %get-tuple-element.235, s32[]{:T(128)} %get-tuple-element.219), kind=kLoop, calls=%fused_computation.37.clone.1 | loop fusion | bytes 655364 | tf_op jit(solution)/shard_map/while/body/jit(dynamic_index_in_dim)/dynamic_slice | solution.py:118
  114.6 2.2 fusion.141
  119.3 3.1 %constant_dynamic-slice_fusion.5 = f32[1,2,64,10,64]{2,0,4,3,1:T(1,128)S(1)} fusion(f32[8,2,64,10,64]{2,0,4,3,1:T(8,128)} %get-tuple-element.235, s32[]{:T(128)} %get-tuple-element.219), kind=kLoop, calls=%fused_computation.37.clone.1 | loop fusion | bytes 655364 | tf_op jit(solution)/shard_map/while/body/jit(dynamic_index_in_dim)/dynamic_slice | solution.py:118
  122.4 2.2 fusion.141
  127.0 3.1 %constant_dynamic-slice_fusion.5 = f32[1,2,64,10,64]{2,0,4,3,1:T(1,128)S(1)} fusion(f32[8,2,64,10,64]{2,0,4,3,1:T(8,128)} %get-tuple-element.235, s32[]{:T(128)} %get-tuple-element.219), kind=kLoop, calls=%fused_computation.37.clone.1 | loop fusion | bytes 655364 | tf_op jit(solution)/shard_map/while/body/jit(dynamic_index_in_dim)/dynamic_slice | solution.py:118
  130.1 2.2 fusion.141
  134.2 2.3 reduce-window.6
  137.1 1.8 all-gather
  138.9 7.7 %all-gather.2 = f32[8,1,10]{2,1,0:T(1,128)S(1)} all-gather(f32[2,1,10]{2,1,0:T(1,128)S(1)} %get-tuple-element.140), channel_id=4, replica_groups=mesh['seq_0'=4,'seq_1'=4,'seq_2'=2,'tp'=8] {'seq_1'}, dimensions={0}, use_global_device_ids=true | all-gather | bytes 400 | tf_op jit(solution)/shard_map/all_gather | solution.py:35
  146.7 1.5 all-gather.11.cloned.1.call-done
  148.2 2.3 bitcast_add_fusion.4
  150.8 37.7 %all-gather.7.cloned.1.call-done = f32[4,2,10,64,128]{4,3,2,1,0:T(8,128)} async-done(((f32[1,2,10,64,128]{4,3,2,1,0:T(8,128)}), f32[4,2,10,64,128]{4,3,2,1,0:T(8,128)}) %all-gather.7.cloned.1.call-update) | async-done | bytes 2621456 | tf_op jit(solution)/shard_map/all_gather | solution.py:35
  188.5 2.8 %multiply_add_fusion.1 = f32[1,2,10,64,128]{4,3,2,1,0:T(8,128)} fusion(f32[4,2,10,64,128]{4,3,2,1,0:T(8,128)} %all-gather.7.cloned.1.call-done, f32[2,10]{1,0:T(2,128)S(1)} %get-tuple-element.144, f32[2,10]{1,0:T(2,128)S(1)} %bitcast.251, f32[2,10]{1,0:T(2,128)S(1)} %bitcast.248, f32[2,10]{1,0:T(2,128)S(1)} %bitcast.254), kind=kLoop, calls=%fused_computation.98 | loop fusion | flops 1146880 | bytes 3277120 | tf_op jit(solution)/shard_map/add | solution.py:77
  191.8 7.1 %fusion.36 = f32[1024,640]{1,0:T(8,128)S(1)} fusion(bf16[1024,2560]{1,0:T(8,128)(2,1)} %bitcast.230, bf16[2560,640]{1,0:T(8,128)(2,1)} %param.13), kind=kOutput, calls=%fused_computation.56 | convolution fusion | flops 3356753920 | bytes 11141120 | tf_op jit(solution)/shard_map/dot_general | solution.py:96
  199.0 2.3 copy.110
  201.3 4.8 %reshape.160 = f32[2,512,10,64]{1,0,3,2:T(2,128)} reshape(f32[1024,640]{0,1:T(8,128)} %copy.110) | data formatting | bytes 5242880 | tf_op jit(solution)/shard_map/convert_element_type | solution.py:143
  206.1 8.6 %all_gather.32 = f32[4,2,10]{2,1,0:T(2,128)S(1)} all-gather(f32[1,2,10]{2,1,0:T(2,128)S(1)} %bitcast.259), channel_id=1, replica_groups=mesh['seq_0'=4,'seq_1'=4,'seq_2'=2,'tp'=8] {'seq_0'}, dimensions={0}, use_global_device_ids=true | all-gather | bytes 400 | tf_op jit(solution)/shard_map/all_gather | solution.py:35
  214.6 9.2 %copy.102 = f32[2,8,64,10,64]{2,1,4,3,0:T(8,128)} copy(f32[2,8,64,10,64]{2,4,3,0,1:T(8,128)} %bitcast.237) | data formatting | bytes 5242880 | tf_op jit(solution)/shard_map/transpose | solution.py:129
  223.8 5.2 %reshape.155 = f32[2,512,10,64]{1,3,2,0:T(8,128)} reshape(f32[2,8,64,10,64]{2,1,4,3,0:T(8,128)} %copy.102) | data formatting | bytes 5242880 | tf_op jit(solution)/shard_map/reshape | solution.py:129
  229.3 9.1 %multiply_reduce_fusion = (f32[2,512]{1,0:T(2,128)S(1)}, f32[2,512,10,64]{1,3,2,0:T(8,128)}) fusion(f32[2,512,10,64]{1,0,3,2:T(2,128)S(1)} %copy-done.6, f32[2,512,10,64]{1,3,2,0:T(8,128)} %reshape.155, f32[2,512,10]{1,2,0:T(8,128)S(1)} %copy.108, f32[4,2,10,64,128]{4,3,2,1,0:T(8,128)} %all-gather.9.cloned.1.call-done, ...), kind=kOutput, calls=%fused_computation.51 | convolution fusion | flops 1017609216 | bytes 14988234 | tf_op jit(solution)/shard_map/btn,bhpn->bthp/dot_general | solution.py:139
  238.4 3.2 %copy.109 = f32[2,512,640]{2,1,0:T(8,128)} copy(f32[2,512,640]{1,2,0:T(8,128)} %bitcast.238) | data formatting | bytes 5242880 | tf_op jit(solution)/shard_map/reshape | solution.py:141
  241.6 13.7 %psum.7 = f32[2,512,1]{1,0,2:T(2,128)S(1)} all-reduce(f32[2,512,1]{1,0,2:T(2,128)S(1)} %bitcast.261), channel_id=1, replica_groups=mesh['seq_0'=4,'seq_1'=4,'seq_2'=2,'tp'=8] {'tp'}, use_global_device_ids=true, to_apply=%region_6.7 | all-reduce | flops 1024 | bytes 8192 | tf_op jit(solution)/shard_map/psum | solution.py:146
  255.4 4.6 %multiply_convert_fusion = bf16[2,512,640]{2,1,0:T(8,128)(2,1)} fusion(f32[2,512,640]{2,1,0:T(8,128)} %copy.109, f32[2,512,640]{2,1,0:T(8,128)} %bitcast.233, f32[640]{0:T(1024)S(1)} %copy-done.12, f32[2,512]{1,0:T(2,128)S(1)} %rsqrt_bitcast_fusion), kind=kLoop, calls=%fused_computation.50 | loop fusion | flops 5242880 | bytes 6560256 | tf_op jit(solution)/shard_map/convert_element_type | solution.py:147
  (187 shorter events, 21.9 us)
Async XLA Ops:
  6.5 1.9 copy-start
  6.5 141.7 %all-gather.11.cloned.1.call-start = ((), (), s32[]{:S(2)}) async-start(), calls=%async_computation.2 | async-start | bytes 1966080 | tf_op jit(solution)/shard_map/all_gather | solution.py:35
  8.5 6.2 %copy-start.3 = (bf16[2,512,2560]{2,1,0:T(8,128)(2,1)S(1)}, bf16[2,512,2560]{2,1,0:T(8,128)(2,1)}, u32[]{:S(2)}) copy-start(bf16[2,512,2560]{2,1,0:T(8,128)(2,1)} %param.12) | copy-start | bytes 15728644
  8.5 6.2 %copy-start.9 = (bf16[2560,32]{0,1:T(8,128)(2,1)S(1)}, bf16[2560,32]{0,1:T(8,128)(2,1)}, u32[]{:S(2)}) copy-start(bf16[2560,32]{0,1:T(8,128)(2,1)} %param.15) | copy-start | bytes 491524
  40.1 14.6 %copy-start.11 = (f32[4,640]{1,0:T(4,128)S(1)}, f32[4,640]{1,0:T(4,128)}, u32[]{:S(2)}) copy-start(f32[4,640]{1,0:T(4,128)} %param.17) | copy-start | bytes 30724
  40.1 14.6 %copy-start.15 = (f32[10]{0:T(128)S(1)}, f32[10]{0:T(128)}, u32[]{:S(2)}) copy-start(f32[10]{0:T(128)} %param.20) | copy-start | bytes 124
  40.1 14.6 %copy-start.10 = (bf16[2560,10]{0,1:T(8,128)(2,1)S(1)}, bf16[2560,10]{0,1:T(8,128)(2,1)}, u32[]{:S(2)}) copy-start(bf16[2560,10]{0,1:T(8,128)(2,1)} %param.16) | copy-start | bytes 153604
  40.1 14.6 %copy-start.14 = (f32[10]{0:T(128)S(1)}, f32[10]{0:T(128)}, u32[]{:S(2)}) copy-start(f32[10]{0:T(128)} %param.19) | copy-start | bytes 124
  44.6 14.2 %copy-start.13 = (f32[4,256]{1,0:T(4,128)S(1)}, f32[4,256]{1,0:T(4,128)}, u32[]{:S(2)}) copy-start(f32[4,256]{1,0:T(4,128)} %param.18) | copy-start | bytes 12292
  44.6 14.6 %collective-permute-start = (bf16[2,3,896]{2,1,0:T(4,128)(2,1)S(1)}, bf16[2,3,896]{2,1,0:T(4,128)(2,1)S(1)}, u32[]{:S(2)}, u32[]{:S(2)}) collective-permute-start(bf16[2,3,896]{2,1,0:T(4,128)(2,1)S(1)} %slice.155), channel_id=1, source_target_pairs={{0,8},{8,16},{16,24},{24,32},{32,40},{40,48},{48,56},{56,64},{64,7... | collective-permute-start | bytes 32264 | tf_op jit(solution)/shard_map/ppermute | solution.py:21
  61.7 2.2 copy-start.4
  66.2 4.9 %copy-start.7 = (f32[2,512,128]{2,1,0:T(8,128)S(1)}, f32[2,512,128]{2,1,0:T(8,128)}, u32[]{:S(2)}) copy-start(f32[2,512,128]{2,1,0:T(8,128)} %get-tuple-element.127) | copy-start | bytes 1572868
  66.2 4.9 %copy-start.8 = (f32[2,512,128]{2,1,0:T(8,128)S(1)}, f32[2,512,128]{2,1,0:T(8,128)}, u32[]{:S(2)}) copy-start(f32[2,512,128]{2,1,0:T(8,128)} %get-tuple-element.128) | copy-start | bytes 1572868
  133.3 0.8 copy-start.2
  134.1 54.4 %all-gather.7.cloned.1.call-start = ((), (), s32[]{:S(2)}) async-start(), calls=%async_computation | async-start | bytes 3276800 | tf_op jit(solution)/shard_map/all_gather | solution.py:35
  150.5 78.8 %all-gather.9.cloned.1.call-start = ((), (), s32[]{:S(2)}) async-start(), calls=%async_computation.1 | async-start | bytes 3276800 | tf_op jit(solution)/shard_map/all_gather | solution.py:35
  199.0 7.1 %copy-start.5 = (f32[1024,640]{1,0:T(8,128)}, f32[1024,640]{1,0:T(8,128)S(1)}, u32[]{:S(2)}) copy-start(f32[1024,640]{1,0:T(8,128)S(1)} %fusion.36) | copy-start | bytes 7864324
  223.8 5.5 %copy-start.6 = (f32[2,512,10,64]{1,0,3,2:T(2,128)S(1)}, f32[2,512,10,64]{1,0,3,2:T(2,128)}, u32[]{:S(2)}) copy-start(f32[2,512,10,64]{1,0,3,2:T(2,128)} %reshape.160) | copy-start | bytes 7864324
  238.4 17.0 %copy-start.12 = (f32[640]{0:T(1024)S(1)}, f32[640]{0:T(1024)}, u32[]{:S(2)}) copy-start(f32[640]{0:T(1024)} %param.21) | copy-start | bytes 7684
  255.3 4.7 %copy-start.1 = (bf16[2560,640]{1,0:T(8,128)(2,1)S(1)}, bf16[2560,640]{1,0:T(8,128)(2,1)}, u32[]{:S(2)}) copy-start(bf16[2560,640]{1,0:T(8,128)(2,1)} %param.14) | copy-start | bytes 9830404
Sparse Core Ops, SparseCore 0:
  134.3 13.8 all-gather.10
  150.6 37.8 all-gather.6
  191.4 37.7 all-gather.8
where the time goes:
time: 271 us; the launch traced here: 267 us
  local copies, waits for them, and re-layouts  69.9 us (26%)
  matrix products  59.8 us (22%)
  blocking collectives  55.5 us (20%)
  waiting for transfers between devices  39.6 us (15%)
  other arithmetic  17.2 us (6%)
  between operations  13.4 us (5%)
  starting transfers between devices  10.4 us (4%)
    all_gather x3, waiting for transfers between devices, entering(): pieces = jax.tree.map(lambda part: lax.all_gather(part, axis), so_far)  39.6 us
    dynamic_slice x32, local copies, waits for them, and re-layouts, on_device(): lax.scan(block_step, initial, (to_blocks(values, batch_size, blocks), to_...  26.5 us
    all_gather x1, blocking collectives, on_device(): bc_pre = lax.all_gather(bc_part, 'tp', axis=1, tiled=True)  23.7 us
    all_gather x3, blocking collectives, entering(): pieces = jax.tree.map(lambda part: lax.all_gather(part, axis), so_far)  18.1 us
    dot_general x8, matrix products, block_step(): jnp.einsum('bijh,bjhp->bihp', mixing, values, precision=lax.Precision.HIG...  17.6 us
    psum x1, blocking collectives, on_device(): whole_sq = lax.psum(squares, 'tp')  13.7 us
    ppermute x1, starting transfers between devices, passed_along(): return lax.ppermute(block, axis, route)  10.1 us
    transpose x1, local copies, waits for them, and re-layouts, on_device(): jnp.moveaxis(outputs, 0, 1)  9.16 us
  transfers between devices with their start and end apart: 4, of which 3 were waited for; matrix products, arithmetic and copies ran while one was open for 14% of the time, Pallas kernels for 0%

commit v1 on v0

v1 whole, which is shorter than its diff:
```python
import functools

import jax
import jax.numpy as jnp
from jax import lax
from jax.experimental import pallas as pl
from jax.experimental.pallas import tpu as pltpu
from jax.sharding import Mesh
from jax.sharding import PartitionSpec as P

DI = 5120
HEAD_DIM = 64
STATE = 128
CONV = 4
BLOCK = 128
LANES = 128
EPSILON = 1e-05

F32 = jnp.float32
BF16 = jnp.bfloat16
HIGHEST = lax.Precision.HIGHEST
NT = (((1,), (1,)), ((), ()))


def dot(a, b):
    return jnp.dot(a, b, preferred_element_type=F32)


def dot_nt(a, b):
    return lax.dot_general(a, b, NT, preferred_element_type=F32)


def silu(x):
    return x / (1.0 + jnp.exp(-x))


def split_in_three(x):
    high = x.astype(BF16)
    rest = x - high.astype(F32)
    middle = rest.astype(BF16)
    return high, middle, (rest - middle.astype(F32)).astype(BF16)


def head_lanes(width):
    head = lax.broadcasted_iota(jnp.int32, (LANES, width), 1) // HEAD_DIM
    row = lax.broadcasted_iota(jnp.int32, (LANES, width), 0)
    return (head == row).astype(BF16)


def over_channels(x, spread):
    high, middle, low = split_in_three(x)
    return dot(high, spread) + dot(middle, spread) + dot(low, spread)


def bc_kernel(batch, length, hidden, halo, weight, out, pad):
    share = weight.shape[0]
    pad[...] = jnp.zeros_like(pad)
    before = dot_nt(halo[...], weight[...])
    for b in range(batch):
        pad[LANES - 8 - 64 * b : LANES - 64 * b, :share] = before[8 * b : 8 * b + 8]
    tile = jnp.transpose(pad[...])[:share].astype(BF16)
    for d in range(out.shape[0]):
        out[d, :, :LANES] = tile
    for j in range(batch * length // LANES):
        part = dot_nt(hidden[j * LANES : (j + 1) * LANES, :], weight[...])
        pad[:, :share] = part
        tile = jnp.transpose(pad[...])[:share].astype(BF16)
        for d in range(out.shape[0]):
            out[d, :, (j + 1) * LANES : (j + 2) * LANES] = tile


def value_kernel(
    batch, length, hidden, halo, weight, taps, step_weight, step_bias, log_rate,
    scaled, opening, rows, decays, padded,
):
    inner = weight.shape[1]
    blocks = length // BLOCK
    spread = head_lanes(inner)
    before = dot(halo[...], weight[...]).astype(BF16).astype(F32)
    rate = jnp.exp(log_rate[0:1, :])
    i = lax.broadcasted_iota(jnp.int32, (BLOCK, BLOCK), 0)
    j = lax.broadcasted_iota(jnp.int32, (BLOCK, BLOCK), 1)
    lower = (i >= j).astype(BF16)
    halves, offsets = [], []
    for b in range(batch):
        own = hidden[b * length : (b + 1) * length, :]
        padded[0:8, :] = before[8 * b : 8 * b + 8]
        padded[8 : 8 + length, :] = dot(own, weight[...]).astype(BF16).astype(F32)
        step_pre = dot_nt(own, step_weight[...]) + step_bias[0:1, :]
        steps = jnp.maximum(step_pre, 0.0) + jnp.log1p(jnp.exp(-jnp.abs(step_pre)))
        total = jnp.zeros((1, LANES), F32)
        for k in range(blocks):
            r = k * BLOCK
            step = steps[r : r + BLOCK]
            high, middle, low = split_in_three(-step * rate)
            cumulative = dot(lower, high) + dot(lower, middle) + dot(lower, low)
            last = cumulative[BLOCK - 1 : BLOCK, :]
            centered = cumulative - 0.5 * last
            halves.append(0.5 * last)
            offsets.append(total + 0.5 * last)
            total = total + last
            value = sum(
                taps[t : t + 1, :] * padded[r + 5 + t : r + 5 + t + BLOCK, :] for t in range(CONV)
            )
            ahead = over_channels(jnp.exp(-centered) * step, spread)
            at = b * length + r
            scaled[at : at + BLOCK, :] = (silu(value) * ahead).astype(BF16)
            opening[at : at + BLOCK, :] = jnp.exp(centered)
        high, middle, low = split_in_three(total)
        decays[b] = jnp.concatenate(
            [high, middle, low, jnp.zeros((5, LANES), BF16)], axis=0
        )
    rows[...] = jnp.exp(over_channels(jnp.concatenate(halves + offsets, axis=0), spread))


def gate_kernel(batch, length, hidden, weight, opening, out):
    spread = head_lanes(weight.shape[1])
    for b in range(batch):
        at = slice(b * length, (b + 1) * length)
        gate = dot(hidden[at, :], weight[...]).astype(BF16).astype(F32)
        out[at, :] = (silu(gate) * over_channels(opening[at, :], spread)).astype(BF16)


def state_kernel(batch, length, bc, taps, scaled, rows, decays, b_rows, c_rows, starts, sent):
    blocks = length // BLOCK
    inner = scaled.shape[1]
    halo = bc[:, :LANES].astype(F32)
    for b in range(batch):
        own = bc[:, LANES + b * length : LANES + (b + 1) * length].astype(F32)
        before = pltpu.roll(halo, 64 * b, 1) if b else halo
        padded = jnp.concatenate([before, own], axis=1)
        mixed = taps[:, CONV - 1 : CONV] * own
        for t in range(CONV - 1):
            mixed = mixed + taps[:, t : t + 1] * pltpu.roll(padded, CONV - 1 - t, 1)[:, LANES:]
        mixed = silu(mixed)
        b_t = mixed[:STATE].astype(BF16)
        b_rows[b] = b_t
        c_rows[b * length : (b + 1) * length, :] = jnp.transpose(mixed[STATE:]).astype(BF16)
        state = jnp.zeros((STATE, inner), F32)
        for k in range(blocks):
            n = b * blocks + k
            half = rows[n : n + 1, :]
            ready = half * state
            starts[n] = ready.astype(BF16)
            at = b * length + k * BLOCK
            added = dot(b_t[:, k * BLOCK : (k + 1) * BLOCK], scaled[at : at + BLOCK, :])
            state = half * (ready + added)
        for g in range(STATE // 8):
            sent[b, g, :, :inner] = state[8 * g : 8 * g + 8].astype(BF16)
            sent[b, g, :, inner:] = decays[b]


def within_kernel(batch, length, b_rows, c_rows, scaled, starts, out):
    blocks = length // BLOCK
    i = lax.broadcasted_iota(jnp.int32, (BLOCK, BLOCK), 0)
    j = lax.broadcasted_iota(jnp.int32, (BLOCK, BLOCK), 1)
    for b in range(batch):
        for k in range(blocks):
            at = slice(b * length + k * BLOCK, b * length + (k + 1) * BLOCK)
            c = c_rows[at, :]
            scores = dot(c, b_rows[b, :, k * BLOCK : (k + 1) * BLOCK])
            scores = jnp.where(i >= j, scores, 0.0).astype(BF16)
            out[at, :] = dot(scores, scaled[at, :]) + dot(c, starts[b * blocks + k])


def scan_kernel(got, out, table, logs):
    devices, _, width = got.shape
    inner = width - LANES
    for s in range(devices):
        parts = got[s, :, inner:].astype(F32)
        table[s : s + 1, :] = parts[0:1] + parts[1:2] + parts[2:3]
    logs[...] = jnp.exp(over_channels(table[...], head_lanes(inner)))
    state = jnp.zeros((8, inner), F32)
    for s in range(devices):
        out[s] = state.astype(BF16)
        state = logs[s : s + 1, :] * state + got[s, :, :inner].astype(F32)


def gated_kernel(batch, length, c_rows, arrived, within, opened, rows, gated, squares):
    blocks = length // BLOCK
    count = batch * blocks
    inner = within.shape[1]
    ones = jnp.ones((8, inner), BF16)
    for b in range(batch):
        for k in range(blocks):
            n = b * blocks + k
            at = slice(n * BLOCK, (n + 1) * BLOCK)
            late = dot(c_rows[at, :], arrived[b])
            y = within[at, :] + rows[count + n : count + n + 1, :] * late
            g = y * opened[at, :].astype(F32)
            gated[at, :] = g
            squares[:, n, :] = dot_nt(ones, (g * g).astype(BF16))


def scale_kernel(gated, squares, gain, out):
    total = squares[0]
    for d in range(1, squares.shape[0]):
        total = total + squares[d]
    scale = lax.rsqrt(total / DI + EPSILON)
    count = scale.shape[0]
    scale = jnp.concatenate([scale, jnp.zeros((LANES - count, LANES), F32)], axis=0)
    columns = jnp.transpose(scale)
    for n in range(count):
        at = slice(n * LANES, (n + 1) * LANES)
        out[at, :] = (gated[at, :] * columns[:, n : n + 1] * gain[0:1, :]).astype(BF16)


def call(kernel, out, scratch=(), mib=28, flops=0):
    shapes = [jax.ShapeDtypeStruct(s, d) for s, d in out]
    return pl.pallas_call(
        kernel,
        out_shape=shapes if len(shapes) > 1 else shapes[0],
        scratch_shapes=[pltpu.VMEM(s, d) for s, d in scratch],
        compiler_params=pltpu.CompilerParams(vmem_limit_bytes=mib << 20),
        cost_estimate=pl.CostEstimate(flops=flops, transcendentals=0, bytes_accessed=0)
        if flops
        else None,
    )


def on_device(
    hidden_in, gate_proj, value_proj, bc_proj, step_proj, value_conv, bc_conv, step_bias, log_rate,
    norm_gain,
):
    batch, length, width = hidden_in.shape
    tokens = batch * length
    inner = value_proj.shape[1]
    heads = step_proj.shape[1]
    share = bc_proj.shape[1]
    states = 2 * STATE
    blocks = tokens // BLOCK
    seq, tp = lax.axis_size("seq"), lax.axis_size("tp")
    hidden = hidden_in.reshape(tokens, width)
    tail = hidden_in[:, length - 8 :, :]
    halo = lax.ppermute(tail, "seq", [(i, i + 1) for i in range(seq - 1)]).reshape(8 * batch, width)
    bc_part = call(
        functools.partial(bc_kernel, batch, length),
        [((tp, share, tokens + LANES), BF16)],
        [((LANES, LANES), F32)],
    )(hidden, halo, bc_proj.T)
    bc = lax.all_to_all(bc_part, "tp", 0, 0, tiled=True).reshape(states, tokens + LANES)
    lane = jnp.pad
    scaled, opening, rows, decays = call(
        functools.partial(value_kernel, batch, length),
        [
            ((tokens, inner), BF16),
            ((tokens, LANES), F32),
            ((2 * blocks, inner), F32),
            ((batch, 8, LANES), BF16),
        ],
        [((length + 8, inner), F32)],
        flops=2 * tokens * width * inner,
    )(
        hidden,
        halo,
        value_proj,
        value_conv,
        lane(step_proj.T, ((0, LANES - heads), (0, 0))),
        lane(step_bias, (0, LANES - heads)).reshape(1, LANES),
        lane(log_rate, (0, LANES - heads), constant_values=-1e30).reshape(1, LANES),
    )
    opened = call(
        functools.partial(gate_kernel, batch, length),
        [((tokens, inner), BF16)],
        flops=2 * tokens * width * inner,
    )(hidden, gate_proj, opening)
    b_rows, c_rows, starts, sent = call(
        functools.partial(state_kernel, batch, length),
        [
            ((batch, STATE, length), BF16),
            ((tokens, STATE), BF16),
            ((blocks, STATE, inner), BF16),
            ((batch, STATE // 8, 8, inner + LANES), BF16),
        ],
    )(bc, bc_conv.T, scaled, rows, decays)
    got = lax.all_to_all(sent.reshape(seq, -1, inner + LANES), "seq", 0, 0, tiled=True)
    within = call(
        functools.partial(within_kernel, batch, length),
        [((tokens, inner), F32)],
        flops=2 * tokens * width * inner // 4,
    )(b_rows, c_rows, scaled, starts)
    prefix = call(
        scan_kernel,
        [((seq, 8, inner), BF16)],
        [((seq, LANES), F32), ((seq, inner), F32)],
    )(got)
    arrived = lax.all_to_all(prefix, "seq", 0, 0, tiled=True).reshape(batch, STATE, inner)
    gated, squares = call(
        functools.partial(gated_kernel, batch, length),
        [((tokens, inner), F32), ((tp, blocks, LANES), F32)],
    )(c_rows, arrived, within, opened, rows)
    whole = lax.all_to_all(squares, "tp", 0, 0, tiled=True)
    out = call(scale_kernel, [((tokens, inner), BF16)])(gated, whole, norm_gain.reshape(1, inner))
    return out.reshape(batch, length, inner)


def solution(mesh):
    placed = (
        P(None, "seq", None),
        P(None, "tp"),
        P(None, "tp"),
        P(None, "tp"),
        P(None, "tp"),
        P(None, "tp"),
        P(),
        P("tp"),
        P("tp"),
        P("tp"),
    )
    return jax.shard_map(
        on_device, mesh=mesh, in_specs=placed, out_specs=P(None, "seq", "tp"), check_vma=False
    )
```

time: 271 us -> 99.1 us (0.37); the launches traced: 267 us -> 98.2 us
  matrix products: 59.8 us -> 0 us
  local copies, waits for them, and re-layouts: 69.9 us -> 22.4 us
  blocking collectives: 55.5 us -> 19 us
  waiting for transfers between devices: 39.6 us -> 12 us
  Pallas kernels: 0 us -> 24.7 us
  other arithmetic: 17.2 us -> 0 us
  between operations: 13.4 us -> 0.23 us
  starting transfers between devices: 10.4 us -> 19.9 us
    dot_general x37 -> x0, matrix products: 59.8 us -> none  [the longest x8 17.6 us: block_step(): jnp.einsum('bijh,bjhp->bihp', mixing, values, precision=lax.Precision.HIG...]
    all_gather x4 -> x0, blocking collectives: 41.8 us -> none  [the longest x1 23.7 us: on_device(): bc_pre = lax.all_gather(bc_part, 'tp', axis=1, tiled=True)]
    all_gather x3 -> x0, waiting for transfers between devices: 39.6 us -> none  [entering(): pieces = jax.tree.map(lambda part: lax.all_gather(part, axis), so_far)]
    dynamic_slice x32 -> x0, local copies, waits for them, and re-layouts: 26.5 us -> none  [on_device(): lax.scan(block_step, initial, (to_blocks(values, batch_size, blocks), to_...]
    pallas_call x0 -> x8, Pallas kernels: none -> 24.7 us  [the longest x1 9.19 us: on_device(): call(functools.partial(value_kernel, batch, length), [((tokens, inner), B...]
    all_to_all x0 -> x1, blocking collectives: none -> 19 us  [on_device(): lax.all_to_all(sent.reshape(seq, -1, inner + LANES), 'seq', 0, 0, tiled=T...]
    unnamed x33 -> x45, local copies, waits for them, and re-layouts: 3.86 us -> 21.4 us
    all_to_all x0 -> x3, starting transfers between devices: none -> 15.4 us  [the longest x1 8.19 us: on_device(): lax.all_to_all(bc_part, 'tp', 0, 0, tiled=True)]
  transfers between devices with their start and end apart: 4 -> 4, of which waited for: 3 -> 3; matrix products, arithmetic and copies ran while one was open for 14% -> 0% of each run, Pallas kernels for 0% -> 16%
where the time goes in v1:
time: 99.1 us; the launch traced here: 98.2 us
  Pallas kernels  24.7 us (25%)
  local copies, waits for them, and re-layouts  22.4 us (23%)
  starting transfers between devices  19.9 us (20%)
  blocking collectives  19 us (19%)
  waiting for transfers between devices  12 us (12%)
    unnamed x45, local copies, waits for them, and re-layouts  21.4 us
    all_to_all x1, blocking collectives, on_device(): lax.all_to_all(sent.reshape(seq, -1, inner + LANES), 'seq', 0, 0, tiled=T...  19 us
    pallas_call x1, Pallas kernels, on_device(): call(functools.partial(value_kernel, batch, length), [((tokens, inner), B...  9.19 us
    all_to_all x1, starting transfers between devices, on_device(): lax.all_to_all(bc_part, 'tp', 0, 0, tiled=True)  8.19 us
    all_to_all x1, waiting for transfers between devices, on_device(): whole = lax.all_to_all(squares, 'tp', 0, 0, tiled=True)  6.6 us
    pallas_call x1, Pallas kernels, on_device(): call(functools.partial(gate_kernel, batch, length), [((tokens, inner), BF...  5.37 us
    ppermute x1, starting transfers between devices, on_device(): lax.ppermute(tail, 'seq', [(i, i + 1) for i in range(seq - 1)])  4.49 us
    all_to_all x1, waiting for transfers between devices, on_device(): lax.all_to_all(bc_part, 'tp', 0, 0, tiled=True)  3.93 us
  transfers between devices with their start and end apart: 4, of which 3 were waited for; matrix products, arithmetic and copies ran while one was open for 0% of the time, Pallas kernels for 16%

profile of v1, /device:TPU:1, one launch (start us, length us, event | category | flops | bytes accessed | tf_op | source)
XLA Modules:
  0.0 98.2 jit_solution(2462426469556619821)
XLA Ops:
  0.0 0.9 slice.3
  0.9 4.5 %collective-permute-start = (bf16[2,8,2560]{2,1,0:T(8,128)(2,1)S(1)}, bf16[2,8,2560]{2,1,0:T(8,128)(2,1)S(1)}, u32[]{:S(2)}, u32[]{:S(2)}) collective-permute-start(bf16[2,8,2560]{2,1,0:T(8,128)(2,1)S(1)} %slice.3), channel_id=1, source_target_pairs={{0,8},{8,16},{16,24},{24,32},{32,40},{40,48},{48,56},{56,64},{64,7... | collective-permute-start | bytes 245768 | tf_op jit(solution)/shard_map/ppermute | solution.py:235
  5.4 1.5 %collective-permute-done = bf16[2,8,2560]{2,1,0:T(8,128)(2,1)S(1)} collective-permute-done((bf16[2,8,2560]{2,1,0:T(8,128)(2,1)S(1)}, bf16[2,8,2560]{2,1,0:T(8,128)(2,1)S(1)}, u32[]{:S(2)}, u32[]{:S(2)}) %collective-permute-start) | collective-permute-done | bytes 81952 | tf_op jit(solution)/shard_map/ppermute | solution.py:235
  6.9 2.5 %copy-done = bf16[2,512,2560]{2,1,0:T(8,128)(2,1)S(1)} copy-done((bf16[2,512,2560]{2,1,0:T(8,128)(2,1)S(1)}, bf16[2,512,2560]{2,1,0:T(8,128)(2,1)}, u32[]{:S(2)}) %copy-start) | copy-done | bytes 5242904
  9.3 0.9 copy-done.11
  10.3 0.0 copy-start.14
  10.3 2.5 %shard_map.100 = bf16[8,32,1152]{2,1,0:T(8,128)(2,1)} custom-call(bf16[1024,2560]{1,0:T(8,128)(2,1)S(1)} %bitcast.13, bf16[16,2560]{1,0:T(8,128)(2,1)S(1)} %bitcast.21, bf16[32,2560]{1,0:T(8,128)(2,1)S(1)} %bitcast.20), custom_call_target="tpu_custom_call" | custom-call | tf_op jit(solution)/shard_map/pallas_call | solution.py:236
  12.8 8.2 %all-to-all-start = ((bf16[8,32,1152]{2,1,0:T(8,128)(2,1)}), bf16[8,32,1152]{2,1,0:T(8,128)(2,1)S(1)}, u32[]{:S(2)}, u32[]{:S(2)}) async-start(bf16[8,32,1152]{2,1,0:T(8,128)(2,1)} %shard_map.100), calls=%async_computation | async-start | bytes 1179648 | tf_op jit(solution)/shard_map/all_to_all | solution.py:241
  20.9 0.0 copy-done.18
  20.9 0.1 copy.11
  21.1 0.0 copy-done.17
  21.2 0.0 copy-done.20
  21.2 0.0 copy-done.21
  21.2 0.0 copy-done.14
  21.2 0.0 copy-start.1
  21.2 2.5 %copy-done.1 = bf16[2,512,2560]{2,1,0:T(8,128)(2,1)S(1)} copy-done((bf16[2,512,2560]{2,1,0:T(8,128)(2,1)S(1)}, bf16[2,512,2560]{2,1,0:T(8,128)(2,1)}, u32[]{:S(2)}) %copy-start.1) | copy-done | bytes 5242904
  23.7 1.9 %copy-done.12 = bf16[2560,640]{1,0:T(8,128)(2,1)S(1)} copy-done((bf16[2560,640]{1,0:T(8,128)(2,1)S(1)}, bf16[2560,640]{1,0:T(8,128)(2,1)}, u32[]{:S(2)}) %copy-start.12) | copy-done | bytes 3276824
  25.6 9.2 %shard_map.101 = (bf16[1024,640]{1,0:T(8,128)(2,1)S(1)}, f32[1024,128]{1,0:T(8,128)S(1)}, f32[16,640]{1,0:T(8,128)S(1)}, bf16[2,8,128]{2,1,0:T(8,128)(2,1)S(1)}) custom-call(bf16[1024,2560]{1,0:T(8,128)(2,1)S(1)} %bitcast.14, bf16[16,2560]{1,0:T(8,128)(2,1)S(1)} %bitcast.22, bf16[2560,640]{1,0:T(8,128)(2,1)S(1)} %copy-done.12, f32[4,640]{1,0:T(4,128)S(1)} %copy-done.14, ...), custom_call_target="tpu_custom_call" | custom-call | flops 3355443200 | tf_op jit(solution)/shard_map/pallas_call | solution.py:243
  34.8 0.0 copy-start.15
  34.8 0.0 copy-start.3
  34.8 3.9 %all-to-all-done = bf16[8,32,1152]{2,1,0:T(8,128)(2,1)S(1)} async-done(((bf16[8,32,1152]{2,1,0:T(8,128)(2,1)}), bf16[8,32,1152]{2,1,0:T(8,128)(2,1)S(1)}, u32[]{:S(2)}, u32[]{:S(2)}) %all-to-all-start) | async-done | bytes 589856 | tf_op jit(solution)/shard_map/all_to_all | solution.py:241
  38.8 1.8 %shard_map.102 = (bf16[2,128,512]{2,1,0:T(8,128)(2,1)S(1)}, bf16[1024,128]{1,0:T(8,128)(2,1)S(1)}, bf16[8,128,640]{2,1,0:T(8,128)(2,1)S(1)}, bf16[2,16,8,768]{3,2,1,0:T(8,128)(2,1)S(1)}) custom-call(bf16[256,1152]{1,0:T(8,128)(2,1)S(1)} %bitcast.16, f32[256,4]{1,0:T(8,128)S(1)} %bitcast.18, bf16[1024,640]{1,0:T(8,128)(2,1)S(1)} %get-tuple-element.15.scaled, ...), custom_call_target="tpu_custom_call" | custom-call | tf_op jit(solution)/shard_map/pallas_call | solution.py:267
  40.6 0.0 copy-start.7
  40.6 1.1 %copy-done.7 = bf16[8,128,640]{2,1,0:T(8,128)(2,1)} copy-done((bf16[8,128,640]{2,1,0:T(8,128)(2,1)}, bf16[8,128,640]{2,1,0:T(8,128)(2,1)S(1)}, u32[]{:S(2)}) %copy-start.7) | copy-done | bytes 1310744
  41.6 19.0 %all_to_all.20.got = bf16[32,8,768]{2,1,0:T(8,128)(2,1)S(1)} all-to-all(bf16[32,8,768]{2,1,0:T(8,128)(2,1)S(1)} %bitcast.19), channel_id=1, replica_groups=mesh['seq'=32,'tp'=8] {'seq'}, dimensions={0} | all-to-all | bytes 786432 | tf_op jit(solution)/shard_map/all_to_all | solution.py:276
  60.6 1.1 %shard_map.103 = bf16[32,8,640]{2,1,0:T(8,128)(2,1)} custom-call(bf16[32,8,768]{2,1,0:T(8,128)(2,1)S(1)} %all_to_all.20.got), custom_call_target="tpu_custom_call" | custom-call | tf_op jit(solution)/shard_map/pallas_call | solution.py:282
  61.7 0.0 copy-done.15
  61.7 3.8 %all-to-all-start.2 = ((bf16[32,8,640]{2,1,0:T(8,128)(2,1)}), bf16[32,8,640]{2,1,0:T(8,128)(2,1)S(1)}, u32[]{:S(2)}, u32[]{:S(2)}) async-start(bf16[32,8,640]{2,1,0:T(8,128)(2,1)} %shard_map.103), calls=%async_computation.2 | async-start | bytes 655360 | tf_op jit(solution)/shard_map/all_to_all | solution.py:287
  65.5 0.0 copy-start.2
  65.5 2.5 %copy-done.2 = bf16[2,512,2560]{2,1,0:T(8,128)(2,1)S(1)} copy-done((bf16[2,512,2560]{2,1,0:T(8,128)(2,1)S(1)}, bf16[2,512,2560]{2,1,0:T(8,128)(2,1)}, u32[]{:S(2)}) %copy-start.2) | copy-done | bytes 5242904
  68.0 1.9 %copy-done.13 = bf16[2560,640]{1,0:T(8,128)(2,1)S(1)} copy-done((bf16[2560,640]{1,0:T(8,128)(2,1)S(1)}, bf16[2560,640]{1,0:T(8,128)(2,1)}, u32[]{:S(2)}) %copy-start.13) | copy-done | bytes 3276824
  69.9 1.0 %copy-done.16 = f32[1024,128]{1,0:T(8,128)S(1)} copy-done((f32[1024,128]{1,0:T(8,128)S(1)}, f32[1024,128]{1,0:T(8,128)}, u32[]{:S(2)}) %copy-start.16) | copy-done | bytes 524312
  71.0 5.4 %shard_map.105.opened = bf16[1024,640]{1,0:T(8,128)(2,1)S(1)} custom-call(bf16[1024,2560]{1,0:T(8,128)(2,1)S(1)} %bitcast.15, bf16[2560,640]{1,0:T(8,128)(2,1)S(1)} %copy-done.13, f32[1024,128]{1,0:T(8,128)S(1)} %copy-done.16), custom_call_target="tpu_custom_call" | custom-call | flops 3355443200 | tf_op jit(solution)/shard_map/pallas_call | solution.py:262
  76.4 0.0 copy-done.3
  76.4 0.0 copy-start.9
  76.4 1.1 %copy-done.9 = bf16[1024,640]{1,0:T(8,128)(2,1)} copy-done((bf16[1024,640]{1,0:T(8,128)(2,1)}, bf16[1024,640]{1,0:T(8,128)(2,1)S(1)}, u32[]{:S(2)}) %copy-start.9) | copy-done | bytes 1310744
  77.5 1.3 %copy-done.4 = bf16[1024,640]{1,0:T(8,128)(2,1)S(1)} copy-done((bf16[1024,640]{1,0:T(8,128)(2,1)S(1)}, bf16[1024,640]{1,0:T(8,128)(2,1)}, u32[]{:S(2)}) %copy-start.4) | copy-done | bytes 1310744
  78.8 1.5 %shard_map.104.within = f32[1024,640]{1,0:T(8,128)S(1)} custom-call(bf16[2,128,512]{2,1,0:T(8,128)(2,1)S(1)} %get-tuple-element.20.b_rows, bf16[1024,128]{1,0:T(8,128)(2,1)S(1)} %get-tuple-element.18.c_rows, bf16[1024,640]{1,0:T(8,128)(2,1)S(1)} %copy-done.4, bf16[8,128,640]{2,1,0:T(8,128)(2,1)S(1)} %copy-done.8), custom_call_target="tpu_custom_call" | custom-call | flops 838860800 | tf_op jit(solution)/shard_map/pallas_call | solution.py:277
  80.3 0.0 all-to-all-done.2
  80.3 0.0 copy-start.10
  80.3 1.3 %copy-done.10 = bf16[1024,640]{1,0:T(8,128)(2,1)S(1)} copy-done((bf16[1024,640]{1,0:T(8,128)(2,1)S(1)}, bf16[1024,640]{1,0:T(8,128)(2,1)}, u32[]{:S(2)}) %copy-start.10) | copy-done | bytes 1310744
  81.6 1.9 %shard_map.106 = (f32[1024,640]{1,0:T(8,128)S(1)}, f32[8,8,128]{2,1,0:T(8,128)}) custom-call(bf16[1024,128]{1,0:T(8,128)(2,1)S(1)} %get-tuple-element.18.c_rows, bf16[2,128,640]{2,1,0:T(8,128)(2,1)S(1)} %bitcast.17, f32[1024,640]{1,0:T(8,128)S(1)} %shard_map.104.within, bf16[1024,640]{1,0:T(8,128)(2,1)S(1)} %copy-done.10, f32[16,640]{1,0:T(8,128)S(1)} %get-tuple-element.16.rows), custom_call_target="tpu_custom_call" | custom-call | tf_op jit(solution)/shard_map/pallas_call | solution.py:288
  83.5 1.5 %copy-done.5 = f32[1024,640]{1,0:T(8,128)} copy-done((f32[1024,640]{1,0:T(8,128)}, f32[1024,640]{1,0:T(8,128)S(1)}, u32[]{:S(2)}) %copy-start.5) | copy-done | bytes 2621464
  85.0 3.3 %all-to-all-start.3 = ((f32[8,8,128]{2,1,0:T(8,128)}), f32[8,8,128]{2,1,0:T(8,128)S(1)}, u32[]{:S(2)}, u32[]{:S(2)}) async-start(f32[8,8,128]{2,1,0:T(8,128)} %get-tuple-element.24), calls=%async_computation.3 | async-start | bytes 65536 | tf_op jit(solution)/shard_map/all_to_all | solution.py:292
  88.4 0.0 copy-done.19
  88.4 6.6 %all-to-all-done.3.squares = f32[8,8,128]{2,1,0:T(8,128)S(1)} async-done(((f32[8,8,128]{2,1,0:T(8,128)}), f32[8,8,128]{2,1,0:T(8,128)S(1)}, u32[]{:S(2)}, u32[]{:S(2)}) %all-to-all-start.3) | async-done | bytes 32800 | tf_op jit(solution)/shard_map/all_to_all | solution.py:292
  95.0 1.7 %copy-done.6 = f32[1024,640]{1,0:T(8,128)S(1)} copy-done((f32[1024,640]{1,0:T(8,128)S(1)}, f32[1024,640]{1,0:T(8,128)}, u32[]{:S(2)}) %copy-start.6) | copy-done | bytes 2621464
  96.7 1.4 %shard_map.107 = bf16[1024,640]{1,0:T(8,128)(2,1)} custom-call(f32[1024,640]{1,0:T(8,128)S(1)} %copy-done.6, f32[8,8,128]{2,1,0:T(8,128)S(1)} %all-to-all-done.3.squares, f32[1,640]{1,0:T(1,128)S(1)} %reshape.34.gain), custom_call_target="tpu_custom_call" | custom-call | tf_op jit(solution)/shard_map/pallas_call | solution.py:293
  (18 shorter events, 0.1 us)
Async XLA Ops:
  0.9 6.0 %collective-permute-start = (bf16[2,8,2560]{2,1,0:T(8,128)(2,1)S(1)}, bf16[2,8,2560]{2,1,0:T(8,128)(2,1)S(1)}, u32[]{:S(2)}, u32[]{:S(2)}) collective-permute-start(bf16[2,8,2560]{2,1,0:T(8,128)(2,1)S(1)} %slice.3), channel_id=1, source_target_pairs={{0,8},{8,16},{16,24},{24,32},{32,40},{40,48},{48,56},{56,64},{64,7... | collective-permute-start | bytes 245768 | tf_op jit(solution)/shard_map/ppermute | solution.py:235
  6.9 2.5 %copy-start = (bf16[2,512,2560]{2,1,0:T(8,128)(2,1)S(1)}, bf16[2,512,2560]{2,1,0:T(8,128)(2,1)}, u32[]{:S(2)}) copy-start(bf16[2,512,2560]{2,1,0:T(8,128)(2,1)} %param.10) | copy-start | bytes 15728644
  9.3 0.9 copy-start.11
  10.3 10.7 %copy-start.18 = (f32[4,256]{1,0:T(4,128)S(1)}, f32[4,256]{1,0:T(4,128)}, u32[]{:S(2)}) copy-start(f32[4,256]{1,0:T(4,128)} %param.16) | copy-start | bytes 12292
  10.3 10.8 %copy-start.17 = (bf16[2560,10]{0,1:T(8,128)(2,1)S(1)}, bf16[2560,10]{0,1:T(8,128)(2,1)}, u32[]{:S(2)}) copy-start(bf16[2560,10]{0,1:T(8,128)(2,1)} %param.14) | copy-start | bytes 153604
  10.3 10.9 %copy-start.20 = (f32[10]{0:T(128)S(1)}, f32[10]{0:T(128)}, u32[]{:S(2)}) copy-start(f32[10]{0:T(128)} %param.18) | copy-start | bytes 124
  10.3 10.9 %copy-start.21 = (f32[10]{0:T(128)S(1)}, f32[10]{0:T(128)}, u32[]{:S(2)}) copy-start(f32[10]{0:T(128)} %param.17) | copy-start | bytes 124
  10.3 10.9 %copy-start.14 = (f32[4,640]{1,0:T(4,128)S(1)}, f32[4,640]{1,0:T(4,128)}, u32[]{:S(2)}) copy-start(f32[4,640]{1,0:T(4,128)} %taps.1) | copy-start | bytes 30724
  12.8 26.0 %all-to-all-start = ((bf16[8,32,1152]{2,1,0:T(8,128)(2,1)}), bf16[8,32,1152]{2,1,0:T(8,128)(2,1)S(1)}, u32[]{:S(2)}, u32[]{:S(2)}) async-start(bf16[8,32,1152]{2,1,0:T(8,128)(2,1)} %shard_map.100), calls=%async_computation | async-start | bytes 1179648 | tf_op jit(solution)/shard_map/all_to_all | solution.py:241
  21.2 2.5 %copy-start.1 = (bf16[2,512,2560]{2,1,0:T(8,128)(2,1)S(1)}, bf16[2,512,2560]{2,1,0:T(8,128)(2,1)}, u32[]{:S(2)}) copy-start(bf16[2,512,2560]{2,1,0:T(8,128)(2,1)} %param.10) | copy-start | bytes 15728644
  23.7 1.9 %copy-start.12 = (bf16[2560,640]{1,0:T(8,128)(2,1)S(1)}, bf16[2560,640]{1,0:T(8,128)(2,1)}, u32[]{:S(2)}) copy-start(bf16[2560,640]{1,0:T(8,128)(2,1)} %weight.2) | copy-start | bytes 9830404
  34.8 26.9 %copy-start.15 = (f32[1024,128]{1,0:T(8,128)}, f32[1024,128]{1,0:T(8,128)S(1)}, u32[]{:S(2)}) copy-start(f32[1024,128]{1,0:T(8,128)S(1)} %get-tuple-element.22.opening) | copy-start | bytes 1572868
  34.8 41.5 %copy-start.3 = (bf16[1024,640]{1,0:T(8,128)(2,1)}, bf16[1024,640]{1,0:T(8,128)(2,1)S(1)}, u32[]{:S(2)}) copy-start(bf16[1024,640]{1,0:T(8,128)(2,1)S(1)} %get-tuple-element.15.scaled) | copy-start | bytes 3932164
  40.6 1.1 %copy-start.7 = (bf16[8,128,640]{2,1,0:T(8,128)(2,1)}, bf16[8,128,640]{2,1,0:T(8,128)(2,1)S(1)}, u32[]{:S(2)}) copy-start(bf16[8,128,640]{2,1,0:T(8,128)(2,1)S(1)} %get-tuple-element.21.starts) | copy-start | bytes 3932164
  61.7 18.6 %all-to-all-start.2 = ((bf16[32,8,640]{2,1,0:T(8,128)(2,1)}), bf16[32,8,640]{2,1,0:T(8,128)(2,1)S(1)}, u32[]{:S(2)}, u32[]{:S(2)}) async-start(bf16[32,8,640]{2,1,0:T(8,128)(2,1)} %shard_map.103), calls=%async_computation.2 | async-start | bytes 655360 | tf_op jit(solution)/shard_map/all_to_all | solution.py:287
  65.5 2.5 %copy-start.2 = (bf16[2,512,2560]{2,1,0:T(8,128)(2,1)S(1)}, bf16[2,512,2560]{2,1,0:T(8,128)(2,1)}, u32[]{:S(2)}) copy-start(bf16[2,512,2560]{2,1,0:T(8,128)(2,1)} %param.10) | copy-start | bytes 15728644
  68.0 1.9 %copy-start.13 = (bf16[2560,640]{1,0:T(8,128)(2,1)S(1)}, bf16[2560,640]{1,0:T(8,128)(2,1)}, u32[]{:S(2)}) copy-start(bf16[2560,640]{1,0:T(8,128)(2,1)} %weight.3) | copy-start | bytes 9830404
  69.9 1.0 %copy-start.16 = (f32[1024,128]{1,0:T(8,128)S(1)}, f32[1024,128]{1,0:T(8,128)}, u32[]{:S(2)}) copy-start(f32[1024,128]{1,0:T(8,128)} %copy-done.15) | copy-start | bytes 1572868
  71.0 6.5 %copy-start.8 = (bf16[8,128,640]{2,1,0:T(8,128)(2,1)S(1)}, bf16[8,128,640]{2,1,0:T(8,128)(2,1)}, u32[]{:S(2)}) copy-start(bf16[8,128,640]{2,1,0:T(8,128)(2,1)} %copy-done.7) | copy-start | bytes 3932164
  76.4 1.1 %copy-start.9 = (bf16[1024,640]{1,0:T(8,128)(2,1)}, bf16[1024,640]{1,0:T(8,128)(2,1)S(1)}, u32[]{:S(2)}) copy-start(bf16[1024,640]{1,0:T(8,128)(2,1)S(1)} %shard_map.105.opened) | copy-start | bytes 3932164
  77.5 1.3 %copy-start.4 = (bf16[1024,640]{1,0:T(8,128)(2,1)S(1)}, bf16[1024,640]{1,0:T(8,128)(2,1)}, u32[]{:S(2)}) copy-start(bf16[1024,640]{1,0:T(8,128)(2,1)} %copy-done.3) | copy-start | bytes 3932164
  78.8 9.6 %copy-start.19 = (f32[640]{0:T(1024)S(1)}, f32[640]{0:T(1024)}, u32[]{:S(2)}) copy-start(f32[640]{0:T(1024)} %param.19) | copy-start | bytes 7684
  80.3 1.3 %copy-start.10 = (bf16[1024,640]{1,0:T(8,128)(2,1)S(1)}, bf16[1024,640]{1,0:T(8,128)(2,1)}, u32[]{:S(2)}) copy-start(bf16[1024,640]{1,0:T(8,128)(2,1)} %copy-done.9) | copy-start | bytes 3932164
  83.5 1.5 %copy-start.5 = (f32[1024,640]{1,0:T(8,128)}, f32[1024,640]{1,0:T(8,128)S(1)}, u32[]{:S(2)}) copy-start(f32[1024,640]{1,0:T(8,128)S(1)} %get-tuple-element.23.gated) | copy-start | bytes 7864324
  85.0 10.0 %all-to-all-start.3 = ((f32[8,8,128]{2,1,0:T(8,128)}), f32[8,8,128]{2,1,0:T(8,128)S(1)}, u32[]{:S(2)}, u32[]{:S(2)}) async-start(f32[8,8,128]{2,1,0:T(8,128)} %get-tuple-element.24), calls=%async_computation.3 | async-start | bytes 65536 | tf_op jit(solution)/shard_map/all_to_all | solution.py:292
  95.0 1.7 %copy-start.6 = (f32[1024,640]{1,0:T(8,128)S(1)}, f32[1024,640]{1,0:T(8,128)}, u32[]{:S(2)}) copy-start(f32[1024,640]{1,0:T(8,128)} %copy-done.5) | copy-start | bytes 7864324

commit v2 on v1

v2 whole, which is shorter than its diff:
```python
import functools

import jax
import jax.numpy as jnp
from jax import lax
from jax.experimental import pallas as pl
from jax.experimental.pallas import tpu as pltpu
from jax.sharding import Mesh
from jax.sharding import PartitionSpec as P

DI = 5120
HEAD_DIM = 64
STATE = 128
CONV = 4
BLOCK = 128
LANES = 128
EPSILON = 1e-05

F32 = jnp.float32
BF16 = jnp.bfloat16
HIGHEST = lax.Precision.HIGHEST
NT = (((1,), (1,)), ((), ()))


def dot(a, b):
    return jnp.dot(a, b, preferred_element_type=F32)


def dot_nt(a, b):
    return lax.dot_general(a, b, NT, preferred_element_type=F32)


def silu(x):
    return x / (1.0 + jnp.exp(-x))


def split_in_three(x):
    high = x.astype(BF16)
    rest = x - high.astype(F32)
    middle = rest.astype(BF16)
    return high, middle, (rest - middle.astype(F32)).astype(BF16)


def head_lanes(width):
    head = lax.broadcasted_iota(jnp.int32, (LANES, width), 1) // HEAD_DIM
    row = lax.broadcasted_iota(jnp.int32, (LANES, width), 0)
    return (head == row).astype(BF16)


def over_channels(x, spread):
    high, middle, low = split_in_three(x)
    return dot(high, spread) + dot(middle, spread) + dot(low, spread)


def transposed(part, pad):
    pad[:, : part.shape[1]] = part
    return jnp.transpose(pad[...])[: part.shape[1]].astype(BF16)


def bc_kernel(hidden, weight, out, pad):
    pad[...] = jnp.zeros_like(pad)
    out[...] = transposed(dot_nt(hidden[...], weight[...]), pad)


def join_kernel(batch, halo, weight, own, out, pad):
    share = weight.shape[0]
    before = dot_nt(halo[...], weight[...])
    pad[...] = jnp.zeros_like(pad)
    for b in range(batch):
        pad[LANES - 8 - 64 * b : LANES - 64 * b, :share] = before[8 * b : 8 * b + 8]
    tile = jnp.transpose(pad[...])[:share].astype(BF16)
    for d in range(out.shape[0]):
        out[d, :, :LANES] = tile
        out[d, :, LANES:] = own[...]


def project_kernel(
    batch, length, chunk, hidden, value_weight, gate_weight, halo, taps, step_weight, step_bias,
    log_rate, gain, scaled, opened, rows, decays, hid, vw, gw, padded, scaled_v, opened_v, sems,
):
    inner = vw.shape[1]
    tokens = batch * length
    chunks = tokens // chunk
    spread = head_lanes(inner)

    def fetch(c):
        at = pl.ds(c * chunk, chunk)
        return pltpu.make_async_copy(hidden.at[at, :], hid.at[at, :], sems.at[c])

    def store(c, source, target, k):
        at = pl.ds(c * chunk, chunk)
        return pltpu.make_async_copy(source.at[at, :], target.at[at, :], sems.at[k * chunks + 2 + c])

    value_copy = pltpu.make_async_copy(value_weight, vw, sems.at[chunks])
    gate_copy = pltpu.make_async_copy(gate_weight, gw, sems.at[chunks + 1])
    value_copy.start()
    fetch(0).start()
    rate = jnp.exp(log_rate[0:1, :])
    i = lax.broadcasted_iota(jnp.int32, (BLOCK, BLOCK), 0)
    j = lax.broadcasted_iota(jnp.int32, (BLOCK, BLOCK), 1)
    lower = (i >= j).astype(BF16)
    halves, offsets = [], []
    fetch(0).wait()
    value_copy.wait()
    for c in range(1, chunks):
        fetch(c).start()
    gate_copy.start()
    before = dot(halo[...], vw[...]).astype(BF16).astype(F32)
    for c in range(chunks):
        at = slice(c * chunk, (c + 1) * chunk)
        b = c * chunk // length
        if c:
            fetch(c).wait()
        own = hid[at, :]
        if c * chunk % length == 0:
            padded[0:8, :] = before[8 * b : 8 * b + 8]
            total = jnp.zeros((1, LANES), F32)
        else:
            padded[0:8, :] = padded[chunk : chunk + 8, :]
        padded[8 : 8 + chunk, :] = dot(own, vw[...]).astype(BF16).astype(F32)
        step_pre = dot_nt(own, step_weight[...]) + step_bias[0:1, :]
        steps = jnp.maximum(step_pre, 0.0) + jnp.log1p(jnp.exp(-jnp.abs(step_pre)))
        opening = []
        for r in range(0, chunk, BLOCK):
            step = steps[r : r + BLOCK]
            high, middle, low = split_in_three(-step * rate)
            cumulative = dot(lower, high) + dot(lower, middle) + dot(lower, low)
            last = cumulative[BLOCK - 1 : BLOCK, :]
            centered = cumulative - 0.5 * last
            halves.append(0.5 * last)
            offsets.append(total + 0.5 * last)
            total = total + last
            value = sum(
                taps[t : t + 1, :] * padded[r + 5 + t : r + 5 + t + BLOCK, :] for t in range(CONV)
            )
            ahead = over_channels(jnp.exp(-centered) * step, spread)
            scaled_v[c * chunk + r : c * chunk + r + BLOCK, :] = (silu(value) * ahead).astype(BF16)
            opening.append(jnp.exp(centered))
        store(c, scaled_v, scaled, 1).start()
        if (c + 1) * chunk % length == 0:
            high, middle, low = split_in_three(total)
            decays[b] = jnp.concatenate([high, middle, low, jnp.zeros((5, LANES), BF16)], axis=0)
        if c == 0:
            gate_copy.wait()
        gate = dot(own, gw[...]).astype(BF16).astype(F32)
        behind = over_channels(jnp.concatenate(opening, axis=0), spread)
        opened_v[at, :] = (silu(gate) * behind).astype(BF16)
        store(c, opened_v, opened, 2).start()
    count = len(halves) + len(offsets)
    rows[:count, :] = jnp.exp(over_channels(jnp.concatenate(halves + offsets, axis=0), spread))
    rows[count:, :] = jnp.concatenate([gain[0:1, :]] * (rows.shape[0] - count), axis=0)
    for c in range(chunks):
        store(c, scaled_v, scaled, 1).wait()
        store(c, opened_v, opened, 2).wait()


def state_kernel(batch, length, bc, taps, scaled, rows, decays, b_rows, c_rows, starts, sent):
    blocks = length // BLOCK
    inner = scaled.shape[1]
    halo = bc[:, :LANES].astype(F32)
    for b in range(batch):
        own = bc[:, LANES + b * length : LANES + (b + 1) * length].astype(F32)
        before = pltpu.roll(halo, 64 * b, 1) if b else halo
        padded = jnp.concatenate([before, own], axis=1)
        mixed = taps[:, CONV - 1 : CONV] * own
        for t in range(CONV - 1):
            mixed = mixed + taps[:, t : t + 1] * pltpu.roll(padded, CONV - 1 - t, 1)[:, LANES:]
        mixed = silu(mixed)
        b_t = mixed[:STATE].astype(BF16)
        b_rows[b] = b_t
        c_rows[b * length : (b + 1) * length, :] = jnp.transpose(mixed[STATE:]).astype(BF16)
        state = jnp.zeros((STATE, inner), F32)
        for k in range(blocks):
            n = b * blocks + k
            half = rows[n : n + 1, :]
            ready = half * state
            starts[n] = ready.astype(BF16)
            at = b * length + k * BLOCK
            added = dot(b_t[:, k * BLOCK : (k + 1) * BLOCK], scaled[at : at + BLOCK, :])
            state = half * (ready + added)
        for g in range(STATE // 8):
            sent[b, g, :, :inner] = state[8 * g : 8 * g + 8].astype(BF16)
            sent[b, g, :, inner:] = decays[b]


def scan_kernel(got, out, table, logs):
    devices, _, width = got.shape
    inner = width - LANES
    for s in range(devices):
        parts = got[s, :, inner:].astype(F32)
        table[s : s + 1, :] = parts[0:1] + parts[1:2] + parts[2:3]
    logs[...] = jnp.exp(over_channels(table[...], head_lanes(inner)))
    state = jnp.zeros((8, inner), F32)
    for s in range(devices):
        out[s] = state.astype(BF16)
        state = logs[s : s + 1, :] * state + got[s, :, :inner].astype(F32)


def gated_kernel(
    batch, length, arrived, b_rows, c_rows, scaled, starts, opened, rows, gated, squares
):
    blocks = length // BLOCK
    count = batch * blocks
    ones = jnp.ones((8, scaled.shape[1]), BF16)
    i = lax.broadcasted_iota(jnp.int32, (BLOCK, BLOCK), 0)
    j = lax.broadcasted_iota(jnp.int32, (BLOCK, BLOCK), 1)
    for b in range(batch):
        for k in range(blocks):
            n = b * blocks + k
            at = slice(n * BLOCK, (n + 1) * BLOCK)
            c = c_rows[at, :]
            scores = dot(c, b_rows[b, :, k * BLOCK : (k + 1) * BLOCK])
            scores = jnp.where(i >= j, scores, 0.0).astype(BF16)
            y = dot(scores, scaled[at, :]) + dot(c, starts[n])
            y = y + rows[count + n : count + n + 1, :] * dot(c, arrived[b])
            g = y * opened[at, :].astype(F32)
            gated[at, :] = g
            squares[:, n, :] = dot_nt(ones, (g * g).astype(BF16))


def scale_kernel(gated, squares, rows, out):
    total = squares[0]
    for d in range(1, squares.shape[0]):
        total = total + squares[d]
    scale = lax.rsqrt(total / DI + EPSILON)
    count = scale.shape[0]
    scale = jnp.concatenate([scale, jnp.zeros((LANES - count, LANES), F32)], axis=0)
    columns = jnp.transpose(scale)
    gain = rows[2 * count : 2 * count + 1, :]
    for n in range(count):
        at = slice(n * LANES, (n + 1) * LANES)
        out[at, :] = (gated[at, :] * columns[:, n : n + 1] * gain).astype(BF16)


ANY = pl.BlockSpec(memory_space=pl.ANY)
WHOLE = pl.BlockSpec(memory_space=pltpu.VMEM)


def call(kernel, out, ins=None, scratch=(), mib=12, flops=0, outs=None, grid=()):
    shapes = [jax.ShapeDtypeStruct(s, d) for s, d in out]
    specs = {} if ins is None else {"in_specs": ins}
    if outs is not None:
        specs["out_specs"] = outs if len(outs) > 1 else outs[0]
    return pl.pallas_call(
        kernel,
        out_shape=shapes if len(shapes) > 1 else shapes[0],
        grid=grid,
        scratch_shapes=[s if not isinstance(s, tuple) else pltpu.VMEM(*s) for s in scratch],
        compiler_params=pltpu.CompilerParams(vmem_limit_bytes=mib << 20),
        cost_estimate=pl.CostEstimate(flops=flops, transcendentals=0, bytes_accessed=0)
        if flops
        else None,
        **specs,
    )


def on_device(
    hidden_in, gate_proj, value_proj, bc_proj, step_proj, value_conv, bc_conv, step_bias, log_rate,
    norm_gain,
):
    batch, length, width = hidden_in.shape
    tokens = batch * length
    inner = value_proj.shape[1]
    heads = step_proj.shape[1]
    share = bc_proj.shape[1]
    states = 2 * STATE
    blocks = tokens // BLOCK
    seq, tp = lax.axis_size("seq"), lax.axis_size("tp")
    hidden = hidden_in.reshape(tokens, width)
    tail = hidden_in[:, length - 8 :, :]
    halo = lax.ppermute(tail, "seq", [(i, i + 1) for i in range(seq - 1)]).reshape(8 * batch, width)
    chunk = 256
    own = call(
        bc_kernel,
        [((share, tokens), BF16)],
        ins=[
            pl.BlockSpec((chunk, width), lambda c: (c, 0)),
            pl.BlockSpec((share, width), lambda c: (0, 0)),
        ],
        outs=[pl.BlockSpec((share, chunk), lambda c: (0, c))],
        scratch=[((chunk, LANES), F32)],
        grid=(tokens // chunk,),
        mib=60,
        flops=2 * tokens * width * share,
    )(hidden, bc_proj.T)
    bc_part = call(
        functools.partial(join_kernel, batch),
        [((tp, share, tokens + LANES), BF16)],
        scratch=[((LANES, LANES), F32)],
    )(halo, bc_proj.T, own)
    bc = lax.all_to_all(bc_part, "tp", 0, 0, tiled=True).reshape(states, tokens + LANES)
    scaled, opened, rows, decays = call(
        functools.partial(project_kernel, batch, length, chunk),
        [
            ((tokens, inner), BF16),
            ((tokens, inner), BF16),
            ((2 * blocks + 8, inner), F32),
            ((batch, 8, LANES), BF16),
        ],
        ins=[ANY, ANY, ANY] + [WHOLE] * 6,
        outs=[ANY, ANY, WHOLE, WHOLE],
        scratch=[
            ((tokens, width), BF16),
            ((width, inner), BF16),
            ((width, inner), BF16),
            ((chunk + 8, inner), F32),
            ((tokens, inner), BF16),
            ((tokens, inner), BF16),
            pltpu.SemaphoreType.DMA((3 * (tokens // chunk) + 2,)),
        ],
        mib=60,
        flops=4 * tokens * width * inner,
    )(
        hidden,
        value_proj,
        gate_proj,
        halo,
        value_conv,
        jnp.pad(step_proj.T, ((0, LANES - heads), (0, 0))),
        jnp.pad(step_bias, (0, LANES - heads)).reshape(1, LANES),
        jnp.pad(log_rate, (0, LANES - heads), constant_values=-1e30).reshape(1, LANES),
        norm_gain.reshape(1, inner),
    )
    b_rows, c_rows, starts, sent = call(
        functools.partial(state_kernel, batch, length),
        [
            ((batch, STATE, length), BF16),
            ((tokens, STATE), BF16),
            ((blocks, STATE, inner), BF16),
            ((batch, STATE // 8, 8, inner + LANES), BF16),
        ],
        mib=16,
    )(bc, bc_conv.T, scaled, rows, decays)
    got = lax.all_to_all(sent.reshape(seq, -1, inner + LANES), "seq", 0, 0, tiled=True)
    prefix = call(
        scan_kernel,
        [((seq, 8, inner), BF16)],
        scratch=[((seq, LANES), F32), ((seq, inner), F32)],
    )(got)
    arrived = lax.all_to_all(prefix, "seq", 0, 0, tiled=True).reshape(batch, STATE, inner)
    gated, squares = call(
        functools.partial(gated_kernel, batch, length),
        [((tokens, inner), F32), ((tp, blocks, LANES), F32)],
        mib=16,
    )(arrived, b_rows, c_rows, scaled, starts, opened, rows)
    whole = lax.all_to_all(squares, "tp", 0, 0, tiled=True)
    out = call(scale_kernel, [((tokens, inner), BF16)], mib=12)(gated, whole, rows)
    return out.reshape(batch, length, inner)


def solution(mesh):
    placed = (
        P(None, "seq", None),
        P(None, "tp"),
        P(None, "tp"),
        P(None, "tp"),
        P(None, "tp"),
        P(None, "tp"),
        P(),
        P("tp"),
        P("tp"),
        P("tp"),
    )
    return jax.shard_map(
        on_device, mesh=mesh, in_specs=placed, out_specs=P(None, "seq", "tp"), check_vma=False
    )
```

time: 99.1 us -> 97.9 us (0.988)
  blocking collectives: 19 us -> 43 us
  local copies, waits for them, and re-layouts: 22.4 us -> 6.83 us
  waiting for transfers between devices: 12 us -> 0.01 us
  Pallas kernels: 24.7 us -> 34.6 us
  starting transfers between devices: 19.9 us -> 12.7 us
    all_to_all x0 -> x2, blocking collectives: none -> 26.2 us  [the longest x1 13.2 us: on_device(): whole = lax.all_to_all(squares, 'tp', 0, 0, tiled=True)]
    unnamed x45 -> x27, local copies, waits for them, and re-layouts: 21.4 us -> 3.86 us
    pallas_call x6 -> x5, Pallas kernels: 21 us -> 30.5 us  [the longest x1 22.5 us: on_device(): call(functools.partial(project_kernel, batch, length, chunk), [((tokens,...]
    all_to_all x2 -> x0, starting transfers between devices: 7.18 us -> none  [the longest x1 3.84 us: on_device(): lax.all_to_all(prefix, 'seq', 0, 0, tiled=True).reshape(batch, STATE, inner)]
    all_to_all x2 -> x0, waiting for transfers between devices: 6.6 us -> none  [the longest x1 6.6 us: on_device(): whole = lax.all_to_all(squares, 'tp', 0, 0, tiled=True)]
    all_to_all x1, waiting for transfers between devices: 3.93 us -> 0.01 us  [on_device(): lax.all_to_all(bc_part, 'tp', 0, 0, tiled=True)]
    all_to_all x1, blocking collectives: 19 us -> 16.9 us  [on_device(): lax.all_to_all(sent.reshape(seq, -1, inner + LANES), 'seq', 0, 0, tiled=T...]
    ppermute x1, waiting for transfers between devices: 1.46 us -> 0.01 us  [on_device(): lax.ppermute(tail, 'seq', [(i, i + 1) for i in range(seq - 1)])]
  transfers between devices with their start and end apart: 4 -> 2, of which waited for: 3 -> 0; matrix products, arithmetic and copies ran while one was open for 0% -> 2% of each run, Pallas kernels for 16% -> 28%
where the time goes in v2:
time: 97.9 us; the launch traced here: 97.3 us
  blocking collectives  43 us (44%)
  Pallas kernels  34.6 us (35%)
  starting transfers between devices  12.7 us (13%)
  local copies, waits for them, and re-layouts  6.83 us (7%)
    pallas_call x1, Pallas kernels, on_device(): call(functools.partial(project_kernel, batch, length, chunk), [((tokens,...  22.5 us
    all_to_all x1, blocking collectives, on_device(): lax.all_to_all(sent.reshape(seq, -1, inner + LANES), 'seq', 0, 0, tiled=T...  16.9 us
    all_to_all x1, blocking collectives, on_device(): whole = lax.all_to_all(squares, 'tp', 0, 0, tiled=True)  13.2 us
    all_to_all x1, blocking collectives, on_device(): lax.all_to_all(prefix, 'seq', 0, 0, tiled=True).reshape(batch, STATE, inner)  13 us
    all_to_all x1, starting transfers between devices, on_device(): lax.all_to_all(bc_part, 'tp', 0, 0, tiled=True)  8.17 us
    pallas_call x1, Pallas kernels, on_device(): call(bc_kernel, [((share, tokens), BF16)], ins=[pl.BlockSpec((chunk, widt...  5.18 us
    ppermute x1, starting transfers between devices, on_device(): lax.ppermute(tail, 'seq', [(i, i + 1) for i in range(seq - 1)])  4.49 us
    unnamed x27, local copies, waits for them, and re-layouts  3.86 us
  transfers between devices with their start and end apart: 2, of which 0 were waited for; matrix products, arithmetic and copies ran while one was open for 2% of the time, Pallas kernels for 28%

profile of v2, /device:TPU:1, one launch (start us, length us, event | category | flops | bytes accessed | tf_op | source)
XLA Modules:
  0.0 97.3 jit_solution(18230832597051910369)
XLA Ops:
  0.0 0.9 slice.3
  0.9 4.5 %collective-permute-start = (bf16[2,8,2560]{2,1,0:T(8,128)(2,1)S(1)}, bf16[2,8,2560]{2,1,0:T(8,128)(2,1)S(1)}, u32[]{:S(2)}, u32[]{:S(2)}) collective-permute-start(bf16[2,8,2560]{2,1,0:T(8,128)(2,1)S(1)} %slice.3), channel_id=1, source_target_pairs={{0,8},{8,16},{16,24},{24,32},{32,40},{40,48},{48,56},{56,64},{64,7... | collective-permute-start | bytes 245768 | tf_op jit(solution)/shard_map/ppermute | solution.py:271
  5.4 0.0 copy-start.2
  5.4 0.0 copy-start.10
  5.4 0.0 copy-start.9
  5.4 0.0 copy-start.8
  5.4 5.2 %shard_map.100.own = bf16[32,1024]{1,0:T(8,128)(2,1)} custom-call(bf16[1024,2560]{1,0:T(8,128)(2,1)} %bitcast.21, bf16[32,2560]{1,0:T(8,128)(2,1)} %bitcast.15), custom_call_target="tpu_custom_call" | custom-call | flops 167772160 | tf_op jit(solution)/shard_map/pallas_call | solution.py:273
  10.6 0.0 copy-start.11
  10.6 0.0 copy-start.12
  10.6 0.0 collective-permute-done
  10.6 0.0 copy-start.6
  10.6 0.0 copy-done.2
  10.7 0.0 copy-start.5
  10.7 0.9 copy-done.5
  11.5 1.1 %shard_map.101 = bf16[8,32,1152]{2,1,0:T(8,128)(2,1)} custom-call(bf16[16,2560]{1,0:T(8,128)(2,1)S(1)} %bitcast.19, bf16[32,2560]{1,0:T(8,128)(2,1)S(1)} %bitcast.16, bf16[32,1024]{1,0:T(8,128)(2,1)S(1)} %copy-done.5), custom_call_target="tpu_custom_call" | custom-call | tf_op jit(solution)/shard_map/pallas_call | solution.py:286
  12.6 8.2 %all-to-all-start = ((bf16[8,32,1152]{2,1,0:T(8,128)(2,1)}), bf16[8,32,1152]{2,1,0:T(8,128)(2,1)S(1)}, u32[]{:S(2)}, u32[]{:S(2)}) async-start(bf16[8,32,1152]{2,1,0:T(8,128)(2,1)} %shard_map.101), calls=%async_computation | async-start | bytes 1179648 | tf_op jit(solution)/shard_map/all_to_all | solution.py:291
  20.8 0.0 copy-done.10
  20.8 0.6 reshape.32.gain
  21.4 0.0 copy-done.9
  21.4 0.1 copy.11
  21.5 0.0 copy-done.8
  21.5 0.9 pad.12.step_weight
  22.4 0.0 copy-done.11
  22.4 0.0 copy-done.12
  22.4 0.6 pad_bitcast_fusion
  23.0 0.0 copy-done.6
  23.0 22.5 %shard_map.102 = (bf16[1024,640]{1,0:T(8,128)(2,1)}, bf16[1024,640]{1,0:T(8,128)(2,1)}, f32[24,640]{1,0:T(8,128)}, bf16[2,8,128]{2,1,0:T(8,128)(2,1)}) custom-call(bf16[1024,2560]{1,0:T(8,128)(2,1)} %bitcast.22, bf16[2560,640]{1,0:T(8,128)(2,1)} %value_weight.1, bf16[2560,640]{1,0:T(8,128)(2,1)} %gate_weight.1, bf16[16,2560]{1,0:T(8,128)(2,1)} %bitcast.20, ...), custom_call_target="tpu_custom_call" | custom-call | flops 6710886400 | tf_op jit(solution)/shard_map/pallas_call | solution.py:292
  45.5 0.0 all-to-all-done
  45.5 0.0 copy-start
  45.6 1.3 %copy-done = bf16[1024,640]{1,0:T(8,128)(2,1)S(1)} copy-done((bf16[1024,640]{1,0:T(8,128)(2,1)S(1)}, bf16[1024,640]{1,0:T(8,128)(2,1)}, u32[]{:S(2)}) %copy-start) | copy-done | bytes 1310744
  46.9 0.0 copy-start.3
  46.9 0.8 copy-done.3
  47.7 0.0 copy-start.7
  47.7 0.7 copy-done.7
  48.4 0.0 copy-start.1
  48.4 0.0 copy-start.4
  48.4 1.8 %shard_map.103 = (bf16[2,128,512]{2,1,0:T(8,128)(2,1)S(1)}, bf16[1024,128]{1,0:T(8,128)(2,1)S(1)}, bf16[8,128,640]{2,1,0:T(8,128)(2,1)S(1)}, bf16[2,16,8,768]{3,2,1,0:T(8,128)(2,1)S(1)}) custom-call(bf16[256,1152]{1,0:T(8,128)(2,1)S(1)} %bitcast.13, f32[256,4]{1,0:T(8,128)S(1)} %bitcast.17, bf16[1024,640]{1,0:T(8,128)(2,1)S(1)} %copy-done, ...), custom_call_target="tpu_custom_call" | custom-call | tf_op jit(solution)/shard_map/pallas_call | solution.py:324
  50.2 16.9 %all_to_all.20.got = bf16[32,8,768]{2,1,0:T(8,128)(2,1)S(1)} all-to-all(bf16[32,8,768]{2,1,0:T(8,128)(2,1)S(1)} %bitcast.18), channel_id=1, replica_groups=mesh['seq'=32,'tp'=8] {'seq'}, dimensions={0} | all-to-all | bytes 786432 | tf_op jit(solution)/shard_map/all_to_all | solution.py:334
  67.0 0.3 shard_map.104
  67.4 13.0 %all_to_all.21 = bf16[32,8,640]{2,1,0:T(8,128)(2,1)S(1)} all-to-all(bf16[32,8,640]{2,1,0:T(8,128)(2,1)S(1)} %shard_map.104), channel_id=1, replica_groups=mesh['seq'=32,'tp'=8] {'seq'}, dimensions={0} | all-to-all | bytes 655360 | tf_op jit(solution)/shard_map/all_to_all | solution.py:340
  80.4 0.0 copy-done.1
  80.4 0.0 copy-done.4
  80.4 2.3 %shard_map.105 = (f32[1024,640]{1,0:T(8,128)S(1)}, f32[8,8,128]{2,1,0:T(8,128)S(1)}) custom-call(bf16[2,128,640]{2,1,0:T(8,128)(2,1)S(1)} %bitcast.14, bf16[2,128,512]{2,1,0:T(8,128)(2,1)S(1)} %get-tuple-element.19.b_rows, bf16[1024,128]{1,0:T(8,128)(2,1)S(1)} %get-tuple-element.20.c_rows, bf16[1024,640]{1,0:T(8,128)(2,1)S(1)} %copy-done, ...), custom_call_target="tpu_custom_call" | custom-call | tf_op jit(solution)/shard_map/pallas_call | solution.py:341
  82.7 13.2 %all_to_all.22.squares = f32[8,8,128]{2,1,0:T(8,128)S(1)} all-to-all(f32[8,8,128]{2,1,0:T(8,128)S(1)} %get-tuple-element.24), channel_id=1, replica_groups=mesh['seq'=32,'tp'=8] {'tp'}, dimensions={0} | all-to-all | bytes 65536 | tf_op jit(solution)/shard_map/all_to_all | solution.py:346
  95.8 1.4 %shard_map.106 = bf16[1024,640]{1,0:T(8,128)(2,1)} custom-call(f32[1024,640]{1,0:T(8,128)S(1)} %get-tuple-element.23.gated, f32[8,8,128]{2,1,0:T(8,128)S(1)} %all_to_all.22.squares, f32[24,640]{1,0:T(8,128)S(1)} %copy-done.4), custom_call_target="tpu_custom_call" | custom-call | tf_op jit(solution)/shard_map/pallas_call | solution.py:347
Async XLA Ops:
  0.9 9.7 %collective-permute-start = (bf16[2,8,2560]{2,1,0:T(8,128)(2,1)S(1)}, bf16[2,8,2560]{2,1,0:T(8,128)(2,1)S(1)}, u32[]{:S(2)}, u32[]{:S(2)}) collective-permute-start(bf16[2,8,2560]{2,1,0:T(8,128)(2,1)S(1)} %slice.3), channel_id=1, source_target_pairs={{0,8},{8,16},{16,24},{24,32},{32,40},{40,48},{48,56},{56,64},{64,7... | collective-permute-start | bytes 245768 | tf_op jit(solution)/shard_map/ppermute | solution.py:271
  5.4 5.2 %copy-start.2 = (bf16[2560,32]{0,1:T(8,128)(2,1)S(1)}, bf16[2560,32]{0,1:T(8,128)(2,1)}, u32[]{:S(2)}) copy-start(bf16[2560,32]{0,1:T(8,128)(2,1)} %param.13) | copy-start | bytes 491524
  5.4 15.4 %copy-start.10 = (f32[640]{0:T(1024)S(1)}, f32[640]{0:T(1024)}, u32[]{:S(2)}) copy-start(f32[640]{0:T(1024)} %param.19) | copy-start | bytes 7684
  5.4 15.9 %copy-start.9 = (f32[4,256]{1,0:T(4,128)S(1)}, f32[4,256]{1,0:T(4,128)}, u32[]{:S(2)}) copy-start(f32[4,256]{1,0:T(4,128)} %param.16) | copy-start | bytes 12292
  5.4 16.1 %copy-start.8 = (bf16[2560,10]{0,1:T(8,128)(2,1)S(1)}, bf16[2560,10]{0,1:T(8,128)(2,1)}, u32[]{:S(2)}) copy-start(bf16[2560,10]{0,1:T(8,128)(2,1)} %param.14) | copy-start | bytes 153604
  10.6 11.8 %copy-start.11 = (f32[10]{0:T(128)S(1)}, f32[10]{0:T(128)}, u32[]{:S(2)}) copy-start(f32[10]{0:T(128)} %param.18) | copy-start | bytes 124
  10.6 11.8 %copy-start.12 = (f32[10]{0:T(128)S(1)}, f32[10]{0:T(128)}, u32[]{:S(2)}) copy-start(f32[10]{0:T(128)} %param.17) | copy-start | bytes 124
  10.6 12.4 %copy-start.6 = (bf16[2,8,2560]{2,1,0:T(8,128)(2,1)}, bf16[2,8,2560]{2,1,0:T(8,128)(2,1)S(1)}, u32[]{:S(2)}) copy-start(bf16[2,8,2560]{2,1,0:T(8,128)(2,1)S(1)} %collective-permute-done) | copy-start | bytes 245764
  10.7 0.9 copy-start.5
  12.6 32.9 %all-to-all-start = ((bf16[8,32,1152]{2,1,0:T(8,128)(2,1)}), bf16[8,32,1152]{2,1,0:T(8,128)(2,1)S(1)}, u32[]{:S(2)}, u32[]{:S(2)}) async-start(bf16[8,32,1152]{2,1,0:T(8,128)(2,1)} %shard_map.101), calls=%async_computation | async-start | bytes 1179648 | tf_op jit(solution)/shard_map/all_to_all | solution.py:291
  45.5 1.3 %copy-start = (bf16[1024,640]{1,0:T(8,128)(2,1)S(1)}, bf16[1024,640]{1,0:T(8,128)(2,1)}, u32[]{:S(2)}) copy-start(bf16[1024,640]{1,0:T(8,128)(2,1)} %get-tuple-element.15.scaled) | copy-start | bytes 3932164
  46.9 0.8 copy-start.3
  47.7 0.7 copy-start.7
  48.4 32.0 %copy-start.1 = (bf16[1024,640]{1,0:T(8,128)(2,1)S(1)}, bf16[1024,640]{1,0:T(8,128)(2,1)}, u32[]{:S(2)}) copy-start(bf16[1024,640]{1,0:T(8,128)(2,1)} %get-tuple-element.22.opened) | copy-start | bytes 3932164
  48.4 32.0 %copy-start.4 = (f32[24,640]{1,0:T(8,128)S(1)}, f32[24,640]{1,0:T(8,128)}, u32[]{:S(2)}) copy-start(f32[24,640]{1,0:T(8,128)} %get-tuple-element.16.rows) | copy-start | bytes 184324

commit v3 on v1

v3 whole, which is shorter than its diff:
```python
import functools

import jax
import jax.numpy as jnp
from jax import lax
from jax.experimental import pallas as pl
from jax.experimental.pallas import tpu as pltpu
from jax.sharding import Mesh
from jax.sharding import PartitionSpec as P

DI = 5120
HEAD_DIM = 64
STATE = 128
CONV = 4
BLOCK = 128
LANES = 128
EPSILON = 1e-05

F32 = jnp.float32
BF16 = jnp.bfloat16
HIGHEST = lax.Precision.HIGHEST
NT = (((1,), (1,)), ((), ()))


def dot(a, b):
    return jnp.dot(a, b, preferred_element_type=F32)


def dot_nt(a, b):
    return lax.dot_general(a, b, NT, preferred_element_type=F32)


def silu(x):
    half = 0.5 * x
    return half + half * jnp.tanh(half)


def split_in_three(x):
    high = x.astype(BF16)
    rest = x - high.astype(F32)
    middle = rest.astype(BF16)
    return high, middle, (rest - middle.astype(F32)).astype(BF16)


def head_lanes(width):
    head = lax.broadcasted_iota(jnp.int32, (2 * LANES, width), 1) // HEAD_DIM
    row = lax.broadcasted_iota(jnp.int32, (2 * LANES, width), 0)
    return (head == lax.rem(row, LANES)).astype(BF16)


def over_channels(x, spread):
    high, middle, _ = split_in_three(x)
    return dot(jnp.concatenate([high, middle], axis=1), spread)


def transposed(part, pad):
    pad[:, : part.shape[1]] = part
    return jnp.transpose(pad[...])[: part.shape[1]].astype(BF16)


def bc_kernel(chunk, hidden, weight, out, pad):
    pad[...] = jnp.zeros_like(pad)
    for r in range(0, hidden.shape[0], chunk):
        part = dot_nt(hidden[r : r + chunk, :], weight[...])
        out[:, r : r + chunk] = transposed(part, pad)


def join_kernel(batch, halo, weight, own, out, pad):
    share = weight.shape[0]
    before = dot_nt(halo[...], weight[...])
    pad[...] = jnp.zeros_like(pad)
    for b in range(batch):
        pad[LANES - 8 - 64 * b : LANES - 64 * b, :share] = before[8 * b : 8 * b + 8]
    out[:, :LANES] = jnp.transpose(pad[...])[:share].astype(BF16)
    out[:, LANES:] = own[...]


def value_kernel(
    b, length, step_bias, log_rate, hidden, halo, weight, taps, step_weight,
    scaled, opening, rows, decays, padded, step_pad,
):
    inner = weight.shape[1]
    heads = step_weight.shape[0]
    spread = head_lanes(inner)
    step_pad[...] = jnp.zeros_like(step_pad)
    step_pad[:heads, :] = step_weight[...]
    lane = lax.broadcasted_iota(jnp.int32, (1, LANES), 1)
    bias, rate = jnp.zeros((1, LANES), F32), jnp.full((1, LANES), -1e30, F32)
    for h in range(heads):
        bias = jnp.where(lane == h, step_bias[h], bias)
        rate = jnp.where(lane == h, log_rate[h], rate)
    rate = jnp.exp(rate)
    own = hidden[b * length : (b + 1) * length, :]
    before = dot(halo[...], weight[...]).astype(BF16).astype(F32)
    padded[0:8, :] = before[8 * b : 8 * b + 8]
    padded[8 : 8 + length, :] = dot(own, weight[...]).astype(BF16).astype(F32)
    step_pre = dot_nt(own, step_pad[...]) + bias
    steps = jnp.maximum(step_pre, 0.0) + jnp.log1p(jnp.exp(-jnp.abs(step_pre)))
    i = lax.broadcasted_iota(jnp.int32, (BLOCK, BLOCK), 0)
    j = lax.broadcasted_iota(jnp.int32, (BLOCK, BLOCK), 1)
    lower = (i >= j).astype(BF16)
    total = jnp.zeros((1, LANES), F32)
    halves, offsets = [], []
    for r in range(0, length, BLOCK):
        step = steps[r : r + BLOCK]
        high, middle, low = split_in_three(-step * rate)
        cumulative = dot(lower, high) + dot(lower, middle) + dot(lower, low)
        last = cumulative[BLOCK - 1 : BLOCK, :]
        centered = cumulative - 0.5 * last
        halves.append(0.5 * last)
        offsets.append(total + 0.5 * last)
        total = total + last
        value = sum(taps[t : t + 1, :] * padded[r + 5 + t : r + 5 + t + BLOCK, :] for t in range(CONV))
        ahead = over_channels(jnp.exp(-centered) * step, spread)
        scaled[r : r + BLOCK, :] = (silu(value) * ahead).astype(BF16)
        opening[r : r + BLOCK, :] = jnp.exp(centered)
    high, middle, low = split_in_three(total)
    decays[...] = jnp.concatenate([high, middle, low, jnp.zeros((5, LANES), BF16)], axis=0)
    rows[...] = jnp.exp(over_channels(jnp.concatenate(halves + offsets, axis=0), spread))


def gate_kernel(b, length, hidden, weight, opening, out):
    gate = dot(hidden[b * length : (b + 1) * length, :], weight[...]).astype(BF16).astype(F32)
    out[...] = (silu(gate) * over_channels(opening[...], head_lanes(weight.shape[1]))).astype(BF16)


def state_kernel(batch, length, steps, place, taps, *refs):
    shards, refs = refs[: len(steps)], refs[len(steps) :]
    scaled, refs = refs[:batch], refs[batch:]
    rows, refs = refs[:batch], refs[batch:]
    decays, (b_rows, c_rows, starts, sent, mixed, columns) = refs[:batch], refs[batch:]
    blocks = length // BLOCK
    inner = scaled[0].shape[1]
    share = shards[0].shape[0]
    rest = jnp.zeros((LANES - CONV, 2 * STATE), F32)
    columns[...] = jnp.transpose(jnp.concatenate([taps[...], rest], axis=0))
    for step, shard in zip(steps, shards):
        first = pl.multiple_of(lax.rem(place[0] + step, len(steps)) * share, share)
        tap = columns[pl.ds(first, share), :]
        halo = shard[:, :LANES].astype(F32)
        for b in range(batch):
            own = shard[:, LANES + b * length : LANES + (b + 1) * length].astype(F32)
            before = pltpu.roll(halo, 64 * b, 1) if b else halo
            padded = jnp.concatenate([before, own], axis=1)
            total = tap[:, CONV - 1 : CONV] * own
            for t in range(CONV - 1):
                total = total + tap[:, t : t + 1] * pltpu.roll(padded, CONV - 1 - t, 1)[:, LANES:]
            mixed[pl.ds(first, share), b * length : (b + 1) * length] = silu(total)
    for b in range(batch):
        own = slice(b * length, (b + 1) * length)
        b_t = mixed[:STATE, own].astype(BF16)
        b_rows[b] = b_t
        c_rows[own, :] = jnp.transpose(mixed[STATE:, own]).astype(BF16)
        state = jnp.zeros((STATE, inner), F32)
        for k in range(blocks):
            half = rows[b][k : k + 1, :]
            ready = half * state
            starts[b * blocks + k] = ready.astype(BF16)
            at = slice(k * BLOCK, (k + 1) * BLOCK)
            state = half * (ready + dot(b_t[:, at], scaled[b][at, :]))
        for g in range(STATE // 8):
            sent[b, g, :, :inner] = state[8 * g : 8 * g + 8].astype(BF16)
            sent[b, g, :, inner:] = decays[b][...]


def scan_kernel(got, out, table, logs):
    devices, _, width = got.shape
    inner = width - LANES
    for s in range(devices):
        parts = got[s, :, inner:].astype(F32)
        table[s : s + 1, :] = parts[0:1] + parts[1:2] + parts[2:3]
    logs[...] = jnp.exp(over_channels(table[...], head_lanes(inner)))
    state = jnp.zeros((8, inner), F32)
    for s in range(devices):
        out[s] = state.astype(BF16)
        state = logs[s : s + 1, :] * state + got[s, :, :inner].astype(F32)


def gated_kernel(batch, length, arrived, b_rows, c_rows, starts, *refs):
    scaled, refs = refs[:batch], refs[batch:]
    opened, refs = refs[:batch], refs[batch:]
    rows, (gated, squares) = refs[:batch], refs[batch:]
    blocks = length // BLOCK
    ones = jnp.ones((8, gated.shape[1]), BF16)
    i = lax.broadcasted_iota(jnp.int32, (BLOCK, BLOCK), 0)
    j = lax.broadcasted_iota(jnp.int32, (BLOCK, BLOCK), 1)
    for b in range(batch):
        for k in range(blocks):
            n = b * blocks + k
            at = slice(k * BLOCK, (k + 1) * BLOCK)
            c = c_rows[n * BLOCK : (n + 1) * BLOCK, :]
            scores = dot(c, b_rows[b, :, at])
            scores = jnp.where(i >= j, scores, 0.0).astype(BF16)
            y = dot(scores, scaled[b][at, :]) + dot(c, starts[n])
            y = y + rows[b][blocks + k : blocks + k + 1, :] * dot(c, arrived[b])
            g = y * opened[b][at, :].astype(F32)
            gated[n * BLOCK : (n + 1) * BLOCK, :] = g
            squares[:, n, :] = dot_nt(ones, (g * g).astype(BF16))


def scale_kernel(gated, squares, gain, out):
    total = squares[0]
    for d in range(1, squares.shape[0]):
        total = total + squares[d]
    scale = lax.rsqrt(total / DI + EPSILON)
    count = scale.shape[0]
    scale = jnp.concatenate([scale, jnp.zeros((LANES - count, LANES), F32)], axis=0)
    columns = jnp.transpose(scale)
    for n in range(count):
        at = slice(n * LANES, (n + 1) * LANES)
        out[at, :] = (gated[at, :] * columns[:, n : n + 1] * gain[...][None, :]).astype(BF16)


ANY = pl.BlockSpec(memory_space=pl.ANY)
WHOLE = pl.BlockSpec(memory_space=pltpu.VMEM)


def call(kernel, out, ins=None, scratch=(), mib=12, flops=0, outs=None, grid=()):
    shapes = [jax.ShapeDtypeStruct(s, d) for s, d in out]
    specs = {} if ins is None else {"in_specs": ins}
    if outs is not None:
        specs["out_specs"] = outs if len(outs) > 1 else outs[0]
    return pl.pallas_call(
        kernel,
        out_shape=shapes if len(shapes) > 1 else shapes[0],
        grid=grid,
        scratch_shapes=[s if not isinstance(s, tuple) else pltpu.VMEM(*s) for s in scratch],
        compiler_params=pltpu.CompilerParams(vmem_limit_bytes=mib << 20),
        cost_estimate=pl.CostEstimate(flops=flops, transcendentals=0, bytes_accessed=0)
        if flops
        else None,
        **specs,
    )


def on_device(
    hidden_in, gate_proj, value_proj, bc_proj, step_proj, value_conv, bc_conv, step_bias, log_rate,
    norm_gain,
):
    batch, length, width = hidden_in.shape
    tokens = batch * length
    inner = value_proj.shape[1]
    heads = step_proj.shape[1]
    share = bc_proj.shape[1]
    states = 2 * STATE
    blocks = tokens // BLOCK
    seq, tp = lax.axis_size("seq"), lax.axis_size("tp")
    hidden = hidden_in.reshape(tokens, width)
    weight = bc_proj.T
    step_weight = step_proj.T
    place = lax.axis_index("tp").reshape(1)
    smem = pl.BlockSpec(memory_space=pltpu.SMEM)
    tail = hidden_in[:, length - 8 :, :]
    halo = lax.ppermute(tail, "seq", [(i, i + 1) for i in range(seq - 1)]).reshape(8 * batch, width)
    own = call(
        functools.partial(bc_kernel, 256),
        [((share, tokens), BF16)],
        scratch=[((256, LANES), F32)],
        flops=2 * tokens * width * share,
    )(hidden, weight)
    shard = call(
        functools.partial(join_kernel, batch),
        [((share, tokens + LANES), BF16)],
        scratch=[((LANES, LANES), F32)],
    )(halo, weight, own)
    work = 2 * length * width * inner

    def value_of(b, hidden):
        return call(
            functools.partial(value_kernel, b, length),
            [
                ((length, inner), BF16),
                ((length, LANES), F32),
                ((2 * length // BLOCK, inner), F32),
                ((8, LANES), BF16),
            ],
            ins=[smem] * 2 + [WHOLE] * 5,
            outs=[WHOLE] * 4,
            scratch=[((length + 8, inner), F32), ((LANES, width), BF16)],
            flops=work,
        )(step_bias, log_rate, hidden, halo, value_proj, value_conv, step_weight)

    def gate_of(b, hidden, opening):
        return call(
            functools.partial(gate_kernel, b, length), [((length, inner), BF16)], flops=work
        )(hidden, gate_proj, opening)

    up = [(i, (i + 1) % tp) for i in range(tp)]
    down = [(i, (i - 1) % tp) for i in range(tp)]
    shards, places = [shard], [0]
    left = right = shard
    scaled, openings, rows, decays, opened = [], [], [], [], []
    for r in range(tp // 2):
        to_left = lax.ppermute(right, "tp", down) if 2 * r + 2 < tp else right
        to_right = lax.ppermute(left, "tp", up)
        if r < batch:
            one = value_of(r, hidden)
            for where, part in zip((scaled, openings, rows, decays), one):
                where.append(part)
            mark = one[3]
        elif r < 2 * batch:
            mark = gate_of(r - batch, hidden, openings[r - batch])
            opened.append(mark)
        left, right, hidden, mark = lax.optimization_barrier((to_right, to_left, hidden, mark))
        if r < batch:
            decays[-1] = mark
        else:
            opened[-1] = mark
        shards.append(left)
        places.append(tp - r - 1)
        if 2 * r + 2 < tp:
            shards.append(right)
            places.append(r + 1)
    b_rows, c_rows, starts, sent = call(
        functools.partial(state_kernel, batch, length, places),
        [
            ((batch, STATE, length), BF16),
            ((tokens, STATE), BF16),
            ((blocks, STATE, inner), BF16),
            ((batch, STATE // 8, 8, inner + LANES), BF16),
        ],
        ins=[smem] + [WHOLE] * (1 + tp + 3 * batch),
        outs=[WHOLE] * 4,
        scratch=[((states, tokens), F32), ((states, LANES), F32)],
    )(place, bc_conv, *shards, *scaled, *rows, *decays)
    got = lax.all_to_all(sent.reshape(seq, -1, inner + LANES), "seq", 0, 0, tiled=True)
    prefix = call(
        scan_kernel,
        [((seq, 8, inner), BF16)],
        scratch=[((seq, LANES), F32), ((seq, inner), F32)],
    )(got)
    arrived = lax.all_to_all(prefix, "seq", 0, 0, tiled=True).reshape(batch, STATE, inner)
    gated, squares = call(
        functools.partial(gated_kernel, batch, length),
        [((tokens, inner), F32), ((tp, blocks, LANES), F32)],
    )(arrived, b_rows, c_rows, starts, *scaled, *opened, *rows)
    whole = lax.all_to_all(squares, "tp", 0, 0, tiled=True)
    out = call(scale_kernel, [((tokens, inner), BF16)])(gated, whole, norm_gain)
    return out.reshape(batch, length, inner)


def solution(mesh):
    placed = (
        P(None, "seq", None),
        P(None, "tp"),
        P(None, "tp"),
        P(None, "tp"),
        P(None, "tp"),
        P(None, "tp"),
        P(),
        P("tp"),
        P("tp"),
        P("tp"),
    )
    return jax.shard_map(
        on_device, mesh=mesh, in_specs=placed, out_specs=P(None, "seq", "tp"), check_vma=False
    )
```

time: 99.1 us -> 90.3 us (0.911)
  blocking collectives: 19 us -> 42.1 us
  local copies, waits for them, and re-layouts: 22.4 us -> 6.3 us
  waiting for transfers between devices: 12 us -> 2.24 us
  starting transfers between devices: 19.9 us -> 15.7 us
  Pallas kernels: 24.7 us -> 23.4 us
    all_to_all x0 -> x2, blocking collectives: none -> 23.8 us  [the longest x1 13 us: on_device(): lax.all_to_all(prefix, 'seq', 0, 0, tiled=True).reshape(batch, STATE, inner)]
    unnamed x45 -> x22, local copies, waits for them, and re-layouts: 21.4 us -> 5.35 us
    all_to_all x3 -> x0, starting transfers between devices: 15.4 us -> none  [the longest x1 8.19 us: on_device(): lax.all_to_all(bc_part, 'tp', 0, 0, tiled=True)]
    ppermute x0 -> x7, starting transfers between devices: none -> 11.2 us  [the longest x3 11 us: on_device(): to_left = lax.ppermute(right, 'tp', down) if 2 * r + 2 < tp else right]
    all_to_all x3 -> x0, waiting for transfers between devices: 10.5 us -> none  [the longest x1 6.6 us: on_device(): whole = lax.all_to_all(squares, 'tp', 0, 0, tiled=True)]
    ppermute x0 -> x7, waiting for transfers between devices: none -> 2.24 us  [the longest x4 2.23 us: on_device(): to_right = lax.ppermute(left, 'tp', up)]
    pallas_call x7 -> x9, Pallas kernels: 22.8 us -> 21.1 us  [the longest x2 10.5 us: value_of(): call(functools.partial(value_kernel, b, length), [((length, inner), BF16)...]
    ppermute x1, waiting for transfers between devices: 1.46 us -> 0.01 us  [on_device(): lax.ppermute(tail, 'seq', [(i, i + 1) for i in range(seq - 1)])]
  transfers between devices with their start and end apart: 4 -> 8, of which waited for: 3 -> 2; matrix products, arithmetic and copies ran while one was open for 0% -> 0% of each run, Pallas kernels for 16% -> 19%
where the time goes in v3:
time: 90.3 us; the launch traced here: 89.9 us
  blocking collectives  42.1 us (47%)
  Pallas kernels  23.4 us (26%)
  starting transfers between devices  15.7 us (17%)
  local copies, waits for them, and re-layouts  6.3 us (7%)
  waiting for transfers between devices  2.24 us (2%)
    all_to_all x1, blocking collectives, on_device(): lax.all_to_all(sent.reshape(seq, -1, inner + LANES), 'seq', 0, 0, tiled=T...  18.3 us
    all_to_all x1, blocking collectives, on_device(): lax.all_to_all(prefix, 'seq', 0, 0, tiled=True).reshape(batch, STATE, inner)  13 us
    ppermute x3, starting transfers between devices, on_device(): to_left = lax.ppermute(right, 'tp', down) if 2 * r + 2 < tp else right  11 us
    all_to_all x1, blocking collectives, on_device(): whole = lax.all_to_all(squares, 'tp', 0, 0, tiled=True)  10.8 us
    pallas_call x2, Pallas kernels, value_of(): call(functools.partial(value_kernel, b, length), [((length, inner), BF16)...  10.5 us
    unnamed x22, local copies, waits for them, and re-layouts  5.35 us
    pallas_call x2, Pallas kernels, gate_of(): call(functools.partial(gate_kernel, b, length), [((length, inner), BF16)]...  4.95 us
    ppermute x1, starting transfers between devices, on_device(): lax.ppermute(tail, 'seq', [(i, i + 1) for i in range(seq - 1)])  4.49 us
  transfers between devices with their start and end apart: 8, of which 2 were waited for; matrix products, arithmetic and copies ran while one was open for 0% of the time, Pallas kernels for 19%

profile of v3, /device:TPU:1, one launch (start us, length us, event | category | flops | bytes accessed | tf_op | source)
XLA Modules:
  0.0 89.9 jit_solution(1928774114696002977)
XLA Ops:
  0.0 0.0 copy-start.10
  0.0 0.0 copy-start.9
  0.0 0.0 copy-start.6
  0.0 0.0 copy-start.5
  0.0 1.0 %slice.3 = bf16[2,8,2560]{2,1,0:T(8,128)(2,1)S(1)} slice(bf16[2,512,2560]{2,1,0:T(8,128)(2,1)} %param.10), slice={[0:2], [504:512], [0:2560]} | slice | bytes 163840 | tf_op jit(solution)/shard_map/slice | solution.py:253
  1.0 4.5 %collective-permute-start = (bf16[2,8,2560]{2,1,0:T(8,128)(2,1)S(1)}, bf16[2,8,2560]{2,1,0:T(8,128)(2,1)S(1)}, u32[]{:S(2)}, u32[]{:S(2)}) collective-permute-start(bf16[2,8,2560]{2,1,0:T(8,128)(2,1)S(1)} %slice.3), channel_id=1, source_target_pairs={{0,8},{8,16},{16,24},{24,32},{32,40},{40,48},{48,56},{56,64},{64,7... | collective-permute-start | bytes 245768 | tf_op jit(solution)/shard_map/ppermute | solution.py:254
  5.5 0.0 copy-start
  5.5 2.5 %copy-done = bf16[2,512,2560]{2,1,0:T(8,128)(2,1)S(1)} copy-done((bf16[2,512,2560]{2,1,0:T(8,128)(2,1)S(1)}, bf16[2,512,2560]{2,1,0:T(8,128)(2,1)}, u32[]{:S(2)}) %copy-start) | copy-done | bytes 5242904
  8.0 0.9 %copy-done.4 = bf16[2560,32]{0,1:T(8,128)(2,1)S(1)} copy-done((bf16[2560,32]{0,1:T(8,128)(2,1)S(1)}, bf16[2560,32]{0,1:T(8,128)(2,1)}, u32[]{:S(2)}) %copy-start.4) | copy-done | bytes 163864
  8.9 1.6 %shard_map.100.own = bf16[32,1024]{1,0:T(8,128)(2,1)S(1)} custom-call(bf16[1024,2560]{1,0:T(8,128)(2,1)S(1)} %bitcast.8, bf16[32,2560]{1,0:T(8,128)(2,1)S(1)} %bitcast.17), custom_call_target="tpu_custom_call" | custom-call | flops 167772160 | tf_op jit(solution)/shard_map/pallas_call | solution.py:255
  10.5 0.0 collective-permute-done
  10.5 0.2 shard_map.101.refs_0_
  10.7 5.6 %collective-permute-start.2 = (bf16[32,1152]{1,0:T(8,128)(2,1)S(1)}, bf16[32,1152]{1,0:T(8,128)(2,1)S(1)}, u32[]{:S(2)}, u32[]{:S(2)}) collective-permute-start(bf16[32,1152]{1,0:T(8,128)(2,1)S(1)} %shard_map.101.refs_0_), channel_id=1, source_target_pairs={{0,7},{1,0},{2,1},{3,2},{4,3},{5,4},{6,5},{7,6},{8,15},{9,8},{10,9... | collective-permute-start | bytes 221192 | tf_op jit(solution)/shard_map/ppermute | solution.py:294
  16.3 0.0 collective-permute-start.1
  16.3 0.0 copy-done.10
  16.3 0.0 copy-done.9
  16.3 0.0 copy-done.6
  16.4 0.0 copy-done.5
  16.4 0.0 copy-done.1
  16.4 0.0 copy-start.2
  16.4 1.9 %copy-done.2 = bf16[2560,640]{1,0:T(8,128)(2,1)S(1)} copy-done((bf16[2560,640]{1,0:T(8,128)(2,1)S(1)}, bf16[2560,640]{1,0:T(8,128)(2,1)}, u32[]{:S(2)}) %copy-start.2) | copy-done | bytes 3276824
  18.3 5.2 %shard_map.102 = (bf16[512,640]{1,0:T(8,128)(2,1)S(1)}, f32[512,128]{1,0:T(8,128)S(1)}, f32[8,640]{1,0:T(8,128)S(1)}, bf16[8,128]{1,0:T(8,128)(2,1)S(1)}) custom-call(f32[10]{0:T(128)S(1)} %copy-done.9, f32[10]{0:T(128)S(1)} %copy-done.10, bf16[1024,2560]{1,0:T(8,128)(2,1)S(1)} %bitcast.9, bf16[16,2560]{1,0:T(8,128)(2,1)S(1)} %bitcast.15, ...), custom_call_target="tpu_custom_call" | custom-call | flops 1677721600 | tf_op jit(solution)/shard_map/pallas_call | solution.py:269
  23.6 0.0 collective-permute-done.2.refs_2_
  23.6 0.0 collective-permute-done.1.refs_1_
  23.6 0.0 copy-start.3
  23.6 0.1 collective-permute-start.3
  23.7 2.7 %collective-permute-start.4 = (bf16[32,1152]{1,0:T(8,128)(2,1)S(1)}, bf16[32,1152]{1,0:T(8,128)(2,1)S(1)}, u32[]{:S(2)}, u32[]{:S(2)}) collective-permute-start(bf16[32,1152]{1,0:T(8,128)(2,1)S(1)} %collective-permute-done.2.refs_2_), channel_id=1, source_target_pairs={{0,7},{1,0},{2,1},{3,2},{4,3},{5,4},{6,5},{7,6},{8,15},{9,8},{10,9... | collective-permute-start | bytes 221192 | tf_op jit(solution)/shard_map/ppermute | solution.py:294
  26.4 5.2 %shard_map.103 = (bf16[512,640]{1,0:T(8,128)(2,1)S(1)}, f32[512,128]{1,0:T(8,128)S(1)}, f32[8,640]{1,0:T(8,128)S(1)}, bf16[8,128]{1,0:T(8,128)(2,1)S(1)}) custom-call(f32[10]{0:T(128)S(1)} %copy-done.9, f32[10]{0:T(128)S(1)} %copy-done.10, bf16[1024,2560]{1,0:T(8,128)(2,1)S(1)} %bitcast.10, bf16[16,2560]{1,0:T(8,128)(2,1)S(1)} %bitcast.16, ...), custom_call_target="tpu_custom_call" | custom-call | flops 1677721600 | tf_op jit(solution)/shard_map/pallas_call | solution.py:269
  31.7 0.0 collective-permute-done.3.refs_3_
  31.7 0.0 collective-permute-done.4.refs_4_
  31.7 0.1 collective-permute-start.5
  31.8 2.7 %collective-permute-start.6 = (bf16[32,1152]{1,0:T(8,128)(2,1)S(1)}, bf16[32,1152]{1,0:T(8,128)(2,1)S(1)}, u32[]{:S(2)}, u32[]{:S(2)}) collective-permute-start(bf16[32,1152]{1,0:T(8,128)(2,1)S(1)} %collective-permute-done.4.refs_4_), channel_id=1, source_target_pairs={{0,7},{1,0},{2,1},{3,2},{4,3},{5,4},{6,5},{7,6},{8,15},{9,8},{10,9... | collective-permute-start | bytes 221192 | tf_op jit(solution)/shard_map/ppermute | solution.py:294
  34.5 0.0 copy-done.3
  34.5 2.5 %shard_map.104.refs_2_ = bf16[512,640]{1,0:T(8,128)(2,1)S(1)} custom-call(bf16[1024,2560]{1,0:T(8,128)(2,1)S(1)} %bitcast.11, bf16[2560,640]{1,0:T(8,128)(2,1)S(1)} %copy-done.3, f32[512,128]{1,0:T(8,128)S(1)} %get-tuple-element.41.opening), custom_call_target="tpu_custom_call" | custom-call | flops 1677721600 | tf_op jit(solution)/shard_map/pallas_call | solution.py:284
  36.9 0.3 collective-permute-done.5.refs_5_
  37.2 0.0 collective-permute-done.6.refs_6_
  37.2 0.0 collective-permute-start.7
  37.3 2.5 %shard_map.105.refs_3_ = bf16[512,640]{1,0:T(8,128)(2,1)S(1)} custom-call(bf16[1024,2560]{1,0:T(8,128)(2,1)S(1)} %bitcast.12, bf16[2560,640]{1,0:T(8,128)(2,1)S(1)} %copy-done.3, f32[512,128]{1,0:T(8,128)S(1)} %get-tuple-element.45.opening), custom_call_target="tpu_custom_call" | custom-call | flops 1677721600 | tf_op jit(solution)/shard_map/pallas_call | solution.py:284
  39.7 1.9 %collective-permute-done.7.refs_7_ = bf16[32,1152]{1,0:T(8,128)(2,1)S(1)} collective-permute-done((bf16[32,1152]{1,0:T(8,128)(2,1)S(1)}, bf16[32,1152]{1,0:T(8,128)(2,1)S(1)}, u32[]{:S(2)}, u32[]{:S(2)}) %collective-permute-start.7) | collective-permute-done | bytes 73760 | tf_op jit(solution)/shard_map/ppermute | solution.py:295
  41.7 0.0 copy-done.7
  41.7 2.2 %shard_map.106 = (bf16[2,128,512]{2,1,0:T(8,128)(2,1)S(1)}, bf16[1024,128]{1,0:T(8,128)(2,1)S(1)}, bf16[8,128,640]{2,1,0:T(8,128)(2,1)S(1)}, bf16[2,16,8,768]{3,2,1,0:T(8,128)(2,1)S(1)}) custom-call(s32[1]{0:T(128)} %bitcast.place, f32[4,256]{1,0:T(4,128)S(1)} %copy-done.7, bf16[32,1152]{1,0:T(8,128)(2,1)S(1)} %shard_map.101.refs_0_, ...), custom_call_target="tpu_custom_call" | custom-call | tf_op jit(solution)/shard_map/pallas_call | solution.py:314
  43.8 18.3 %all_to_all.15.got = bf16[32,8,768]{2,1,0:T(8,128)(2,1)S(1)} all-to-all(bf16[32,8,768]{2,1,0:T(8,128)(2,1)S(1)} %bitcast.19), channel_id=1, replica_groups=mesh['seq'=32,'tp'=8] {'seq'}, dimensions={0} | all-to-all | bytes 786432 | tf_op jit(solution)/shard_map/all_to_all | solution.py:326
  62.2 0.3 shard_map.107
  62.4 13.0 %all_to_all.16 = bf16[32,8,640]{2,1,0:T(8,128)(2,1)S(1)} all-to-all(bf16[32,8,640]{2,1,0:T(8,128)(2,1)S(1)} %shard_map.107), channel_id=1, replica_groups=mesh['seq'=32,'tp'=8] {'seq'}, dimensions={0} | all-to-all | bytes 655360 | tf_op jit(solution)/shard_map/all_to_all | solution.py:332
  75.5 2.3 %shard_map.108 = (f32[1024,640]{1,0:T(8,128)S(1)}, f32[8,8,128]{2,1,0:T(8,128)S(1)}) custom-call(bf16[2,128,640]{2,1,0:T(8,128)(2,1)S(1)} %bitcast.13, bf16[2,128,512]{2,1,0:T(8,128)(2,1)S(1)} %get-tuple-element.54.b_rows, bf16[1024,128]{1,0:T(8,128)(2,1)S(1)} %get-tuple-element.55.c_rows, bf16[8,128,640]{2,1,0:T(8,128)(2,1)S(1)} %get-tuple-element.56.starts, ...), custom_call_target="tpu_custom_call" | custom-call | tf_op jit(solution)/shard_map/pallas_call | solution.py:333
  77.7 10.8 %all_to_all.17.squares = f32[8,8,128]{2,1,0:T(8,128)S(1)} all-to-all(f32[8,8,128]{2,1,0:T(8,128)S(1)} %get-tuple-element.60), channel_id=1, replica_groups=mesh['seq'=32,'tp'=8] {'tp'}, dimensions={0} | all-to-all | bytes 65536 | tf_op jit(solution)/shard_map/all_to_all | solution.py:337
  88.5 0.0 copy-done.8
  88.5 1.4 %shard_map.109 = bf16[1024,640]{1,0:T(8,128)(2,1)} custom-call(f32[1024,640]{1,0:T(8,128)S(1)} %get-tuple-element.59.gated, f32[8,8,128]{2,1,0:T(8,128)S(1)} %all_to_all.17.squares, f32[640]{0:T(1024)S(1)} %copy-done.8), custom_call_target="tpu_custom_call" | custom-call | tf_op jit(solution)/shard_map/pallas_call | solution.py:338
  (4 shorter events, 0.0 us)
Async XLA Ops:
  0.0 16.3 %copy-start.10 = (f32[10]{0:T(128)S(1)}, f32[10]{0:T(128)}, u32[]{:S(2)}) copy-start(f32[10]{0:T(128)} %log_rate.3) | copy-start | bytes 124
  0.0 16.3 %copy-start.9 = (f32[10]{0:T(128)S(1)}, f32[10]{0:T(128)}, u32[]{:S(2)}) copy-start(f32[10]{0:T(128)} %step_bias.3) | copy-start | bytes 124
  0.0 16.3 %copy-start.6 = (f32[4,640]{1,0:T(4,128)S(1)}, f32[4,640]{1,0:T(4,128)}, u32[]{:S(2)}) copy-start(f32[4,640]{1,0:T(4,128)} %taps.4) | copy-start | bytes 30724
  0.0 16.3 %copy-start.5 = (bf16[2560,10]{0,1:T(8,128)(2,1)S(1)}, bf16[2560,10]{0,1:T(8,128)(2,1)}, u32[]{:S(2)}) copy-start(bf16[2560,10]{0,1:T(8,128)(2,1)} %param.14) | copy-start | bytes 153604
  1.0 9.5 %collective-permute-start = (bf16[2,8,2560]{2,1,0:T(8,128)(2,1)S(1)}, bf16[2,8,2560]{2,1,0:T(8,128)(2,1)S(1)}, u32[]{:S(2)}, u32[]{:S(2)}) collective-permute-start(bf16[2,8,2560]{2,1,0:T(8,128)(2,1)S(1)} %slice.3), channel_id=1, source_target_pairs={{0,8},{8,16},{16,24},{24,32},{32,40},{40,48},{48,56},{56,64},{64,7... | collective-permute-start | bytes 245768 | tf_op jit(solution)/shard_map/ppermute | solution.py:254
  5.5 2.5 %copy-start = (bf16[2,512,2560]{2,1,0:T(8,128)(2,1)S(1)}, bf16[2,512,2560]{2,1,0:T(8,128)(2,1)}, u32[]{:S(2)}) copy-start(bf16[2,512,2560]{2,1,0:T(8,128)(2,1)} %param.10) | copy-start | bytes 15728644
  8.0 0.9 %copy-start.4 = (bf16[2560,32]{0,1:T(8,128)(2,1)S(1)}, bf16[2560,32]{0,1:T(8,128)(2,1)}, u32[]{:S(2)}) copy-start(bf16[2560,32]{0,1:T(8,128)(2,1)} %param.13) | copy-start | bytes 491524
  8.9 7.5 %copy-start.1 = (bf16[2,512,2560]{2,1,0:T(8,128)(2,1)S(1)}, bf16[2,512,2560]{2,1,0:T(8,128)(2,1)}, u32[]{:S(2)}) copy-start(bf16[2,512,2560]{2,1,0:T(8,128)(2,1)} %param.10) | copy-start | bytes 15728644
  10.7 12.9 %collective-permute-start.2 = (bf16[32,1152]{1,0:T(8,128)(2,1)S(1)}, bf16[32,1152]{1,0:T(8,128)(2,1)S(1)}, u32[]{:S(2)}, u32[]{:S(2)}) collective-permute-start(bf16[32,1152]{1,0:T(8,128)(2,1)S(1)} %shard_map.101.refs_0_), channel_id=1, source_target_pairs={{0,7},{1,0},{2,1},{3,2},{4,3},{5,4},{6,5},{7,6},{8,15},{9,8},{10,9... | collective-permute-start | bytes 221192 | tf_op jit(solution)/shard_map/ppermute | solution.py:294
  16.3 7.2 %collective-permute-start.1 = (bf16[32,1152]{1,0:T(8,128)(2,1)S(1)}, bf16[32,1152]{1,0:T(8,128)(2,1)S(1)}, u32[]{:S(2)}, u32[]{:S(2)}) collective-permute-start(bf16[32,1152]{1,0:T(8,128)(2,1)S(1)} %shard_map.101.refs_0_), channel_id=1, source_target_pairs={{0,1},{1,2},{2,3},{3,4},{4,5},{5,6},{6,7},{7,0},{8,9},{9,10},{10,1... | collective-permute-start | bytes 221192 | tf_op jit(solution)/shard_map/ppermute | solution.py:295
  16.4 1.9 %copy-start.2 = (bf16[2560,640]{1,0:T(8,128)(2,1)S(1)}, bf16[2560,640]{1,0:T(8,128)(2,1)}, u32[]{:S(2)}) copy-start(bf16[2560,640]{1,0:T(8,128)(2,1)} %weight.5) | copy-start | bytes 9830404
  23.6 10.9 %copy-start.3 = (bf16[2560,640]{1,0:T(8,128)(2,1)S(1)}, bf16[2560,640]{1,0:T(8,128)(2,1)}, u32[]{:S(2)}) copy-start(bf16[2560,640]{1,0:T(8,128)(2,1)} %weight.7) | copy-start | bytes 9830404
  23.6 8.1 %collective-permute-start.3 = (bf16[32,1152]{1,0:T(8,128)(2,1)S(1)}, bf16[32,1152]{1,0:T(8,128)(2,1)S(1)}, u32[]{:S(2)}, u32[]{:S(2)}) collective-permute-start(bf16[32,1152]{1,0:T(8,128)(2,1)S(1)} %collective-permute-done.1.refs_1_), channel_id=1, source_target_pairs={{0,1},{1,2},{2,3},{3,4},{4,5},{5,6},{6,7},{7,0},{8,9},{9,10},{10,1... | collective-permute-start | bytes 221192 | tf_op jit(solution)/shard_map/ppermute | solution.py:295
  23.7 8.0 %collective-permute-start.4 = (bf16[32,1152]{1,0:T(8,128)(2,1)S(1)}, bf16[32,1152]{1,0:T(8,128)(2,1)S(1)}, u32[]{:S(2)}, u32[]{:S(2)}) collective-permute-start(bf16[32,1152]{1,0:T(8,128)(2,1)S(1)} %collective-permute-done.2.refs_2_), channel_id=1, source_target_pairs={{0,7},{1,0},{2,1},{3,2},{4,3},{5,4},{6,5},{7,6},{8,15},{9,8},{10,9... | collective-permute-start | bytes 221192 | tf_op jit(solution)/shard_map/ppermute | solution.py:294
  31.7 5.5 %collective-permute-start.5 = (bf16[32,1152]{1,0:T(8,128)(2,1)S(1)}, bf16[32,1152]{1,0:T(8,128)(2,1)S(1)}, u32[]{:S(2)}, u32[]{:S(2)}) collective-permute-start(bf16[32,1152]{1,0:T(8,128)(2,1)S(1)} %collective-permute-done.3.refs_3_), channel_id=1, source_target_pairs={{0,1},{1,2},{2,3},{3,4},{4,5},{5,6},{6,7},{7,0},{8,9},{9,10},{10,1... | collective-permute-start | bytes 221192 | tf_op jit(solution)/shard_map/ppermute | solution.py:295
  31.8 5.5 %collective-permute-start.6 = (bf16[32,1152]{1,0:T(8,128)(2,1)S(1)}, bf16[32,1152]{1,0:T(8,128)(2,1)S(1)}, u32[]{:S(2)}, u32[]{:S(2)}) collective-permute-start(bf16[32,1152]{1,0:T(8,128)(2,1)S(1)} %collective-permute-done.4.refs_4_), channel_id=1, source_target_pairs={{0,7},{1,0},{2,1},{3,2},{4,3},{5,4},{6,5},{7,6},{8,15},{9,8},{10,9... | collective-permute-start | bytes 221192 | tf_op jit(solution)/shard_map/ppermute | solution.py:294
  37.2 4.4 %collective-permute-start.7 = (bf16[32,1152]{1,0:T(8,128)(2,1)S(1)}, bf16[32,1152]{1,0:T(8,128)(2,1)S(1)}, u32[]{:S(2)}, u32[]{:S(2)}) collective-permute-start(bf16[32,1152]{1,0:T(8,128)(2,1)S(1)} %collective-permute-done.5.refs_5_), channel_id=1, source_target_pairs={{0,1},{1,2},{2,3},{3,4},{4,5},{5,6},{6,7},{7,0},{8,9},{9,10},{10,1... | collective-permute-start | bytes 221192 | tf_op jit(solution)/shard_map/ppermute | solution.py:295
  37.2 4.4 %copy-start.7 = (f32[4,256]{1,0:T(4,128)S(1)}, f32[4,256]{1,0:T(4,128)}, u32[]{:S(2)}) copy-start(f32[4,256]{1,0:T(4,128)} %taps.5) | copy-start | bytes 12292
  62.2 26.3 %copy-start.8 = (f32[640]{0:T(1024)S(1)}, f32[640]{0:T(1024)}, u32[]{:S(2)}) copy-start(f32[640]{0:T(1024)} %gain.1) | copy-start | bytes 7684

commit v4 on v3

--- a/solution.py
+++ b/solution.py
@@ -96,24 +96,30 @@
     padded[8 : 8 + length, :] = dot(own, weight[...]).astype(BF16).astype(F32)
     step_pre = dot_nt(own, step_pad[...]) + bias
     steps = jnp.maximum(step_pre, 0.0) + jnp.log1p(jnp.exp(-jnp.abs(step_pre)))
-    i = lax.broadcasted_iota(jnp.int32, (BLOCK, BLOCK), 0)
-    j = lax.broadcasted_iota(jnp.int32, (BLOCK, BLOCK), 1)
+    width = 3 * BLOCK
+    i = lax.broadcasted_iota(jnp.int32, (BLOCK, width), 0)
+    j = lax.rem(lax.broadcasted_iota(jnp.int32, (BLOCK, width), 1), BLOCK)
     lower = (i >= j).astype(BF16)
+    blocks = range(0, length, BLOCK)
+    parts = split_in_three(-steps * rate)
+    side = [jnp.concatenate([part[r : r + BLOCK] for r in blocks], axis=1) for part in parts]
+    cumulative = dot(lower, jnp.concatenate(side, axis=0))
+    half = 0.5 * cumulative[BLOCK - 1 : BLOCK, :]
+    centered = cumulative - half
+    ahead = jnp.exp(-centered)
+    behind = jnp.exp(centered)
+    ahead = jnp.concatenate([ahead[:, k * LANES : (k + 1) * LANES] for k in range(len(blocks))], axis=0)
+    ahead = over_channels(ahead * steps, spread)
     total = jnp.zeros((1, LANES), F32)
     halves, offsets = [], []
-    for r in range(0, length, BLOCK):
-        step = steps[r : r + BLOCK]
-        high, middle, low = split_in_three(-step * rate)
-        cumulative = dot(lower, high) + dot(lower, middle) + dot(lower, low)
-        last = cumulative[BLOCK - 1 : BLOCK, :]
-        centered = cumulative - 0.5 * last
-        halves.append(0.5 * last)
-        offsets.append(total + 0.5 * last)
-        total = total + last
+    for k, r in enumerate(blocks):
+        lanes = slice(k * LANES, (k + 1) * LANES)
+        halves.append(half[:, lanes])
+        offsets.append(total + half[:, lanes])
+        total = total + 2.0 * half[:, lanes]
         value = sum(taps[t : t + 1, :] * padded[r + 5 + t : r + 5 + t + BLOCK, :] for t in range(CONV))
-        ahead = over_channels(jnp.exp(-centered) * step, spread)
-        scaled[r : r + BLOCK, :] = (silu(value) * ahead).astype(BF16)
-        opening[r : r + BLOCK, :] = jnp.exp(centered)
+        scaled[r : r + BLOCK, :] = (silu(value) * ahead[r : r + BLOCK]).astype(BF16)
+        opening[r : r + BLOCK, :] = behind[:, lanes]
     high, middle, low = split_in_three(total)
     decays[...] = jnp.concatenate([high, middle, low, jnp.zeros((5, LANES), BF16)], axis=0)
     rows[...] = jnp.exp(over_channels(jnp.concatenate(halves + offsets, axis=0), spread))
@@ -256,12 +262,13 @@
         functools.partial(bc_kernel, 256),
         [((share, tokens), BF16)],
         scratch=[((256, LANES), F32)],
-        flops=2 * tokens * width * share,
+        flops=6 * tokens * width * share,
     )(hidden, weight)
     shard = call(
         functools.partial(join_kernel, batch),
         [((share, tokens + LANES), BF16)],
         scratch=[((LANES, LANES), F32)],
+        flops=30 * tokens * width * share,
     )(halo, weight, own)
     work = 2 * length * width * inner
 

time: 90.3 us -> 88.2 us (0.977)
  local copies, waits for them, and re-layouts: 6.3 us -> 4.35 us
    unnamed x22 -> x24, local copies, waits for them, and re-layouts: 5.35 us -> 3.46 us
    all_to_all x1, blocking collectives: 18.3 us -> 19.5 us  [on_device(): lax.all_to_all(sent.reshape(seq, -1, inner + LANES), 'seq', 0, 0, tiled=T...]
  transfers between devices with their start and end apart: 8 -> 8, of which waited for: 2 -> 1; matrix products, arithmetic and copies ran while one was open for 0% -> 0% of each run, Pallas kernels for 19% -> 19%
where the time goes in v4:
time: 88.2 us; the launch traced here: 87.9 us
  blocking collectives  42.6 us (48%)
  Pallas kernels  22.9 us (26%)
  starting transfers between devices  15.8 us (18%)
  local copies, waits for them, and re-layouts  4.35 us (5%)
  waiting for transfers between devices  1.97 us (2%)
    all_to_all x1, blocking collectives, on_device(): lax.all_to_all(sent.reshape(seq, -1, inner + LANES), 'seq', 0, 0, tiled=T...  19.5 us
    all_to_all x1, blocking collectives, on_device(): lax.all_to_all(prefix, 'seq', 0, 0, tiled=True).reshape(batch, STATE, inner)  13 us
    ppermute x3, starting transfers between devices, on_device(): to_left = lax.ppermute(right, 'tp', down) if 2 * r + 2 < tp else right  11 us
    all_to_all x1, blocking collectives, on_device(): whole = lax.all_to_all(squares, 'tp', 0, 0, tiled=True)  10.1 us
    pallas_call x2, Pallas kernels, value_of(): call(functools.partial(value_kernel, b, length), [((length, inner), BF16)...  10.1 us
    pallas_call x2, Pallas kernels, gate_of(): call(functools.partial(gate_kernel, b, length), [((length, inner), BF16)]...  4.86 us
    ppermute x1, starting transfers between devices, on_device(): lax.ppermute(tail, 'seq', [(i, i + 1) for i in range(seq - 1)])  4.49 us
    unnamed x24, local copies, waits for them, and re-layouts  3.46 us
  transfers between devices with their start and end apart: 8, of which 1 were waited for; matrix products, arithmetic and copies ran while one was open for 0% of the time, Pallas kernels for 19%

profile of v4, /device:TPU:1, one launch (start us, length us, event | category | flops | bytes accessed | tf_op | source)
XLA Modules:
  0.0 87.9 jit_solution(2607510488450997752)
XLA Ops:
  0.0 0.9 %slice.3 = bf16[2,8,2560]{2,1,0:T(8,128)(2,1)S(1)} slice(bf16[2,512,2560]{2,1,0:T(8,128)(2,1)} %param.10), slice={[0:2], [504:512], [0:2560]} | slice | bytes 163840 | tf_op jit(solution)/shard_map/slice | solution.py:259
  0.9 4.5 %collective-permute-start = (bf16[2,8,2560]{2,1,0:T(8,128)(2,1)S(1)}, bf16[2,8,2560]{2,1,0:T(8,128)(2,1)S(1)}, u32[]{:S(2)}, u32[]{:S(2)}) collective-permute-start(bf16[2,8,2560]{2,1,0:T(8,128)(2,1)S(1)} %slice.3), channel_id=1, source_target_pairs={{0,8},{8,16},{16,24},{24,32},{32,40},{40,48},{48,56},{56,64},{64,7... | collective-permute-start | bytes 245768 | tf_op jit(solution)/shard_map/ppermute | solution.py:260
  5.4 0.0 copy-start
  5.4 2.5 %copy-done = bf16[2,512,2560]{2,1,0:T(8,128)(2,1)S(1)} copy-done((bf16[2,512,2560]{2,1,0:T(8,128)(2,1)S(1)}, bf16[2,512,2560]{2,1,0:T(8,128)(2,1)}, u32[]{:S(2)}) %copy-start) | copy-done | bytes 5242904
  7.9 0.9 %copy-done.4 = bf16[2560,32]{0,1:T(8,128)(2,1)S(1)} copy-done((bf16[2560,32]{0,1:T(8,128)(2,1)S(1)}, bf16[2560,32]{0,1:T(8,128)(2,1)}, u32[]{:S(2)}) %copy-start.4) | copy-done | bytes 163864
  8.8 1.6 %shard_map.100.own = bf16[32,1024]{1,0:T(8,128)(2,1)S(1)} custom-call(bf16[1024,2560]{1,0:T(8,128)(2,1)S(1)} %bitcast.8, bf16[32,2560]{1,0:T(8,128)(2,1)S(1)} %bitcast.22), custom_call_target="tpu_custom_call" | custom-call | flops 503316480 | tf_op jit(solution)/shard_map/pallas_call | solution.py:261
  10.4 0.0 collective-permute-done
  10.4 0.0 slice-start.1
  10.4 0.0 copy-start.1
  10.4 0.0 copy-start.3
  10.5 0.0 copy-start.5
  10.5 0.0 copy-start.8
  10.5 0.0 copy-start.9
  10.5 0.2 shard_map.101.refs_0_
  10.7 5.6 %collective-permute-start.2 = (bf16[32,1152]{1,0:T(8,128)(2,1)S(1)}, bf16[32,1152]{1,0:T(8,128)(2,1)S(1)}, u32[]{:S(2)}, u32[]{:S(2)}) collective-permute-start(bf16[32,1152]{1,0:T(8,128)(2,1)S(1)} %shard_map.101.refs_0_), channel_id=1, source_target_pairs={{0,7},{1,0},{2,1},{3,2},{4,3},{5,4},{6,5},{7,6},{8,15},{9,8},{10,9... | collective-permute-start | bytes 221192 | tf_op jit(solution)/shard_map/ppermute | solution.py:301
  16.3 0.0 collective-permute-start.1
  16.3 0.0 slice-done
  16.3 0.0 slice-done.1
  16.3 0.0 copy-done.1
  16.3 0.0 copy-done.3
  16.4 0.0 copy-done.5
  16.4 0.0 copy-done.8
  16.4 5.0 %shard_map.102 = (bf16[512,640]{1,0:T(8,128)(2,1)S(1)}, f32[512,128]{1,0:T(8,128)S(1)}, f32[8,640]{1,0:T(8,128)S(1)}, bf16[8,128]{1,0:T(8,128)(2,1)S(1)}) custom-call(f32[10]{0:T(128)S(1)} %copy-done.8, f32[10]{0:T(128)S(1)} %copy-done.9, bf16[1024,2560]{1,0:T(8,128)(2,1)S(1)} %bitcast.11, bf16[16,2560]{1,0:T(8,128)(2,1)S(1)} %bitcast.20, ...), custom_call_target="tpu_custom_call" | custom-call | flops 1677721600 | tf_op jit(solution)/shard_map/pallas_call | solution.py:276
  21.4 0.0 collective-permute-done.2.refs_2_
  21.5 0.0 collective-permute-done.1.refs_1_
  21.5 0.0 copy-start.2
  21.5 0.1 collective-permute-start.3
  21.6 2.7 %collective-permute-start.4 = (bf16[32,1152]{1,0:T(8,128)(2,1)S(1)}, bf16[32,1152]{1,0:T(8,128)(2,1)S(1)}, u32[]{:S(2)}, u32[]{:S(2)}) collective-permute-start(bf16[32,1152]{1,0:T(8,128)(2,1)S(1)} %collective-permute-done.2.refs_2_), channel_id=1, source_target_pairs={{0,7},{1,0},{2,1},{3,2},{4,3},{5,4},{6,5},{7,6},{8,15},{9,8},{10,9... | collective-permute-start | bytes 221192 | tf_op jit(solution)/shard_map/ppermute | solution.py:301
  24.3 5.0 %shard_map.103 = (bf16[512,640]{1,0:T(8,128)(2,1)S(1)}, f32[512,128]{1,0:T(8,128)S(1)}, f32[8,640]{1,0:T(8,128)S(1)}, bf16[8,128]{1,0:T(8,128)(2,1)S(1)}) custom-call(f32[10]{0:T(128)S(1)} %copy-done.8, f32[10]{0:T(128)S(1)} %copy-done.9, bf16[1024,2560]{1,0:T(8,128)(2,1)S(1)} %bitcast.12, bf16[16,2560]{1,0:T(8,128)(2,1)S(1)} %bitcast.21, ...), custom_call_target="tpu_custom_call" | custom-call | flops 1677721600 | tf_op jit(solution)/shard_map/pallas_call | solution.py:276
  29.4 0.0 collective-permute-done.3.refs_3_
  29.4 0.0 collective-permute-done.4.refs_4_
  29.4 0.1 collective-permute-start.5
  29.5 2.7 %collective-permute-start.6 = (bf16[32,1152]{1,0:T(8,128)(2,1)S(1)}, bf16[32,1152]{1,0:T(8,128)(2,1)S(1)}, u32[]{:S(2)}, u32[]{:S(2)}) collective-permute-start(bf16[32,1152]{1,0:T(8,128)(2,1)S(1)} %collective-permute-done.4.refs_4_), channel_id=1, source_target_pairs={{0,7},{1,0},{2,1},{3,2},{4,3},{5,4},{6,5},{7,6},{8,15},{9,8},{10,9... | collective-permute-start | bytes 221192 | tf_op jit(solution)/shard_map/ppermute | solution.py:301
  32.1 2.4 %shard_map.104.refs_2_ = bf16[512,640]{1,0:T(8,128)(2,1)S(1)} custom-call(bf16[1024,2560]{1,0:T(8,128)(2,1)S(1)} %bitcast.13, bf16[2560,640]{1,0:T(8,128)(2,1)S(1)} %copy-done.2, f32[512,128]{1,0:T(8,128)S(1)} %get-tuple-element.41.opening), custom_call_target="tpu_custom_call" | custom-call | flops 1677721600 | tf_op jit(solution)/shard_map/pallas_call | solution.py:291
  34.6 0.0 collective-permute-done.5.refs_5_
  34.6 0.0 collective-permute-done.6.refs_6_
  34.6 0.1 collective-permute-start.7
  34.7 0.0 copy-start.6
  34.7 2.4 %shard_map.105.refs_3_ = bf16[512,640]{1,0:T(8,128)(2,1)S(1)} custom-call(bf16[1024,2560]{1,0:T(8,128)(2,1)S(1)} %bitcast.14, bf16[2560,640]{1,0:T(8,128)(2,1)S(1)} %copy-done.2, f32[512,128]{1,0:T(8,128)S(1)} %get-tuple-element.45.opening), custom_call_target="tpu_custom_call" | custom-call | flops 1677721600 | tf_op jit(solution)/shard_map/pallas_call | solution.py:291
  37.1 2.0 %collective-permute-done.7.refs_7_ = bf16[32,1152]{1,0:T(8,128)(2,1)S(1)} collective-permute-done((bf16[32,1152]{1,0:T(8,128)(2,1)S(1)}, bf16[32,1152]{1,0:T(8,128)(2,1)S(1)}, u32[]{:S(2)}, u32[]{:S(2)}) %collective-permute-start.7) | collective-permute-done | bytes 73760 | tf_op jit(solution)/shard_map/ppermute | solution.py:302
  39.1 2.2 %shard_map.106 = (bf16[2,128,512]{2,1,0:T(8,128)(2,1)S(1)}, bf16[1024,128]{1,0:T(8,128)(2,1)S(1)}, bf16[8,128,640]{2,1,0:T(8,128)(2,1)S(1)}, bf16[2,16,8,768]{3,2,1,0:T(8,128)(2,1)S(1)}) custom-call(s32[1]{0:T(128)} %bitcast.place, f32[4,256]{1,0:T(4,128)S(1)} %copy-done.6, bf16[32,1152]{1,0:T(8,128)(2,1)S(1)} %shard_map.101.refs_0_, ...), custom_call_target="tpu_custom_call" | custom-call | tf_op jit(solution)/shard_map/pallas_call | solution.py:321
  41.3 19.5 %all_to_all.15.got = bf16[32,8,768]{2,1,0:T(8,128)(2,1)S(1)} all-to-all(bf16[32,8,768]{2,1,0:T(8,128)(2,1)S(1)} %bitcast.16), channel_id=1, replica_groups=mesh['seq'=32,'tp'=8] {'seq'}, dimensions={0} | all-to-all | bytes 786432 | tf_op jit(solution)/shard_map/all_to_all | solution.py:333
  60.8 0.3 shard_map.107
  61.0 13.0 %all_to_all.16 = bf16[32,8,640]{2,1,0:T(8,128)(2,1)S(1)} all-to-all(bf16[32,8,640]{2,1,0:T(8,128)(2,1)S(1)} %shard_map.107), channel_id=1, replica_groups=mesh['seq'=32,'tp'=8] {'seq'}, dimensions={0} | all-to-all | bytes 655360 | tf_op jit(solution)/shard_map/all_to_all | solution.py:339
  74.1 2.3 %shard_map.108 = (f32[1024,640]{1,0:T(8,128)S(1)}, f32[8,8,128]{2,1,0:T(8,128)S(1)}) custom-call(bf16[2,128,640]{2,1,0:T(8,128)(2,1)S(1)} %bitcast.15, bf16[2,128,512]{2,1,0:T(8,128)(2,1)S(1)} %get-tuple-element.54.b_rows, bf16[1024,128]{1,0:T(8,128)(2,1)S(1)} %get-tuple-element.55.c_rows, bf16[8,128,640]{2,1,0:T(8,128)(2,1)S(1)} %get-tuple-element.56.starts, ...), custom_call_target="tpu_custom_call" | custom-call | tf_op jit(solution)/shard_map/pallas_call | solution.py:340
  76.3 10.1 %all_to_all.17.squares = f32[8,8,128]{2,1,0:T(8,128)S(1)} all-to-all(f32[8,8,128]{2,1,0:T(8,128)S(1)} %get-tuple-element.60), channel_id=1, replica_groups=mesh['seq'=32,'tp'=8] {'tp'}, dimensions={0} | all-to-all | bytes 65536 | tf_op jit(solution)/shard_map/all_to_all | solution.py:344
  86.5 0.0 copy-done.7
  86.5 1.4 %shard_map.109 = bf16[1024,640]{1,0:T(8,128)(2,1)} custom-call(f32[1024,640]{1,0:T(8,128)S(1)} %get-tuple-element.59.gated, f32[8,8,128]{2,1,0:T(8,128)S(1)} %all_to_all.17.squares, f32[640]{0:T(1024)S(1)} %copy-done.7), custom_call_target="tpu_custom_call" | custom-call | tf_op jit(solution)/shard_map/pallas_call | solution.py:345
  (7 shorter events, 0.0 us)
Async XLA Ops:
  0.9 9.5 %collective-permute-start = (bf16[2,8,2560]{2,1,0:T(8,128)(2,1)S(1)}, bf16[2,8,2560]{2,1,0:T(8,128)(2,1)S(1)}, u32[]{:S(2)}, u32[]{:S(2)}) collective-permute-start(bf16[2,8,2560]{2,1,0:T(8,128)(2,1)S(1)} %slice.3), channel_id=1, source_target_pairs={{0,8},{8,16},{16,24},{24,32},{32,40},{40,48},{48,56},{56,64},{64,7... | collective-permute-start | bytes 245768 | tf_op jit(solution)/shard_map/ppermute | solution.py:260
  5.4 2.5 %copy-start = (bf16[2,512,2560]{2,1,0:T(8,128)(2,1)S(1)}, bf16[2,512,2560]{2,1,0:T(8,128)(2,1)}, u32[]{:S(2)}) copy-start(bf16[2,512,2560]{2,1,0:T(8,128)(2,1)} %param.10) | copy-start | bytes 15728644
  7.9 0.9 %copy-start.4 = (bf16[2560,32]{0,1:T(8,128)(2,1)S(1)}, bf16[2560,32]{0,1:T(8,128)(2,1)}, u32[]{:S(2)}) copy-start(bf16[2560,32]{0,1:T(8,128)(2,1)} %param.13) | copy-start | bytes 491524
  8.8 7.5 %slice-start = ((s8[5242880]{0:T(1024)(128)(4,1)}), s8[4194304]{0:T(1024)(128)(4,1)S(1)}, s32[]{:S(2)}) async-start(s8[5242880]{0:T(1024)(128)(4,1)} %bitcast.9), calls=%async_computation.3 | async-start | bytes 8388608
  10.4 5.9 %slice-start.1 = ((s8[5242880]{0:T(1024)(128)(4,1)}), s8[1048576]{0:T(1024)(128)(4,1)S(1)}, s32[]{:S(2)}) async-start(s8[5242880]{0:T(1024)(128)(4,1)} %bitcast.9), calls=%async_computation.4 | async-start | bytes 2097152
  10.4 5.9 %copy-start.1 = (bf16[2560,640]{1,0:T(8,128)(2,1)S(1)}, bf16[2560,640]{1,0:T(8,128)(2,1)}, u32[]{:S(2)}) copy-start(bf16[2560,640]{1,0:T(8,128)(2,1)} %weight.5) | copy-start | bytes 9830404
  10.4 5.9 %copy-start.3 = (bf16[2560,10]{0,1:T(8,128)(2,1)S(1)}, bf16[2560,10]{0,1:T(8,128)(2,1)}, u32[]{:S(2)}) copy-start(bf16[2560,10]{0,1:T(8,128)(2,1)} %param.14) | copy-start | bytes 153604
  10.5 5.9 %copy-start.5 = (f32[4,640]{1,0:T(4,128)S(1)}, f32[4,640]{1,0:T(4,128)}, u32[]{:S(2)}) copy-start(f32[4,640]{1,0:T(4,128)} %taps.4) | copy-start | bytes 30724
  10.5 5.9 %copy-start.8 = (f32[10]{0:T(128)S(1)}, f32[10]{0:T(128)}, u32[]{:S(2)}) copy-start(f32[10]{0:T(128)} %step_bias.3) | copy-start | bytes 124
  10.5 5.9 %copy-start.9 = (f32[10]{0:T(128)S(1)}, f32[10]{0:T(128)}, u32[]{:S(2)}) copy-start(f32[10]{0:T(128)} %log_rate.3) | copy-start | bytes 124
  10.7 10.8 %collective-permute-start.2 = (bf16[32,1152]{1,0:T(8,128)(2,1)S(1)}, bf16[32,1152]{1,0:T(8,128)(2,1)S(1)}, u32[]{:S(2)}, u32[]{:S(2)}) collective-permute-start(bf16[32,1152]{1,0:T(8,128)(2,1)S(1)} %shard_map.101.refs_0_), channel_id=1, source_target_pairs={{0,7},{1,0},{2,1},{3,2},{4,3},{5,4},{6,5},{7,6},{8,15},{9,8},{10,9... | collective-permute-start | bytes 221192 | tf_op jit(solution)/shard_map/ppermute | solution.py:301
  16.3 5.1 %collective-permute-start.1 = (bf16[32,1152]{1,0:T(8,128)(2,1)S(1)}, bf16[32,1152]{1,0:T(8,128)(2,1)S(1)}, u32[]{:S(2)}, u32[]{:S(2)}) collective-permute-start(bf16[32,1152]{1,0:T(8,128)(2,1)S(1)} %shard_map.101.refs_0_), channel_id=1, source_target_pairs={{0,1},{1,2},{2,3},{3,4},{4,5},{5,6},{6,7},{7,0},{8,9},{9,10},{10,1... | collective-permute-start | bytes 221192 | tf_op jit(solution)/shard_map/ppermute | solution.py:302
  21.5 10.7 %copy-start.2 = (bf16[2560,640]{1,0:T(8,128)(2,1)S(1)}, bf16[2560,640]{1,0:T(8,128)(2,1)}, u32[]{:S(2)}) copy-start(bf16[2560,640]{1,0:T(8,128)(2,1)} %weight.7) | copy-start | bytes 9830404
  21.5 7.9 %collective-permute-start.3 = (bf16[32,1152]{1,0:T(8,128)(2,1)S(1)}, bf16[32,1152]{1,0:T(8,128)(2,1)S(1)}, u32[]{:S(2)}, u32[]{:S(2)}) collective-permute-start(bf16[32,1152]{1,0:T(8,128)(2,1)S(1)} %collective-permute-done.1.refs_1_), channel_id=1, source_target_pairs={{0,1},{1,2},{2,3},{3,4},{4,5},{5,6},{6,7},{7,0},{8,9},{9,10},{10,1... | collective-permute-start | bytes 221192 | tf_op jit(solution)/shard_map/ppermute | solution.py:302
  21.6 7.8 %collective-permute-start.4 = (bf16[32,1152]{1,0:T(8,128)(2,1)S(1)}, bf16[32,1152]{1,0:T(8,128)(2,1)S(1)}, u32[]{:S(2)}, u32[]{:S(2)}) collective-permute-start(bf16[32,1152]{1,0:T(8,128)(2,1)S(1)} %collective-permute-done.2.refs_2_), channel_id=1, source_target_pairs={{0,7},{1,0},{2,1},{3,2},{4,3},{5,4},{6,5},{7,6},{8,15},{9,8},{10,9... | collective-permute-start | bytes 221192 | tf_op jit(solution)/shard_map/ppermute | solution.py:301
  29.4 5.2 %collective-permute-start.5 = (bf16[32,1152]{1,0:T(8,128)(2,1)S(1)}, bf16[32,1152]{1,0:T(8,128)(2,1)S(1)}, u32[]{:S(2)}, u32[]{:S(2)}) collective-permute-start(bf16[32,1152]{1,0:T(8,128)(2,1)S(1)} %collective-permute-done.3.refs_3_), channel_id=1, source_target_pairs={{0,1},{1,2},{2,3},{3,4},{4,5},{5,6},{6,7},{7,0},{8,9},{9,10},{10,1... | collective-permute-start | bytes 221192 | tf_op jit(solution)/shard_map/ppermute | solution.py:302
  29.5 5.1 %collective-permute-start.6 = (bf16[32,1152]{1,0:T(8,128)(2,1)S(1)}, bf16[32,1152]{1,0:T(8,128)(2,1)S(1)}, u32[]{:S(2)}, u32[]{:S(2)}) collective-permute-start(bf16[32,1152]{1,0:T(8,128)(2,1)S(1)} %collective-permute-done.4.refs_4_), channel_id=1, source_target_pairs={{0,7},{1,0},{2,1},{3,2},{4,3},{5,4},{6,5},{7,6},{8,15},{9,8},{10,9... | collective-permute-start | bytes 221192 | tf_op jit(solution)/shard_map/ppermute | solution.py:301
  34.6 4.5 %collective-permute-start.7 = (bf16[32,1152]{1,0:T(8,128)(2,1)S(1)}, bf16[32,1152]{1,0:T(8,128)(2,1)S(1)}, u32[]{:S(2)}, u32[]{:S(2)}) collective-permute-start(bf16[32,1152]{1,0:T(8,128)(2,1)S(1)} %collective-permute-done.5.refs_5_), channel_id=1, source_target_pairs={{0,1},{1,2},{2,3},{3,4},{4,5},{5,6},{6,7},{7,0},{8,9},{9,10},{10,1... | collective-permute-start | bytes 221192 | tf_op jit(solution)/shard_map/ppermute | solution.py:302
  34.7 4.4 %copy-start.6 = (f32[4,256]{1,0:T(4,128)S(1)}, f32[4,256]{1,0:T(4,128)}, u32[]{:S(2)}) copy-start(f32[4,256]{1,0:T(4,128)} %taps.5) | copy-start | bytes 12292
  60.8 25.7 %copy-start.7 = (f32[640]{0:T(1024)S(1)}, f32[640]{0:T(1024)}, u32[]{:S(2)}) copy-start(f32[640]{0:T(1024)} %gain.1) | copy-start | bytes 7684

commit v5 on v4

--- a/solution.py
+++ b/solution.py
@@ -53,16 +53,16 @@
     return dot(jnp.concatenate([high, middle], axis=1), spread)
 
 
-def transposed(part, pad):
-    pad[:, : part.shape[1]] = part
-    return jnp.transpose(pad[...])[: part.shape[1]].astype(BF16)
-
-
-def bc_kernel(chunk, hidden, weight, out, pad):
+def bc_kernel(chunk, hidden, weight, step_weight, out, steps, pad, joined):
+    share = weight.shape[0]
+    joined[...] = jnp.zeros_like(joined)
+    joined[: step_weight.shape[0], :] = step_weight[...]
+    joined[16 : 16 + share, :] = weight[...]
     pad[...] = jnp.zeros_like(pad)
     for r in range(0, hidden.shape[0], chunk):
-        part = dot_nt(hidden[r : r + chunk, :], weight[...])
-        out[:, r : r + chunk] = transposed(part, pad)
+        pad[:, : 16 + share] = dot_nt(hidden[r : r + chunk, :], joined[...])
+        steps[r : r + chunk, :] = pad[...]
+        out[:, r : r + chunk] = jnp.transpose(pad[...])[16 : 16 + share].astype(BF16)
 
 
 def join_kernel(batch, halo, weight, own, out, pad):
@@ -76,25 +76,24 @@
 
 
 def value_kernel(
-    b, length, step_bias, log_rate, hidden, halo, weight, taps, step_weight,
-    scaled, opening, rows, decays, padded, step_pad,
+    b, length, heads, step_bias, log_rate, hidden, halo, weight, taps, steps_in,
+    scaled, opening, rows, decays, padded,
 ):
     inner = weight.shape[1]
-    heads = step_weight.shape[0]
     spread = head_lanes(inner)
-    step_pad[...] = jnp.zeros_like(step_pad)
-    step_pad[:heads, :] = step_weight[...]
     lane = lax.broadcasted_iota(jnp.int32, (1, LANES), 1)
     bias, rate = jnp.zeros((1, LANES), F32), jnp.full((1, LANES), -1e30, F32)
     for h in range(heads):
         bias = jnp.where(lane == h, step_bias[h], bias)
         rate = jnp.where(lane == h, log_rate[h], rate)
     rate = jnp.exp(rate)
-    own = hidden[b * length : (b + 1) * length, :]
-    before = dot(halo[...], weight[...]).astype(BF16).astype(F32)
-    padded[0:8, :] = before[8 * b : 8 * b + 8]
-    padded[8 : 8 + length, :] = dot(own, weight[...]).astype(BF16).astype(F32)
-    step_pre = dot_nt(own, step_pad[...]) + bias
+    own = slice(b * length, (b + 1) * length)
+    both = jnp.concatenate([halo[...], hidden[own, :]], axis=0)
+    first = halo.shape[0]
+    both = dot(both, weight[...]).astype(BF16).astype(F32)
+    padded[0:8, :] = both[8 * b : 8 * b + 8]
+    padded[8:, :] = both[first:]
+    step_pre = steps_in[own, :] + bias
     steps = jnp.maximum(step_pre, 0.0) + jnp.log1p(jnp.exp(-jnp.abs(step_pre)))
     width = 3 * BLOCK
     i = lax.broadcasted_iota(jnp.int32, (BLOCK, width), 0)
@@ -258,12 +257,12 @@
     smem = pl.BlockSpec(memory_space=pltpu.SMEM)
     tail = hidden_in[:, length - 8 :, :]
     halo = lax.ppermute(tail, "seq", [(i, i + 1) for i in range(seq - 1)]).reshape(8 * batch, width)
-    own = call(
+    own, step_pre = call(
         functools.partial(bc_kernel, 256),
-        [((share, tokens), BF16)],
-        scratch=[((256, LANES), F32)],
+        [((share, tokens), BF16), ((tokens, LANES), F32)],
+        scratch=[((256, LANES), F32), ((16 + share, width), BF16)],
         flops=6 * tokens * width * share,
-    )(hidden, weight)
+    )(hidden, weight, step_weight)
     shard = call(
         functools.partial(join_kernel, batch),
         [((share, tokens + LANES), BF16)],
@@ -274,7 +273,7 @@
 
     def value_of(b, hidden):
         return call(
-            functools.partial(value_kernel, b, length),
+            functools.partial(value_kernel, b, length, heads),
             [
                 ((length, inner), BF16),
                 ((length, LANES), F32),
@@ -283,9 +282,9 @@
             ],
             ins=[smem] * 2 + [WHOLE] * 5,
             outs=[WHOLE] * 4,
-            scratch=[((length + 8, inner), F32), ((LANES, width), BF16)],
+            scratch=[((length + 8, inner), F32)],
             flops=work,
-        )(step_bias, log_rate, hidden, halo, value_proj, value_conv, step_weight)
+        )(step_bias, log_rate, hidden, halo, value_proj, value_conv, step_pre)
 
     def gate_of(b, hidden, opening):
         return call(

time: 88.2 us -> 87.1 us (0.988)
  Pallas kernels: 22.9 us -> 20.4 us
    pallas_call x3, Pallas kernels: 11.7 us -> 9.19 us  [the longest x2 7.57 us: value_of(): call(functools.partial(value_kernel, b, length, heads), [((length, inner)...]
  transfers between devices with their start and end apart: 8 -> 8, of which waited for: 1 -> 2; matrix products, arithmetic and copies ran while one was open for 0% -> 0% of each run, Pallas kernels for 19% -> 16%
where the time goes in v5:
time: 87.1 us; the launch traced here: 86.7 us
  blocking collectives  42.4 us (49%)
  Pallas kernels  20.4 us (23%)
  starting transfers between devices  15.7 us (18%)
  local copies, waits for them, and re-layouts  5.23 us (6%)
  waiting for transfers between devices  2.78 us (3%)
    all_to_all x1, blocking collectives, on_device(): lax.all_to_all(sent.reshape(seq, -1, inner + LANES), 'seq', 0, 0, tiled=T...  20.1 us
    all_to_all x1, blocking collectives, on_device(): lax.all_to_all(prefix, 'seq', 0, 0, tiled=True).reshape(batch, STATE, inner)  13 us
    ppermute x3, starting transfers between devices, on_device(): to_left = lax.ppermute(right, 'tp', down) if 2 * r + 2 < tp else right  11 us
    all_to_all x1, blocking collectives, on_device(): whole = lax.all_to_all(squares, 'tp', 0, 0, tiled=True)  9.33 us
    pallas_call x2, Pallas kernels, value_of(): call(functools.partial(value_kernel, b, length, heads), [((length, inner)...  7.57 us
    pallas_call x2, Pallas kernels, gate_of(): call(functools.partial(gate_kernel, b, length), [((length, inner), BF16)]...  4.86 us
    ppermute x1, starting transfers between devices, on_device(): lax.ppermute(tail, 'seq', [(i, i + 1) for i in range(seq - 1)])  4.49 us
    unnamed x24, local copies, waits for them, and re-layouts  4.33 us
  transfers between devices with their start and end apart: 8, of which 2 were waited for; matrix products, arithmetic and copies ran while one was open for 0% of the time, Pallas kernels for 16%

profile of v5, /device:TPU:1, one launch (start us, length us, event | category | flops | bytes accessed | tf_op | source)
XLA Modules:
  0.0 86.7 jit_solution(11902818430143179918)
XLA Ops:
  0.0 0.9 %slice.3 = bf16[2,8,2560]{2,1,0:T(8,128)(2,1)S(1)} slice(bf16[2,512,2560]{2,1,0:T(8,128)(2,1)} %param.10), slice={[0:2], [504:512], [0:2560]} | slice | bytes 163840 | tf_op jit(solution)/shard_map/slice | solution.py:258
  0.9 4.5 %collective-permute-start = (bf16[2,8,2560]{2,1,0:T(8,128)(2,1)S(1)}, bf16[2,8,2560]{2,1,0:T(8,128)(2,1)S(1)}, u32[]{:S(2)}, u32[]{:S(2)}) collective-permute-start(bf16[2,8,2560]{2,1,0:T(8,128)(2,1)S(1)} %slice.3), channel_id=1, source_target_pairs={{0,8},{8,16},{16,24},{24,32},{32,40},{40,48},{48,56},{56,64},{64,7... | collective-permute-start | bytes 245768 | tf_op jit(solution)/shard_map/ppermute | solution.py:259
  5.4 0.0 copy-start
  5.4 2.5 %copy-done = bf16[2,512,2560]{2,1,0:T(8,128)(2,1)S(1)} copy-done((bf16[2,512,2560]{2,1,0:T(8,128)(2,1)S(1)}, bf16[2,512,2560]{2,1,0:T(8,128)(2,1)}, u32[]{:S(2)}) %copy-start) | copy-done | bytes 5242904
  7.9 0.9 %copy-done.3 = bf16[2560,32]{0,1:T(8,128)(2,1)S(1)} copy-done((bf16[2560,32]{0,1:T(8,128)(2,1)S(1)}, bf16[2560,32]{0,1:T(8,128)(2,1)}, u32[]{:S(2)}) %copy-start.3) | copy-done | bytes 163864
  8.8 0.9 %copy-done.4 = bf16[2560,10]{0,1:T(8,128)(2,1)S(1)} copy-done((bf16[2560,10]{0,1:T(8,128)(2,1)S(1)}, bf16[2560,10]{0,1:T(8,128)(2,1)}, u32[]{:S(2)}) %copy-start.4) | copy-done | bytes 51224
  9.7 1.6 %shard_map.100 = (bf16[32,1024]{1,0:T(8,128)(2,1)S(1)}, f32[1024,128]{1,0:T(8,128)S(1)}) custom-call(bf16[1024,2560]{1,0:T(8,128)(2,1)S(1)} %bitcast.8, bf16[32,2560]{1,0:T(8,128)(2,1)S(1)} %bitcast.20, bf16[10,2560]{1,0:T(8,128)(2,1)S(1)} %bitcast.22), custom_call_target="tpu_custom_call" | custom-call | flops 503316480 | tf_op jit(solution)/shard_map/pallas_call | solution.py:260
  11.3 0.0 collective-permute-done
  11.3 0.0 slice-start.1
  11.3 0.0 copy-start.1
  11.4 0.0 copy-start.5
  11.4 0.0 copy-start.8
  11.4 0.0 copy-start.9
  11.4 0.2 shard_map.101.refs_0_
  11.6 5.6 %collective-permute-start.2 = (bf16[32,1152]{1,0:T(8,128)(2,1)S(1)}, bf16[32,1152]{1,0:T(8,128)(2,1)S(1)}, u32[]{:S(2)}, u32[]{:S(2)}) collective-permute-start(bf16[32,1152]{1,0:T(8,128)(2,1)S(1)} %shard_map.101.refs_0_), channel_id=1, source_target_pairs={{0,7},{1,0},{2,1},{3,2},{4,3},{5,4},{6,5},{7,6},{8,15},{9,8},{10,9... | collective-permute-start | bytes 221192 | tf_op jit(solution)/shard_map/ppermute | solution.py:300
  17.2 0.0 collective-permute-start.1
  17.2 0.0 slice-done
  17.2 0.0 slice-done.1
  17.2 0.0 copy-done.1
  17.3 0.0 copy-done.5
  17.3 0.0 copy-done.8
  17.3 3.8 %shard_map.102 = (bf16[512,640]{1,0:T(8,128)(2,1)S(1)}, f32[512,128]{1,0:T(8,128)S(1)}, f32[8,640]{1,0:T(8,128)S(1)}, bf16[8,128]{1,0:T(8,128)(2,1)S(1)}) custom-call(f32[10]{0:T(128)S(1)} %copy-done.8, f32[10]{0:T(128)S(1)} %copy-done.9, bf16[1024,2560]{1,0:T(8,128)(2,1)S(1)} %bitcast.11, bf16[16,2560]{1,0:T(8,128)(2,1)S(1)} %bitcast.18, ...), custom_call_target="tpu_custom_call" | custom-call | flops 1677721600 | tf_op jit(solution)/shard_map/pallas_call | solution.py:275
  21.1 0.0 collective-permute-done.2.refs_2_
  21.1 0.8 collective-permute-done.1.refs_1_
  21.9 0.0 collective-permute-start.3
  21.9 2.7 %collective-permute-start.4 = (bf16[32,1152]{1,0:T(8,128)(2,1)S(1)}, bf16[32,1152]{1,0:T(8,128)(2,1)S(1)}, u32[]{:S(2)}, u32[]{:S(2)}) collective-permute-start(bf16[32,1152]{1,0:T(8,128)(2,1)S(1)} %collective-permute-done.2.refs_2_), channel_id=1, source_target_pairs={{0,7},{1,0},{2,1},{3,2},{4,3},{5,4},{6,5},{7,6},{8,15},{9,8},{10,9... | collective-permute-start | bytes 221192 | tf_op jit(solution)/shard_map/ppermute | solution.py:300
  24.6 3.8 %shard_map.103 = (bf16[512,640]{1,0:T(8,128)(2,1)S(1)}, f32[512,128]{1,0:T(8,128)S(1)}, f32[8,640]{1,0:T(8,128)S(1)}, bf16[8,128]{1,0:T(8,128)(2,1)S(1)}) custom-call(f32[10]{0:T(128)S(1)} %copy-done.8, f32[10]{0:T(128)S(1)} %copy-done.9, bf16[1024,2560]{1,0:T(8,128)(2,1)S(1)} %bitcast.12, bf16[16,2560]{1,0:T(8,128)(2,1)S(1)} %bitcast.19, ...), custom_call_target="tpu_custom_call" | custom-call | flops 1677721600 | tf_op jit(solution)/shard_map/pallas_call | solution.py:275
  28.4 0.0 collective-permute-done.3.refs_3_
  28.4 0.0 collective-permute-done.4.refs_4_
  28.4 0.1 collective-permute-start.5
  28.5 2.7 %collective-permute-start.6 = (bf16[32,1152]{1,0:T(8,128)(2,1)S(1)}, bf16[32,1152]{1,0:T(8,128)(2,1)S(1)}, u32[]{:S(2)}, u32[]{:S(2)}) collective-permute-start(bf16[32,1152]{1,0:T(8,128)(2,1)S(1)} %collective-permute-done.4.refs_4_), channel_id=1, source_target_pairs={{0,7},{1,0},{2,1},{3,2},{4,3},{5,4},{6,5},{7,6},{8,15},{9,8},{10,9... | collective-permute-start | bytes 221192 | tf_op jit(solution)/shard_map/ppermute | solution.py:300
  31.2 0.0 copy-done.2
  31.2 2.4 %shard_map.104.refs_2_ = bf16[512,640]{1,0:T(8,128)(2,1)S(1)} custom-call(bf16[1024,2560]{1,0:T(8,128)(2,1)S(1)} %bitcast.13, bf16[2560,640]{1,0:T(8,128)(2,1)S(1)} %copy-done.2, f32[512,128]{1,0:T(8,128)S(1)} %get-tuple-element.45.opening), custom_call_target="tpu_custom_call" | custom-call | flops 1677721600 | tf_op jit(solution)/shard_map/pallas_call | solution.py:290
  33.6 0.0 collective-permute-done.5.refs_5_
  33.6 0.0 collective-permute-done.6.refs_6_
  33.6 0.1 collective-permute-start.7
  33.7 0.0 copy-start.6
  33.7 2.4 %shard_map.105.refs_3_ = bf16[512,640]{1,0:T(8,128)(2,1)S(1)} custom-call(bf16[1024,2560]{1,0:T(8,128)(2,1)S(1)} %bitcast.14, bf16[2560,640]{1,0:T(8,128)(2,1)S(1)} %copy-done.2, f32[512,128]{1,0:T(8,128)S(1)} %get-tuple-element.49.opening), custom_call_target="tpu_custom_call" | custom-call | flops 1677721600 | tf_op jit(solution)/shard_map/pallas_call | solution.py:290
  36.2 2.0 %collective-permute-done.7.refs_7_ = bf16[32,1152]{1,0:T(8,128)(2,1)S(1)} collective-permute-done((bf16[32,1152]{1,0:T(8,128)(2,1)S(1)}, bf16[32,1152]{1,0:T(8,128)(2,1)S(1)}, u32[]{:S(2)}, u32[]{:S(2)}) %collective-permute-start.7) | collective-permute-done | bytes 73760 | tf_op jit(solution)/shard_map/ppermute | solution.py:301
  38.1 0.0 copy-done.6
  38.1 2.2 %shard_map.106 = (bf16[2,128,512]{2,1,0:T(8,128)(2,1)S(1)}, bf16[1024,128]{1,0:T(8,128)(2,1)S(1)}, bf16[8,128,640]{2,1,0:T(8,128)(2,1)S(1)}, bf16[2,16,8,768]{3,2,1,0:T(8,128)(2,1)S(1)}) custom-call(s32[1]{0:T(128)} %bitcast.place, f32[4,256]{1,0:T(4,128)S(1)} %copy-done.6, bf16[32,1152]{1,0:T(8,128)(2,1)S(1)} %shard_map.101.refs_0_, ...), custom_call_target="tpu_custom_call" | custom-call | tf_op jit(solution)/shard_map/pallas_call | solution.py:320
  40.3 20.1 %all_to_all.15.got = bf16[32,8,768]{2,1,0:T(8,128)(2,1)S(1)} all-to-all(bf16[32,8,768]{2,1,0:T(8,128)(2,1)S(1)} %bitcast.16), channel_id=1, replica_groups=mesh['seq'=32,'tp'=8] {'seq'}, dimensions={0} | all-to-all | bytes 786432 | tf_op jit(solution)/shard_map/all_to_all | solution.py:332
  60.4 0.3 shard_map.107
  60.7 13.0 %all_to_all.16 = bf16[32,8,640]{2,1,0:T(8,128)(2,1)S(1)} all-to-all(bf16[32,8,640]{2,1,0:T(8,128)(2,1)S(1)} %shard_map.107), channel_id=1, replica_groups=mesh['seq'=32,'tp'=8] {'seq'}, dimensions={0} | all-to-all | bytes 655360 | tf_op jit(solution)/shard_map/all_to_all | solution.py:338
  73.7 2.3 %shard_map.108 = (f32[1024,640]{1,0:T(8,128)S(1)}, f32[8,8,128]{2,1,0:T(8,128)S(1)}) custom-call(bf16[2,128,640]{2,1,0:T(8,128)(2,1)S(1)} %bitcast.15, bf16[2,128,512]{2,1,0:T(8,128)(2,1)S(1)} %get-tuple-element.58.b_rows, bf16[1024,128]{1,0:T(8,128)(2,1)S(1)} %get-tuple-element.59.c_rows, bf16[8,128,640]{2,1,0:T(8,128)(2,1)S(1)} %get-tuple-element.60.starts, ...), custom_call_target="tpu_custom_call" | custom-call | tf_op jit(solution)/shard_map/pallas_call | solution.py:339
  76.0 9.3 %all_to_all.17.squares = f32[8,8,128]{2,1,0:T(8,128)S(1)} all-to-all(f32[8,8,128]{2,1,0:T(8,128)S(1)} %get-tuple-element.64), channel_id=1, replica_groups=mesh['seq'=32,'tp'=8] {'tp'}, dimensions={0} | all-to-all | bytes 65536 | tf_op jit(solution)/shard_map/all_to_all | solution.py:343
  85.3 0.0 copy-done.7
  85.3 1.4 %shard_map.109 = bf16[1024,640]{1,0:T(8,128)(2,1)} custom-call(f32[1024,640]{1,0:T(8,128)S(1)} %get-tuple-element.63.gated, f32[8,8,128]{2,1,0:T(8,128)S(1)} %all_to_all.17.squares, f32[640]{0:T(1024)S(1)} %copy-done.7), custom_call_target="tpu_custom_call" | custom-call | tf_op jit(solution)/shard_map/pallas_call | solution.py:344
  (7 shorter events, 0.0 us)
Async XLA Ops:
  0.9 10.4 %collective-permute-start = (bf16[2,8,2560]{2,1,0:T(8,128)(2,1)S(1)}, bf16[2,8,2560]{2,1,0:T(8,128)(2,1)S(1)}, u32[]{:S(2)}, u32[]{:S(2)}) collective-permute-start(bf16[2,8,2560]{2,1,0:T(8,128)(2,1)S(1)} %slice.3), channel_id=1, source_target_pairs={{0,8},{8,16},{16,24},{24,32},{32,40},{40,48},{48,56},{56,64},{64,7... | collective-permute-start | bytes 245768 | tf_op jit(solution)/shard_map/ppermute | solution.py:259
  5.4 2.5 %copy-start = (bf16[2,512,2560]{2,1,0:T(8,128)(2,1)S(1)}, bf16[2,512,2560]{2,1,0:T(8,128)(2,1)}, u32[]{:S(2)}) copy-start(bf16[2,512,2560]{2,1,0:T(8,128)(2,1)} %param.10) | copy-start | bytes 15728644
  7.9 0.9 %copy-start.3 = (bf16[2560,32]{0,1:T(8,128)(2,1)S(1)}, bf16[2560,32]{0,1:T(8,128)(2,1)}, u32[]{:S(2)}) copy-start(bf16[2560,32]{0,1:T(8,128)(2,1)} %param.13) | copy-start | bytes 491524
  8.8 0.9 %copy-start.4 = (bf16[2560,10]{0,1:T(8,128)(2,1)S(1)}, bf16[2560,10]{0,1:T(8,128)(2,1)}, u32[]{:S(2)}) copy-start(bf16[2560,10]{0,1:T(8,128)(2,1)} %param.14) | copy-start | bytes 153604
  9.7 7.5 %slice-start = ((s8[5242880]{0:T(1024)(128)(4,1)}), s8[4194304]{0:T(1024)(128)(4,1)S(1)}, s32[]{:S(2)}) async-start(s8[5242880]{0:T(1024)(128)(4,1)} %bitcast.9), calls=%async_computation.3 | async-start | bytes 8388608
  11.3 5.9 %slice-start.1 = ((s8[5242880]{0:T(1024)(128)(4,1)}), s8[1048576]{0:T(1024)(128)(4,1)S(1)}, s32[]{:S(2)}) async-start(s8[5242880]{0:T(1024)(128)(4,1)} %bitcast.9), calls=%async_computation.4 | async-start | bytes 2097152
  11.3 5.9 %copy-start.1 = (bf16[2560,640]{1,0:T(8,128)(2,1)S(1)}, bf16[2560,640]{1,0:T(8,128)(2,1)}, u32[]{:S(2)}) copy-start(bf16[2560,640]{1,0:T(8,128)(2,1)} %weight.5) | copy-start | bytes 9830404
  11.4 5.9 %copy-start.5 = (f32[4,640]{1,0:T(4,128)S(1)}, f32[4,640]{1,0:T(4,128)}, u32[]{:S(2)}) copy-start(f32[4,640]{1,0:T(4,128)} %taps.4) | copy-start | bytes 30724
  11.4 5.9 %copy-start.8 = (f32[10]{0:T(128)S(1)}, f32[10]{0:T(128)}, u32[]{:S(2)}) copy-start(f32[10]{0:T(128)} %step_bias.3) | copy-start | bytes 124
  11.4 5.9 %copy-start.9 = (f32[10]{0:T(128)S(1)}, f32[10]{0:T(128)}, u32[]{:S(2)}) copy-start(f32[10]{0:T(128)} %log_rate.3) | copy-start | bytes 124
  11.6 9.5 %collective-permute-start.2 = (bf16[32,1152]{1,0:T(8,128)(2,1)S(1)}, bf16[32,1152]{1,0:T(8,128)(2,1)S(1)}, u32[]{:S(2)}, u32[]{:S(2)}) collective-permute-start(bf16[32,1152]{1,0:T(8,128)(2,1)S(1)} %shard_map.101.refs_0_), channel_id=1, source_target_pairs={{0,7},{1,0},{2,1},{3,2},{4,3},{5,4},{6,5},{7,6},{8,15},{9,8},{10,9... | collective-permute-start | bytes 221192 | tf_op jit(solution)/shard_map/ppermute | solution.py:300
  17.2 4.7 %collective-permute-start.1 = (bf16[32,1152]{1,0:T(8,128)(2,1)S(1)}, bf16[32,1152]{1,0:T(8,128)(2,1)S(1)}, u32[]{:S(2)}, u32[]{:S(2)}) collective-permute-start(bf16[32,1152]{1,0:T(8,128)(2,1)S(1)} %shard_map.101.refs_0_), channel_id=1, source_target_pairs={{0,1},{1,2},{2,3},{3,4},{4,5},{5,6},{6,7},{7,0},{8,9},{9,10},{10,1... | collective-permute-start | bytes 221192 | tf_op jit(solution)/shard_map/ppermute | solution.py:301
  21.9 9.2 %copy-start.2 = (bf16[2560,640]{1,0:T(8,128)(2,1)S(1)}, bf16[2560,640]{1,0:T(8,128)(2,1)}, u32[]{:S(2)}) copy-start(bf16[2560,640]{1,0:T(8,128)(2,1)} %weight.7) | copy-start | bytes 9830404
  21.9 6.5 %collective-permute-start.3 = (bf16[32,1152]{1,0:T(8,128)(2,1)S(1)}, bf16[32,1152]{1,0:T(8,128)(2,1)S(1)}, u32[]{:S(2)}, u32[]{:S(2)}) collective-permute-start(bf16[32,1152]{1,0:T(8,128)(2,1)S(1)} %collective-permute-done.1.refs_1_), channel_id=1, source_target_pairs={{0,1},{1,2},{2,3},{3,4},{4,5},{5,6},{6,7},{7,0},{8,9},{9,10},{10,1... | collective-permute-start | bytes 221192 | tf_op jit(solution)/shard_map/ppermute | solution.py:301
  21.9 6.5 %collective-permute-start.4 = (bf16[32,1152]{1,0:T(8,128)(2,1)S(1)}, bf16[32,1152]{1,0:T(8,128)(2,1)S(1)}, u32[]{:S(2)}, u32[]{:S(2)}) collective-permute-start(bf16[32,1152]{1,0:T(8,128)(2,1)S(1)} %collective-permute-done.2.refs_2_), channel_id=1, source_target_pairs={{0,7},{1,0},{2,1},{3,2},{4,3},{5,4},{6,5},{7,6},{8,15},{9,8},{10,9... | collective-permute-start | bytes 221192 | tf_op jit(solution)/shard_map/ppermute | solution.py:300
  28.4 5.2 %collective-permute-start.5 = (bf16[32,1152]{1,0:T(8,128)(2,1)S(1)}, bf16[32,1152]{1,0:T(8,128)(2,1)S(1)}, u32[]{:S(2)}, u32[]{:S(2)}) collective-permute-start(bf16[32,1152]{1,0:T(8,128)(2,1)S(1)} %collective-permute-done.3.refs_3_), channel_id=1, source_target_pairs={{0,1},{1,2},{2,3},{3,4},{4,5},{5,6},{6,7},{7,0},{8,9},{9,10},{10,1... | collective-permute-start | bytes 221192 | tf_op jit(solution)/shard_map/ppermute | solution.py:301
  28.5 5.1 %collective-permute-start.6 = (bf16[32,1152]{1,0:T(8,128)(2,1)S(1)}, bf16[32,1152]{1,0:T(8,128)(2,1)S(1)}, u32[]{:S(2)}, u32[]{:S(2)}) collective-permute-start(bf16[32,1152]{1,0:T(8,128)(2,1)S(1)} %collective-permute-done.4.refs_4_), channel_id=1, source_target_pairs={{0,7},{1,0},{2,1},{3,2},{4,3},{5,4},{6,5},{7,6},{8,15},{9,8},{10,9... | collective-permute-start | bytes 221192 | tf_op jit(solution)/shard_map/ppermute | solution.py:300
  33.6 4.5 %collective-permute-start.7 = (bf16[32,1152]{1,0:T(8,128)(2,1)S(1)}, bf16[32,1152]{1,0:T(8,128)(2,1)S(1)}, u32[]{:S(2)}, u32[]{:S(2)}) collective-permute-start(bf16[32,1152]{1,0:T(8,128)(2,1)S(1)} %collective-permute-done.5.refs_5_), channel_id=1, source_target_pairs={{0,1},{1,2},{2,3},{3,4},{4,5},{5,6},{6,7},{7,0},{8,9},{9,10},{10,1... | collective-permute-start | bytes 221192 | tf_op jit(solution)/shard_map/ppermute | solution.py:301
  33.7 4.4 %copy-start.6 = (f32[4,256]{1,0:T(4,128)S(1)}, f32[4,256]{1,0:T(4,128)}, u32[]{:S(2)}) copy-start(f32[4,256]{1,0:T(4,128)} %taps.5) | copy-start | bytes 12292
  60.4 24.9 %copy-start.7 = (f32[640]{0:T(1024)S(1)}, f32[640]{0:T(1024)}, u32[]{:S(2)}) copy-start(f32[640]{0:T(1024)} %gain.1) | copy-start | bytes 7684

commit v6 on v5

--- a/solution.py
+++ b/solution.py
@@ -13,6 +13,7 @@
 STATE = 128
 CONV = 4
 BLOCK = 128
+WAYS = 4
 LANES = 128
 EPSILON = 1e-05
 
@@ -133,7 +134,7 @@
     shards, refs = refs[: len(steps)], refs[len(steps) :]
     scaled, refs = refs[:batch], refs[batch:]
     rows, refs = refs[:batch], refs[batch:]
-    decays, (b_rows, c_rows, starts, sent, mixed, columns) = refs[:batch], refs[batch:]
+    decays, (b_rows, c_rows, starts, mine, other, mixed, columns) = refs[:batch], refs[batch:]
     blocks = length // BLOCK
     inner = scaled[0].shape[1]
     share = shards[0].shape[0]
@@ -163,30 +164,113 @@
             starts[b * blocks + k] = ready.astype(BF16)
             at = slice(k * BLOCK, (k + 1) * BLOCK)
             state = half * (ready + dot(b_t[:, at], scaled[b][at, :]))
-        for g in range(STATE // 8):
-            sent[b, g, :, :inner] = state[8 * g : 8 * g + 8].astype(BF16)
-            sent[b, g, :, inner:] = decays[b][...]
-
-
-def scan_kernel(got, out, table, logs):
-    devices, _, width = got.shape
+
+        def keep(target, state=state, b=b):
+            for g in range(STATE // 8):
+                target[g, :, :inner] = state[8 * g : 8 * g + 8].astype(BF16)
+                target[g, :, inner:] = decays[b][...]
+
+        pl.when(place[1] == b)(functools.partial(keep, mine))
+        pl.when(place[1] != b)(functools.partial(keep, other))
+
+
+def log_decay(state):
+    parts = state[0, :, state.shape[2] - LANES :].astype(F32)
+    return parts[0:1] + parts[1:2] + parts[2:3]
+
+
+def log_rows(log):
+    high, middle, low = split_in_three(log)
+    return jnp.concatenate([high, middle, low, jnp.zeros((5, LANES), BF16)], axis=0)
+
+
+def with_log(target, g, state, log):
+    inner = target.shape[2] - LANES
+    target[g, :, :inner] = state.astype(BF16)
+    target[g, :, inner:] = log
+
+
+def decay_rows(logs, inner):
+    logs = logs + [jnp.zeros((1, LANES), F32)] * (8 - len(logs))
+    return jnp.exp(over_channels(jnp.concatenate(logs, axis=0), head_lanes(inner)))
+
+
+def chip_kernel(place, mine, got, *refs):
+    parts, chip = refs[:-1], refs[-1]
+    groups, _, width = mine.shape
     inner = width - LANES
-    for s in range(devices):
-        parts = got[s, :, inner:].astype(F32)
-        table[s : s + 1, :] = parts[0:1] + parts[1:2] + parts[2:3]
-    logs[...] = jnp.exp(over_channels(table[...], head_lanes(inner)))
-    state = jnp.zeros((8, inner), F32)
-    for s in range(devices):
-        out[s] = state.astype(BF16)
-        state = logs[s : s + 1, :] * state + got[s, :, :inner].astype(F32)
-
-
-def gated_kernel(batch, length, arrived, b_rows, c_rows, starts, *refs):
-    scaled, refs = refs[:batch], refs[batch:]
-    opened, refs = refs[:batch], refs[batch:]
-    rows, (gated, squares) = refs[:batch], refs[batch:]
+    first = place[1] == 0
+    log_mine, log_got = log_decay(mine), log_decay(got)
+    later = decay_rows([jnp.where(first, log_got, log_mine)], inner)[0:1]
+    log = log_rows(log_mine + log_got)
+    for g in range(groups):
+        a, b = mine[g, :, :inner].astype(F32), got[g, :, :inner].astype(F32)
+        with_log(chip, g, later * jnp.where(first, a, b) + jnp.where(first, b, a), log)
+    count = groups // len(parts)
+    for d, part in enumerate(parts):
+        part[...] = chip[pl.ds(lax.rem(place[2] + d, len(parts)) * count, count)]
+
+
+def row_kernel(place, *refs):
+    ways = (len(refs) - 4)
+    parts, (row, before, logs, table) = refs[:ways], refs[ways:]
+    count, _, width = row.shape
+    inner = width - LANES
+    for d, part in enumerate(parts):
+        table[lax.rem(place[2] + ways - d, ways)] = part[...]
+    each = [log_decay(table.at[k]) for k in range(ways)]
+    decay = decay_rows(each, inner)
+    total = jnp.zeros((1, LANES), F32)
+    sums = []
+    for k in range(ways):
+        sums.append(total)
+        total = total + each[k]
+    logs[...] = jnp.concatenate(sums + [total] * (8 - ways), axis=0)
+    log = log_rows(total)
+    for g in range(count):
+        state = jnp.zeros((8, inner), F32)
+        for k in range(ways):
+            before[k, g] = state
+            state = decay[k : k + 1] * state + table[k, g, :, :inner].astype(F32)
+        with_log(row, g, state, log)
+
+
+def entering_kernel(place, before, logs, *refs):
+    ways, count, _, inner = before.shape
+    rows, parts, entering = refs[: ways - 1], refs[ways - 1 : -1], refs[-1]
+    decay = decay_rows([log_decay(row) for row in rows], inner)
+    inside = decay_rows([logs[k : k + 1, :] for k in range(ways)], inner)
+    for g in range(count):
+        state = jnp.zeros((8, inner), F32)
+        for d in reversed(range(1, ways)):
+            ahead = decay[d - 1 : d] * state + rows[d - 1][g, :, :inner].astype(F32)
+            state = jnp.where(place[3] >= d, ahead, state)
+        for k in range(ways):
+            entering[k, g] = (before[k, g] + inside[k : k + 1] * state).astype(BF16)
+    for d, part in enumerate(parts):
+        part[...] = entering[lax.rem(place[2] + d, ways)]
+
+
+def arrive_kernel(place, mine, got, *refs):
+    parts, (own, give, whole) = refs[:-3], refs[-3:]
+    ways = len(parts)
+    groups, _, inner = whole.shape
+    count = groups // ways
+    for d, part in enumerate(parts):
+        whole[pl.ds(lax.rem(place[2] + ways - d, ways) * count, count)] = part[...]
+    first = place[1] == 0
+    decay = decay_rows([jnp.where(first, log_decay(mine), log_decay(got))], inner)[0:1]
+    for g in range(groups):
+        state = whole[g].astype(F32)
+        a, b = mine[g, :, :inner].astype(F32), got[g, :, :inner].astype(F32)
+        after = decay * state + jnp.where(first, a, b)
+        own[8 * g : 8 * g + 8, :] = jnp.where(first, state, after).astype(BF16)
+        give[8 * g : 8 * g + 8, :] = jnp.where(first, after, state).astype(BF16)
+
+
+def within_kernel(batch, length, b_rows, c_rows, starts, *refs):
+    scaled, out = refs[:batch], refs[batch]
     blocks = length // BLOCK
-    ones = jnp.ones((8, gated.shape[1]), BF16)
     i = lax.broadcasted_iota(jnp.int32, (BLOCK, BLOCK), 0)
     j = lax.broadcasted_iota(jnp.int32, (BLOCK, BLOCK), 1)
     for b in range(batch):
@@ -196,10 +280,25 @@
             c = c_rows[n * BLOCK : (n + 1) * BLOCK, :]
             scores = dot(c, b_rows[b, :, at])
             scores = jnp.where(i >= j, scores, 0.0).astype(BF16)
-            y = dot(scores, scaled[b][at, :]) + dot(c, starts[n])
-            y = y + rows[b][blocks + k : blocks + k + 1, :] * dot(c, arrived[b])
+            out[n * BLOCK : (n + 1) * BLOCK, :] = dot(scores, scaled[b][at, :]) + dot(c, starts[n])
+
+
+def gated_kernel(batch, length, place, own, taken, within, c_rows, *refs):
+    opened, refs = refs[:batch], refs[batch:]
+    rows, (gated, squares, arrived) = refs[:batch], refs[batch:]
+    blocks = length // BLOCK
+    ones = jnp.ones((8, gated.shape[1]), BF16)
+    arrived[place[1]] = own[...]
+    arrived[1 - place[1]] = taken[...]
+    for b in range(batch):
+        for k in range(blocks):
+            n = b * blocks + k
+            at = slice(k * BLOCK, (k + 1) * BLOCK)
+            token = slice(n * BLOCK, (n + 1) * BLOCK)
+            late = dot(c_rows[token, :], arrived[b])
+            y = within[token, :] + rows[b][blocks + k : blocks + k + 1, :] * late
             g = y * opened[b][at, :].astype(F32)
-            gated[n * BLOCK : (n + 1) * BLOCK, :] = g
+            gated[token, :] = g
             squares[:, n, :] = dot_nt(ones, (g * g).astype(BF16))
 
 
@@ -253,7 +352,8 @@
     hidden = hidden_in.reshape(tokens, width)
     weight = bc_proj.T
     step_weight = step_proj.T
-    place = lax.axis_index("tp").reshape(1)
+    at = lax.axis_index("seq")
+    place = jnp.stack([lax.axis_index("tp"), at % 2, at // 2 % WAYS, at // (2 * WAYS)])
     smem = pl.BlockSpec(memory_space=pltpu.SMEM)
     tail = hidden_in[:, length - 8 :, :]
     halo = lax.ppermute(tail, "seq", [(i, i + 1) for i in range(seq - 1)]).reshape(8 * batch, width)
@@ -317,29 +417,82 @@
         if 2 * r + 2 < tp:
             shards.append(right)
             places.append(r + 1)
-    b_rows, c_rows, starts, sent = call(
+    group, quarter = STATE // 8, STATE // 8 // WAYS
+    full = (group, 8, inner + LANES)
+    part = (quarter, 8, inner + LANES)
+    b_rows, c_rows, starts, mine, other = call(
         functools.partial(state_kernel, batch, length, places),
         [
             ((batch, STATE, length), BF16),
             ((tokens, STATE), BF16),
             ((blocks, STATE, inner), BF16),
-            ((batch, STATE // 8, 8, inner + LANES), BF16),
+            (full, BF16),
+            (full, BF16),
         ],
         ins=[smem] + [WHOLE] * (1 + tp + 3 * batch),
-        outs=[WHOLE] * 4,
+        outs=[WHOLE] * 5,
         scratch=[((states, tokens), F32), ((states, LANES), F32)],
     )(place, bc_conv, *shards, *scaled, *rows, *decays)
-    got = lax.all_to_all(sent.reshape(seq, -1, inner + LANES), "seq", 0, 0, tiled=True)
-    prefix = call(
-        scan_kernel,
-        [((seq, 8, inner), BF16)],
-        scratch=[((seq, LANES), F32), ((seq, inner), F32)],
-    )(got)
-    arrived = lax.all_to_all(prefix, "seq", 0, 0, tiled=True).reshape(batch, STATE, inner)
+
+    def to_core(x):
+        return lax.ppermute(x, "seq", [(i, i ^ 1) for i in range(seq)])
+
+    def along(x, step, stride):
+        ring = stride * WAYS
+        pairs = [(i, i // ring * ring + (i + step * stride) % ring) for i in range(seq)]
+        return lax.ppermute(x, "seq", pairs)
+
+    order = (1, WAYS - 1, *range(2, WAYS - 1))
+
+    def hop(parts, stride):
+        moved = {d: along(parts[d], d, stride) for d in order}
+        return [moved[d] for d in range(1, WAYS)]
+
+    got = to_core(other)
+    leaving = call(
+        chip_kernel,
+        [(part, BF16)] * WAYS,
+        ins=[smem, WHOLE, WHOLE],
+        outs=[WHOLE] * WAYS,
+        scratch=[(full, BF16)],
+    )(place, mine, got)
+    parts = hop(leaving, 2)
+    row, before, logs = call(
+        row_kernel,
+        [(part, BF16), ((WAYS, quarter, 8, inner), F32), ((8, LANES), F32)],
+        ins=[smem] + [WHOLE] * WAYS,
+        outs=[WHOLE] * 3,
+        scratch=[((WAYS,) + part, BF16)],
+    )(place, leaving[0], *parts)
+    row, starts = lax.optimization_barrier((row, starts))
+    others = hop([row] * WAYS, 2 * WAYS)
+    within = call(
+        functools.partial(within_kernel, batch, length), [((tokens, inner), F32)], flops=work // 4
+    )(b_rows, c_rows, starts, *scaled)
+    *others, within = lax.optimization_barrier((*others, within))
+    leaving = call(
+        entering_kernel,
+        [((quarter, 8, inner), BF16)] * WAYS,
+        ins=[smem] + [WHOLE] * (1 + WAYS),
+        outs=[WHOLE] * WAYS,
+        scratch=[((WAYS, quarter, 8, inner), BF16)],
+    )(place, before, logs, *others)
+    parts = hop(leaving, 2)
+    own, give = call(
+        arrive_kernel,
+        [((STATE, inner), BF16)] * 2,
+        ins=[smem] + [WHOLE] * (2 + WAYS),
+        outs=[WHOLE] * 2,
+        scratch=[((group, 8, inner), BF16)],
+    )(place, mine, got, leaving[0], *parts)
+    taken = to_core(give)
     gated, squares = call(
         functools.partial(gated_kernel, batch, length),
         [((tokens, inner), F32), ((tp, blocks, LANES), F32)],
-    )(arrived, b_rows, c_rows, starts, *scaled, *opened, *rows)
+        ins=[smem] + [WHOLE] * (4 + 2 * batch),
+        outs=[WHOLE] * 2,
+        scratch=[((batch, STATE, inner), BF16)],
+    )(place, own, taken, within, c_rows, *opened, *rows)
     whole = lax.all_to_all(squares, "tp", 0, 0, tiled=True)
     out = call(scale_kernel, [((tokens, inner), BF16)])(gated, whole, norm_gain)
     return out.reshape(batch, length, inner)

time: 87.1 us -> 88.6 us (1.017)
  blocking collectives: 42.4 us -> 9.3 us
  starting transfers between devices: 15.7 us -> 37 us
  waiting for transfers between devices: 2.78 us -> 11.4 us
  Pallas kernels: 20.4 us -> 24.9 us
    all_to_all x2 -> x0, blocking collectives: 33.1 us -> none  [the longest x1 20.1 us: on_device(): lax.all_to_all(sent.reshape(seq, -1, inner + LANES), 'seq', 0, 0, tiled=T...]
    ppermute x0 -> x11, starting transfers between devices: none -> 21.4 us  [the longest x9 13.6 us: along(): return lax.ppermute(x, 'seq', pairs)]
    ppermute x0 -> x11, waiting for transfers between devices: none -> 8.61 us  [the longest x9 6.52 us: along(): return lax.ppermute(x, 'seq', pairs)]
    pallas_call x1 -> x5, Pallas kernels: 0.29 us -> 4.49 us  [the longest x1 1.48 us: on_device(): call(functools.partial(within_kernel, batch, length), [((tokens, inner),...]
  transfers between devices with their start and end apart: 8 -> 19, of which waited for: 2 -> 11; matrix products, arithmetic and copies ran while one was open for 0% -> 0% of each run, Pallas kernels for 16% -> 18%
where the time goes in v6:
time: 88.6 us; the launch traced here: 88.3 us
  starting transfers between devices  37 us (42%)
  Pallas kernels  24.9 us (28%)
  waiting for transfers between devices  11.4 us (13%)
  blocking collectives  9.3 us (10%)
  local copies, waits for them, and re-layouts  5.22 us (6%)
    ppermute x9, starting transfers between devices, along(): return lax.ppermute(x, 'seq', pairs)  13.6 us
    ppermute x3, starting transfers between devices, on_device(): to_left = lax.ppermute(right, 'tp', down) if 2 * r + 2 < tp else right  11 us
    all_to_all x1, blocking collectives, on_device(): whole = lax.all_to_all(squares, 'tp', 0, 0, tiled=True)  9.3 us
    ppermute x2, starting transfers between devices, to_core(): return lax.ppermute(x, 'seq', [(i, i ^ 1) for i in range(seq)])  7.83 us
    pallas_call x2, Pallas kernels, value_of(): call(functools.partial(value_kernel, b, length, heads), [((length, inner)...  7.56 us
    ppermute x9, waiting for transfers between devices, along(): return lax.ppermute(x, 'seq', pairs)  6.52 us
    pallas_call x2, Pallas kernels, gate_of(): call(functools.partial(gate_kernel, b, length), [((length, inner), BF16)]...  4.85 us
    ppermute x1, starting transfers between devices, on_device(): lax.ppermute(tail, 'seq', [(i, i + 1) for i in range(seq - 1)])  4.49 us
  transfers between devices with their start and end apart: 19, of which 11 were waited for; matrix products, arithmetic and copies ran while one was open for 0% of the time, Pallas kernels for 18%

profile of v6, /device:TPU:1, one launch (start us, length us, event | category | flops | bytes accessed | tf_op | source)
XLA Modules:
  0.0 88.3 jit_solution(2838557028200255316)
XLA Ops:
  0.0 0.9 %slice.3 = bf16[2,8,2560]{2,1,0:T(8,128)(2,1)S(1)} slice(bf16[2,512,2560]{2,1,0:T(8,128)(2,1)} %param.10), slice={[0:2], [504:512], [0:2560]} | slice | bytes 163840 | tf_op jit(solution)/shard_map/slice | solution.py:358
  0.9 4.5 %collective-permute-start = (bf16[2,8,2560]{2,1,0:T(8,128)(2,1)S(1)}, bf16[2,8,2560]{2,1,0:T(8,128)(2,1)S(1)}, u32[]{:S(2)}, u32[]{:S(2)}) collective-permute-start(bf16[2,8,2560]{2,1,0:T(8,128)(2,1)S(1)} %slice.3), channel_id=1, source_target_pairs={{0,8},{8,16},{16,24},{24,32},{32,40},{40,48},{48,56},{56,64},{64,7... | collective-permute-start | bytes 245768 | tf_op jit(solution)/shard_map/ppermute | solution.py:359
  5.5 2.5 %copy-done = bf16[2,512,2560]{2,1,0:T(8,128)(2,1)S(1)} copy-done((bf16[2,512,2560]{2,1,0:T(8,128)(2,1)S(1)}, bf16[2,512,2560]{2,1,0:T(8,128)(2,1)}, u32[]{:S(2)}) %copy-start) | copy-done | bytes 5242904
  7.9 0.9 %copy-done.3 = bf16[2560,32]{0,1:T(8,128)(2,1)S(1)} copy-done((bf16[2560,32]{0,1:T(8,128)(2,1)S(1)}, bf16[2560,32]{0,1:T(8,128)(2,1)}, u32[]{:S(2)}) %copy-start.3) | copy-done | bytes 163864
  8.8 0.9 %copy-done.4 = bf16[2560,10]{0,1:T(8,128)(2,1)S(1)} copy-done((bf16[2560,10]{0,1:T(8,128)(2,1)S(1)}, bf16[2560,10]{0,1:T(8,128)(2,1)}, u32[]{:S(2)}) %copy-start.4) | copy-done | bytes 51224
  9.7 1.6 %shard_map.100 = (bf16[32,1024]{1,0:T(8,128)(2,1)S(1)}, f32[1024,128]{1,0:T(8,128)S(1)}) custom-call(bf16[1024,2560]{1,0:T(8,128)(2,1)S(1)} %bitcast.9, bf16[32,2560]{1,0:T(8,128)(2,1)S(1)} %bitcast.19, bf16[10,2560]{1,0:T(8,128)(2,1)S(1)} %bitcast.21), custom_call_target="tpu_custom_call" | custom-call | flops 503316480 | tf_op jit(solution)/shard_map/pallas_call | solution.py:360
  11.4 0.1 pad_add_fusion.place
  11.5 0.2 shard_map.101.refs_0_
  11.7 5.6 %collective-permute-start.2 = (bf16[32,1152]{1,0:T(8,128)(2,1)S(1)}, bf16[32,1152]{1,0:T(8,128)(2,1)S(1)}, u32[]{:S(2)}, u32[]{:S(2)}) collective-permute-start(bf16[32,1152]{1,0:T(8,128)(2,1)S(1)} %shard_map.101.refs_0_), channel_id=1, source_target_pairs={{0,7},{1,0},{2,1},{3,2},{4,3},{5,4},{6,5},{7,6},{8,15},{9,8},{10,9... | collective-permute-start | bytes 221192 | tf_op jit(solution)/shard_map/ppermute | solution.py:400
  17.4 3.8 %shard_map.102 = (bf16[512,640]{1,0:T(8,128)(2,1)S(1)}, f32[512,128]{1,0:T(8,128)S(1)}, f32[8,640]{1,0:T(8,128)S(1)}, bf16[8,128]{1,0:T(8,128)(2,1)S(1)}) custom-call(f32[10]{0:T(128)S(1)} %copy-done.8, f32[10]{0:T(128)S(1)} %copy-done.9, bf16[1024,2560]{1,0:T(8,128)(2,1)S(1)} %bitcast.12, bf16[16,2560]{1,0:T(8,128)(2,1)S(1)} %bitcast.17, ...), custom_call_target="tpu_custom_call" | custom-call | flops 1677721600 | tf_op jit(solution)/shard_map/pallas_call | solution.py:375
  21.2 0.8 collective-permute-done.1.refs_1_
  22.0 2.7 %collective-permute-start.4 = (bf16[32,1152]{1,0:T(8,128)(2,1)S(1)}, bf16[32,1152]{1,0:T(8,128)(2,1)S(1)}, u32[]{:S(2)}, u32[]{:S(2)}) collective-permute-start(bf16[32,1152]{1,0:T(8,128)(2,1)S(1)} %collective-permute-done.2.refs_2_), channel_id=1, source_target_pairs={{0,7},{1,0},{2,1},{3,2},{4,3},{5,4},{6,5},{7,6},{8,15},{9,8},{10,9... | collective-permute-start | bytes 221192 | tf_op jit(solution)/shard_map/ppermute | solution.py:400
  24.7 3.8 %shard_map.103 = (bf16[512,640]{1,0:T(8,128)(2,1)S(1)}, f32[512,128]{1,0:T(8,128)S(1)}, f32[8,640]{1,0:T(8,128)S(1)}, bf16[8,128]{1,0:T(8,128)(2,1)S(1)}) custom-call(f32[10]{0:T(128)S(1)} %copy-done.8, f32[10]{0:T(128)S(1)} %copy-done.9, bf16[1024,2560]{1,0:T(8,128)(2,1)S(1)} %bitcast.13, bf16[16,2560]{1,0:T(8,128)(2,1)S(1)} %bitcast.18, ...), custom_call_target="tpu_custom_call" | custom-call | flops 1677721600 | tf_op jit(solution)/shard_map/pallas_call | solution.py:375
  28.5 0.1 collective-permute-start.5
  28.6 2.7 %collective-permute-start.6 = (bf16[32,1152]{1,0:T(8,128)(2,1)S(1)}, bf16[32,1152]{1,0:T(8,128)(2,1)S(1)}, u32[]{:S(2)}, u32[]{:S(2)}) collective-permute-start(bf16[32,1152]{1,0:T(8,128)(2,1)S(1)} %collective-permute-done.4.refs_4_), channel_id=1, source_target_pairs={{0,7},{1,0},{2,1},{3,2},{4,3},{5,4},{6,5},{7,6},{8,15},{9,8},{10,9... | collective-permute-start | bytes 221192 | tf_op jit(solution)/shard_map/ppermute | solution.py:400
  31.3 2.4 %shard_map.104.refs_0_ = bf16[512,640]{1,0:T(8,128)(2,1)S(1)} custom-call(bf16[1024,2560]{1,0:T(8,128)(2,1)S(1)} %bitcast.14, bf16[2560,640]{1,0:T(8,128)(2,1)S(1)} %copy-done.2, f32[512,128]{1,0:T(8,128)S(1)} %get-tuple-element.65.opening), custom_call_target="tpu_custom_call" | custom-call | flops 1677721600 | tf_op jit(solution)/shard_map/pallas_call | solution.py:390
  33.7 0.1 collective-permute-start.7
  33.8 2.4 %shard_map.105.refs_1_ = bf16[512,640]{1,0:T(8,128)(2,1)S(1)} custom-call(bf16[1024,2560]{1,0:T(8,128)(2,1)S(1)} %bitcast.15, bf16[2560,640]{1,0:T(8,128)(2,1)S(1)} %copy-done.2, f32[512,128]{1,0:T(8,128)S(1)} %get-tuple-element.69.opening), custom_call_target="tpu_custom_call" | custom-call | flops 1677721600 | tf_op jit(solution)/shard_map/pallas_call | solution.py:390
  36.3 2.0 %collective-permute-done.7.refs_7_ = bf16[32,1152]{1,0:T(8,128)(2,1)S(1)} collective-permute-done((bf16[32,1152]{1,0:T(8,128)(2,1)S(1)}, bf16[32,1152]{1,0:T(8,128)(2,1)S(1)}, u32[]{:S(2)}, u32[]{:S(2)}) %collective-permute-start.7) | collective-permute-done | bytes 73760 | tf_op jit(solution)/shard_map/ppermute | solution.py:401
  38.2 2.9 %shard_map.106 = (bf16[2,128,512]{2,1,0:T(8,128)(2,1)S(1)}, bf16[1024,128]{1,0:T(8,128)(2,1)S(1)}, bf16[8,128,640]{2,1,0:T(8,128)(2,1)S(1)}, bf16[16,8,768]{2,1,0:T(8,128)(2,1)S(1)}, bf16[16,8,768]{2,1,0:T(8,128)(2,1)S(1)}) custom-call(s32[4]{0:T(128)S(1)} %pad_add_fusion.place, f32[4,256]{1,0:T(4,128)S(1)} %copy-done.6, ...), custom_call_target="tpu_custom_call" | custom-call | tf_op jit(solution)/shard_map/pallas_call | solution.py:423
  41.1 2.5 %collective-permute-start.8 = (bf16[16,8,768]{2,1,0:T(8,128)(2,1)S(1)}, bf16[16,8,768]{2,1,0:T(8,128)(2,1)S(1)}, u32[]{:S(2)}, u32[]{:S(2)}) collective-permute-start(bf16[16,8,768]{2,1,0:T(8,128)(2,1)S(1)} %get-tuple-element.78), channel_id=1, source_target_pairs={{0,8},{8,0},{16,24},{24,16},{32,40},{40,32},{48,56},{56,48},{64,72... | collective-permute-start | bytes 589832 | tf_op jit(solution)/shard_map/ppermute | solution.py:438
  43.6 1.1 %collective-permute-done.8.got = bf16[16,8,768]{2,1,0:T(8,128)(2,1)S(1)} collective-permute-done((bf16[16,8,768]{2,1,0:T(8,128)(2,1)S(1)}, bf16[16,8,768]{2,1,0:T(8,128)(2,1)S(1)}, u32[]{:S(2)}, u32[]{:S(2)}) %collective-permute-start.8) | collective-permute-done | bytes 196640 | tf_op jit(solution)/shard_map/ppermute | solution.py:438
  44.7 0.7 shard_map.107
  45.5 1.6 %collective-permute-start.9 = (bf16[4,8,768]{2,1,0:T(8,128)(2,1)S(1)}, bf16[4,8,768]{2,1,0:T(8,128)(2,1)S(1)}, u32[]{:S(2)}, u32[]{:S(2)}) collective-permute-start(bf16[4,8,768]{2,1,0:T(8,128)(2,1)S(1)} %get-tuple-element.80), channel_id=1, source_target_pairs={{0,16},{8,24},{16,32},{24,40},{32,48},{40,56},{48,0},{56,8},{64,80... | collective-permute-start | bytes 147464 | tf_op jit(solution)/shard_map/ppermute | solution.py:443
  47.1 2.4 %collective-permute-start.10 = (bf16[4,8,768]{2,1,0:T(8,128)(2,1)S(1)}, bf16[4,8,768]{2,1,0:T(8,128)(2,1)S(1)}, u32[]{:S(2)}, u32[]{:S(2)}) collective-permute-start(bf16[4,8,768]{2,1,0:T(8,128)(2,1)S(1)} %get-tuple-element.81), channel_id=1, source_target_pairs={{0,32},{8,40},{16,48},{24,56},{32,0},{40,8},{48,16},{56,24},{64,96... | collective-permute-start | bytes 147464 | tf_op jit(solution)/shard_map/ppermute | solution.py:443
  49.5 1.5 %collective-permute-start.11 = (bf16[4,8,768]{2,1,0:T(8,128)(2,1)S(1)}, bf16[4,8,768]{2,1,0:T(8,128)(2,1)S(1)}, u32[]{:S(2)}, u32[]{:S(2)}) collective-permute-start(bf16[4,8,768]{2,1,0:T(8,128)(2,1)S(1)} %get-tuple-element.82), channel_id=1, source_target_pairs={{0,48},{8,56},{16,0},{24,8},{32,16},{40,24},{48,32},{56,40},{64,11... | collective-permute-start | bytes 147464 | tf_op jit(solution)/shard_map/ppermute | solution.py:443
  51.0 0.8 collective-permute-done.10.refs_2_
  51.8 1.0 %collective-permute-done.11.refs_3_ = bf16[4,8,768]{2,1,0:T(8,128)(2,1)S(1)} collective-permute-done((bf16[4,8,768]{2,1,0:T(8,128)(2,1)S(1)}, bf16[4,8,768]{2,1,0:T(8,128)(2,1)S(1)}, u32[]{:S(2)}, u32[]{:S(2)}) %collective-permute-start.11) | collective-permute-done | bytes 49184 | tf_op jit(solution)/shard_map/ppermute | solution.py:443
  52.8 0.7 shard_map.108
  53.5 2.6 %collective-permute-start.14 = (bf16[4,8,768]{2,1,0:T(8,128)(2,1)S(1)}, bf16[4,8,768]{2,1,0:T(8,128)(2,1)S(1)}, u32[]{:S(2)}, u32[]{:S(2)}) collective-permute-start(bf16[4,8,768]{2,1,0:T(8,128)(2,1)S(1)} %get-tuple-element.87), channel_id=1, source_target_pairs={{0,192},{8,200},{16,208},{24,216},{32,224},{40,232},{48,240},{56,2... | collective-permute-start | bytes 147464 | tf_op jit(solution)/shard_map/ppermute | solution.py:443
  56.1 0.8 collective-permute-start.13
  56.9 0.8 collective-permute-start.12
  57.7 1.5 %shard_map.109.within = f32[1024,640]{1,0:T(8,128)S(1)} custom-call(bf16[2,128,512]{2,1,0:T(8,128)(2,1)S(1)} %get-tuple-element.88.b_rows, bf16[1024,128]{1,0:T(8,128)(2,1)S(1)} %get-tuple-element.89.c_rows, bf16[8,128,640]{2,1,0:T(8,128)(2,1)S(1)} %get-tuple-element.90.starts, bf16[512,640]{1,0:T(8,128)(2,1)S(1)} %get-tuple-element.71.refs_8_.refs_0_, ...), custom_call_target="tpu_custom_call" | custom-call | flops 419430400 | tf_op jit(solution)/shard_map/pallas_call | solution.py:469
  59.2 1.4 %collective-permute-done.13.refs_1_ = bf16[4,8,768]{2,1,0:T(8,128)(2,1)S(1)} collective-permute-done((bf16[4,8,768]{2,1,0:T(8,128)(2,1)S(1)}, bf16[4,8,768]{2,1,0:T(8,128)(2,1)S(1)}, u32[]{:S(2)}, u32[]{:S(2)}) %collective-permute-start.13) | collective-permute-done | bytes 49184 | tf_op jit(solution)/shard_map/ppermute | solution.py:443
  60.5 0.5 collective-permute-done.12.refs_0_
  61.1 0.8 shard_map.110
  61.9 0.6 collective-permute-start.15
  62.4 3.3 %collective-permute-start.16 = (bf16[4,8,640]{2,1,0:T(8,128)(2,1)S(1)}, bf16[4,8,640]{2,1,0:T(8,128)(2,1)S(1)}, u32[]{:S(2)}, u32[]{:S(2)}) collective-permute-start(bf16[4,8,640]{2,1,0:T(8,128)(2,1)S(1)} %get-tuple-element.96), channel_id=1, source_target_pairs={{0,32},{8,40},{16,48},{24,56},{32,0},{40,8},{48,16},{56,24},{64,96... | collective-permute-start | bytes 122888 | tf_op jit(solution)/shard_map/ppermute | solution.py:443
  65.7 0.0 collective-permute-start.17
  65.7 0.3 collective-permute-done.15.refs_1_
  66.0 1.5 %collective-permute-done.16.refs_2_ = bf16[4,8,640]{2,1,0:T(8,128)(2,1)S(1)} collective-permute-done((bf16[4,8,640]{2,1,0:T(8,128)(2,1)S(1)}, bf16[4,8,640]{2,1,0:T(8,128)(2,1)S(1)}, u32[]{:S(2)}, u32[]{:S(2)}) %collective-permute-start.16) | collective-permute-done | bytes 40992 | tf_op jit(solution)/shard_map/ppermute | solution.py:443
  67.5 1.0 %collective-permute-done.17.refs_3_ = bf16[4,8,640]{2,1,0:T(8,128)(2,1)S(1)} collective-permute-done((bf16[4,8,640]{2,1,0:T(8,128)(2,1)S(1)}, bf16[4,8,640]{2,1,0:T(8,128)(2,1)S(1)}, u32[]{:S(2)}, u32[]{:S(2)}) %collective-permute-start.17) | collective-permute-done | bytes 40992 | tf_op jit(solution)/shard_map/ppermute | solution.py:443
  68.6 0.8 shard_map.111
  69.3 5.3 %collective-permute-start.18 = (bf16[128,640]{1,0:T(8,128)(2,1)S(1)}, bf16[128,640]{1,0:T(8,128)(2,1)S(1)}, u32[]{:S(2)}, u32[]{:S(2)}) collective-permute-start(bf16[128,640]{1,0:T(8,128)(2,1)S(1)} %get-tuple-element.99), channel_id=1, source_target_pairs={{0,8},{8,0},{16,24},{24,16},{32,40},{40,32},{48,56},{56,48},{64,72... | collective-permute-start | bytes 491528 | tf_op jit(solution)/shard_map/ppermute | solution.py:438
  74.6 1.0 %collective-permute-done.18.taken = bf16[128,640]{1,0:T(8,128)(2,1)S(1)} collective-permute-done((bf16[128,640]{1,0:T(8,128)(2,1)S(1)}, bf16[128,640]{1,0:T(8,128)(2,1)S(1)}, u32[]{:S(2)}, u32[]{:S(2)}) %collective-permute-start.18) | collective-permute-done | bytes 163872 | tf_op jit(solution)/shard_map/ppermute | solution.py:438
  75.7 1.9 %shard_map.112 = (f32[1024,640]{1,0:T(8,128)S(1)}, f32[8,8,128]{2,1,0:T(8,128)S(1)}) custom-call(s32[4]{0:T(128)S(1)} %pad_add_fusion.place, bf16[128,640]{1,0:T(8,128)(2,1)S(1)} %get-tuple-element.98.own, bf16[128,640]{1,0:T(8,128)(2,1)S(1)} %collective-permute-done.18.taken, f32[1024,640]{1,0:T(8,128)S(1)} %shard_map.109.within, ...), custom_call_target="tpu_custom_call" | custom-call | tf_op jit(solution)/shard_map/pallas_call | solution.py:489
  77.5 9.3 %all_to_all.5.squares = f32[8,8,128]{2,1,0:T(8,128)S(1)} all-to-all(f32[8,8,128]{2,1,0:T(8,128)S(1)} %get-tuple-element.104), channel_id=1, replica_groups=mesh['seq'=32,'tp'=8] {'tp'}, dimensions={0} | all-to-all | bytes 65536 | tf_op jit(solution)/shard_map/all_to_all | solution.py:496
  86.8 1.5 %shard_map.113 = bf16[1024,640]{1,0:T(8,128)(2,1)} custom-call(f32[1024,640]{1,0:T(8,128)S(1)} %get-tuple-element.103.gated, f32[8,8,128]{2,1,0:T(8,128)S(1)} %all_to_all.5.squares, f32[640]{0:T(1024)S(1)} %copy-done.7), custom_call_target="tpu_custom_call" | custom-call | tf_op jit(solution)/shard_map/pallas_call | solution.py:497
  (32 shorter events, 0.1 us)
Async XLA Ops:
  0.9 10.6 %collective-permute-start = (bf16[2,8,2560]{2,1,0:T(8,128)(2,1)S(1)}, bf16[2,8,2560]{2,1,0:T(8,128)(2,1)S(1)}, u32[]{:S(2)}, u32[]{:S(2)}) collective-permute-start(bf16[2,8,2560]{2,1,0:T(8,128)(2,1)S(1)} %slice.3), channel_id=1, source_target_pairs={{0,8},{8,16},{16,24},{24,32},{32,40},{40,48},{48,56},{56,64},{64,7... | collective-permute-start | bytes 245768 | tf_op jit(solution)/shard_map/ppermute | solution.py:359
  5.4 2.5 %copy-start = (bf16[2,512,2560]{2,1,0:T(8,128)(2,1)S(1)}, bf16[2,512,2560]{2,1,0:T(8,128)(2,1)}, u32[]{:S(2)}) copy-start(bf16[2,512,2560]{2,1,0:T(8,128)(2,1)} %param.10) | copy-start | bytes 15728644
  7.9 0.9 %copy-start.3 = (bf16[2560,32]{0,1:T(8,128)(2,1)S(1)}, bf16[2560,32]{0,1:T(8,128)(2,1)}, u32[]{:S(2)}) copy-start(bf16[2560,32]{0,1:T(8,128)(2,1)} %param.13) | copy-start | bytes 491524
  8.8 0.9 %copy-start.4 = (bf16[2560,10]{0,1:T(8,128)(2,1)S(1)}, bf16[2560,10]{0,1:T(8,128)(2,1)}, u32[]{:S(2)}) copy-start(bf16[2560,10]{0,1:T(8,128)(2,1)} %param.14) | copy-start | bytes 153604
  9.7 7.6 %slice-start = ((s8[5242880]{0:T(1024)(128)(4,1)}), s8[4194304]{0:T(1024)(128)(4,1)S(1)}, s32[]{:S(2)}) async-start(s8[5242880]{0:T(1024)(128)(4,1)} %bitcast.10), calls=%async_computation.1 | async-start | bytes 8388608
  11.4 5.9 %slice-start.1 = ((s8[5242880]{0:T(1024)(128)(4,1)}), s8[1048576]{0:T(1024)(128)(4,1)S(1)}, s32[]{:S(2)}) async-start(s8[5242880]{0:T(1024)(128)(4,1)} %bitcast.10), calls=%async_computation.2 | async-start | bytes 2097152
  11.4 5.9 %copy-start.1 = (bf16[2560,640]{1,0:T(8,128)(2,1)S(1)}, bf16[2560,640]{1,0:T(8,128)(2,1)}, u32[]{:S(2)}) copy-start(bf16[2560,640]{1,0:T(8,128)(2,1)} %weight.5) | copy-start | bytes 9830404
  11.5 5.9 %copy-start.5 = (f32[4,640]{1,0:T(4,128)S(1)}, f32[4,640]{1,0:T(4,128)}, u32[]{:S(2)}) copy-start(f32[4,640]{1,0:T(4,128)} %taps.4) | copy-start | bytes 30724
  11.5 5.9 %copy-start.8 = (f32[10]{0:T(128)S(1)}, f32[10]{0:T(128)}, u32[]{:S(2)}) copy-start(f32[10]{0:T(128)} %step_bias.3) | copy-start | bytes 124
  11.5 5.9 %copy-start.9 = (f32[10]{0:T(128)S(1)}, f32[10]{0:T(128)}, u32[]{:S(2)}) copy-start(f32[10]{0:T(128)} %log_rate.3) | copy-start | bytes 124
  11.7 9.5 %collective-permute-start.2 = (bf16[32,1152]{1,0:T(8,128)(2,1)S(1)}, bf16[32,1152]{1,0:T(8,128)(2,1)S(1)}, u32[]{:S(2)}, u32[]{:S(2)}) collective-permute-start(bf16[32,1152]{1,0:T(8,128)(2,1)S(1)} %shard_map.101.refs_0_), channel_id=1, source_target_pairs={{0,7},{1,0},{2,1},{3,2},{4,3},{5,4},{6,5},{7,6},{8,15},{9,8},{10,9... | collective-permute-start | bytes 221192 | tf_op jit(solution)/shard_map/ppermute | solution.py:400
  17.3 4.7 %collective-permute-start.1 = (bf16[32,1152]{1,0:T(8,128)(2,1)S(1)}, bf16[32,1152]{1,0:T(8,128)(2,1)S(1)}, u32[]{:S(2)}, u32[]{:S(2)}) collective-permute-start(bf16[32,1152]{1,0:T(8,128)(2,1)S(1)} %shard_map.101.refs_0_), channel_id=1, source_target_pairs={{0,1},{1,2},{2,3},{3,4},{4,5},{5,6},{6,7},{7,0},{8,9},{9,10},{10,1... | collective-permute-start | bytes 221192 | tf_op jit(solution)/shard_map/ppermute | solution.py:401
  22.0 9.2 %copy-start.2 = (bf16[2560,640]{1,0:T(8,128)(2,1)S(1)}, bf16[2560,640]{1,0:T(8,128)(2,1)}, u32[]{:S(2)}) copy-start(bf16[2560,640]{1,0:T(8,128)(2,1)} %weight.7) | copy-start | bytes 9830404
  22.0 6.5 %collective-permute-start.3 = (bf16[32,1152]{1,0:T(8,128)(2,1)S(1)}, bf16[32,1152]{1,0:T(8,128)(2,1)S(1)}, u32[]{:S(2)}, u32[]{:S(2)}) collective-permute-start(bf16[32,1152]{1,0:T(8,128)(2,1)S(1)} %collective-permute-done.1.refs_1_), channel_id=1, source_target_pairs={{0,1},{1,2},{2,3},{3,4},{4,5},{5,6},{6,7},{7,0},{8,9},{9,10},{10,1... | collective-permute-start | bytes 221192 | tf_op jit(solution)/shard_map/ppermute | solution.py:401
  22.0 6.5 %collective-permute-start.4 = (bf16[32,1152]{1,0:T(8,128)(2,1)S(1)}, bf16[32,1152]{1,0:T(8,128)(2,1)S(1)}, u32[]{:S(2)}, u32[]{:S(2)}) collective-permute-start(bf16[32,1152]{1,0:T(8,128)(2,1)S(1)} %collective-permute-done.2.refs_2_), channel_id=1, source_target_pairs={{0,7},{1,0},{2,1},{3,2},{4,3},{5,4},{6,5},{7,6},{8,15},{9,8},{10,9... | collective-permute-start | bytes 221192 | tf_op jit(solution)/shard_map/ppermute | solution.py:400
  28.5 5.2 %collective-permute-start.5 = (bf16[32,1152]{1,0:T(8,128)(2,1)S(1)}, bf16[32,1152]{1,0:T(8,128)(2,1)S(1)}, u32[]{:S(2)}, u32[]{:S(2)}) collective-permute-start(bf16[32,1152]{1,0:T(8,128)(2,1)S(1)} %collective-permute-done.3.refs_3_), channel_id=1, source_target_pairs={{0,1},{1,2},{2,3},{3,4},{4,5},{5,6},{6,7},{7,0},{8,9},{9,10},{10,1... | collective-permute-start | bytes 221192 | tf_op jit(solution)/shard_map/ppermute | solution.py:401
  28.6 5.1 %collective-permute-start.6 = (bf16[32,1152]{1,0:T(8,128)(2,1)S(1)}, bf16[32,1152]{1,0:T(8,128)(2,1)S(1)}, u32[]{:S(2)}, u32[]{:S(2)}) collective-permute-start(bf16[32,1152]{1,0:T(8,128)(2,1)S(1)} %collective-permute-done.4.refs_4_), channel_id=1, source_target_pairs={{0,7},{1,0},{2,1},{3,2},{4,3},{5,4},{6,5},{7,6},{8,15},{9,8},{10,9... | collective-permute-start | bytes 221192 | tf_op jit(solution)/shard_map/ppermute | solution.py:400
  33.7 4.5 %collective-permute-start.7 = (bf16[32,1152]{1,0:T(8,128)(2,1)S(1)}, bf16[32,1152]{1,0:T(8,128)(2,1)S(1)}, u32[]{:S(2)}, u32[]{:S(2)}) collective-permute-start(bf16[32,1152]{1,0:T(8,128)(2,1)S(1)} %collective-permute-done.5.refs_5_), channel_id=1, source_target_pairs={{0,1},{1,2},{2,3},{3,4},{4,5},{5,6},{6,7},{7,0},{8,9},{9,10},{10,1... | collective-permute-start | bytes 221192 | tf_op jit(solution)/shard_map/ppermute | solution.py:401
  33.8 4.4 %copy-start.6 = (f32[4,256]{1,0:T(4,128)S(1)}, f32[4,256]{1,0:T(4,128)}, u32[]{:S(2)}) copy-start(f32[4,256]{1,0:T(4,128)} %taps.5) | copy-start | bytes 12292
  41.1 3.6 %collective-permute-start.8 = (bf16[16,8,768]{2,1,0:T(8,128)(2,1)S(1)}, bf16[16,8,768]{2,1,0:T(8,128)(2,1)S(1)}, u32[]{:S(2)}, u32[]{:S(2)}) collective-permute-start(bf16[16,8,768]{2,1,0:T(8,128)(2,1)S(1)} %get-tuple-element.78), channel_id=1, source_target_pairs={{0,8},{8,0},{16,24},{24,16},{32,40},{40,32},{48,56},{56,48},{64,72... | collective-permute-start | bytes 589832 | tf_op jit(solution)/shard_map/ppermute | solution.py:438
  45.5 5.6 %collective-permute-start.9 = (bf16[4,8,768]{2,1,0:T(8,128)(2,1)S(1)}, bf16[4,8,768]{2,1,0:T(8,128)(2,1)S(1)}, u32[]{:S(2)}, u32[]{:S(2)}) collective-permute-start(bf16[4,8,768]{2,1,0:T(8,128)(2,1)S(1)} %get-tuple-element.80), channel_id=1, source_target_pairs={{0,16},{8,24},{16,32},{24,40},{32,48},{40,56},{48,0},{56,8},{64,80... | collective-permute-start | bytes 147464 | tf_op jit(solution)/shard_map/ppermute | solution.py:443
  47.1 4.7 %collective-permute-start.10 = (bf16[4,8,768]{2,1,0:T(8,128)(2,1)S(1)}, bf16[4,8,768]{2,1,0:T(8,128)(2,1)S(1)}, u32[]{:S(2)}, u32[]{:S(2)}) collective-permute-start(bf16[4,8,768]{2,1,0:T(8,128)(2,1)S(1)} %get-tuple-element.81), channel_id=1, source_target_pairs={{0,32},{8,40},{16,48},{24,56},{32,0},{40,8},{48,16},{56,24},{64,96... | collective-permute-start | bytes 147464 | tf_op jit(solution)/shard_map/ppermute | solution.py:443
  49.5 3.2 %collective-permute-start.11 = (bf16[4,8,768]{2,1,0:T(8,128)(2,1)S(1)}, bf16[4,8,768]{2,1,0:T(8,128)(2,1)S(1)}, u32[]{:S(2)}, u32[]{:S(2)}) collective-permute-start(bf16[4,8,768]{2,1,0:T(8,128)(2,1)S(1)} %get-tuple-element.82), channel_id=1, source_target_pairs={{0,48},{8,56},{16,0},{24,8},{32,16},{40,24},{48,32},{56,40},{64,11... | collective-permute-start | bytes 147464 | tf_op jit(solution)/shard_map/ppermute | solution.py:443
  53.5 5.6 %collective-permute-start.14 = (bf16[4,8,768]{2,1,0:T(8,128)(2,1)S(1)}, bf16[4,8,768]{2,1,0:T(8,128)(2,1)S(1)}, u32[]{:S(2)}, u32[]{:S(2)}) collective-permute-start(bf16[4,8,768]{2,1,0:T(8,128)(2,1)S(1)} %get-tuple-element.87), channel_id=1, source_target_pairs={{0,192},{8,200},{16,208},{24,216},{32,224},{40,232},{48,240},{56,2... | collective-permute-start | bytes 147464 | tf_op jit(solution)/shard_map/ppermute | solution.py:443
  56.1 4.4 %collective-permute-start.13 = (bf16[4,8,768]{2,1,0:T(8,128)(2,1)S(1)}, bf16[4,8,768]{2,1,0:T(8,128)(2,1)S(1)}, u32[]{:S(2)}, u32[]{:S(2)}) collective-permute-start(bf16[4,8,768]{2,1,0:T(8,128)(2,1)S(1)} %get-tuple-element.87), channel_id=1, source_target_pairs={{0,128},{8,136},{16,144},{24,152},{32,160},{40,168},{48,176},{56,1... | collective-permute-start | bytes 147464 | tf_op jit(solution)/shard_map/ppermute | solution.py:443
  56.9 4.2 %collective-permute-start.12 = (bf16[4,8,768]{2,1,0:T(8,128)(2,1)S(1)}, bf16[4,8,768]{2,1,0:T(8,128)(2,1)S(1)}, u32[]{:S(2)}, u32[]{:S(2)}) collective-permute-start(bf16[4,8,768]{2,1,0:T(8,128)(2,1)S(1)} %get-tuple-element.87), channel_id=1, source_target_pairs={{0,64},{8,72},{16,80},{24,88},{32,96},{40,104},{48,112},{56,120},{... | collective-permute-start | bytes 147464 | tf_op jit(solution)/shard_map/ppermute | solution.py:443
  61.8 25.0 %copy-start.7 = (f32[640]{0:T(1024)S(1)}, f32[640]{0:T(1024)}, u32[]{:S(2)}) copy-start(f32[640]{0:T(1024)} %gain.1) | copy-start | bytes 7684
  61.9 4.1 %collective-permute-start.15 = (bf16[4,8,640]{2,1,0:T(8,128)(2,1)S(1)}, bf16[4,8,640]{2,1,0:T(8,128)(2,1)S(1)}, u32[]{:S(2)}, u32[]{:S(2)}) collective-permute-start(bf16[4,8,640]{2,1,0:T(8,128)(2,1)S(1)} %get-tuple-element.95), channel_id=1, source_target_pairs={{0,16},{8,24},{16,32},{24,40},{32,48},{40,56},{48,0},{56,8},{64,80... | collective-permute-start | bytes 122888 | tf_op jit(solution)/shard_map/ppermute | solution.py:443
  62.4 5.1 %collective-permute-start.16 = (bf16[4,8,640]{2,1,0:T(8,128)(2,1)S(1)}, bf16[4,8,640]{2,1,0:T(8,128)(2,1)S(1)}, u32[]{:S(2)}, u32[]{:S(2)}) collective-permute-start(bf16[4,8,640]{2,1,0:T(8,128)(2,1)S(1)} %get-tuple-element.96), channel_id=1, source_target_pairs={{0,32},{8,40},{16,48},{24,56},{32,0},{40,8},{48,16},{56,24},{64,96... | collective-permute-start | bytes 122888 | tf_op jit(solution)/shard_map/ppermute | solution.py:443
  65.7 2.9 %collective-permute-start.17 = (bf16[4,8,640]{2,1,0:T(8,128)(2,1)S(1)}, bf16[4,8,640]{2,1,0:T(8,128)(2,1)S(1)}, u32[]{:S(2)}, u32[]{:S(2)}) collective-permute-start(bf16[4,8,640]{2,1,0:T(8,128)(2,1)S(1)} %get-tuple-element.97), channel_id=1, source_target_pairs={{0,48},{8,56},{16,0},{24,8},{32,16},{40,24},{48,32},{56,40},{64,11... | collective-permute-start | bytes 122888 | tf_op jit(solution)/shard_map/ppermute | solution.py:443
  69.3 6.3 %collective-permute-start.18 = (bf16[128,640]{1,0:T(8,128)(2,1)S(1)}, bf16[128,640]{1,0:T(8,128)(2,1)S(1)}, u32[]{:S(2)}, u32[]{:S(2)}) collective-permute-start(bf16[128,640]{1,0:T(8,128)(2,1)S(1)} %get-tuple-element.99), channel_id=1, source_target_pairs={{0,8},{8,0},{16,24},{24,16},{32,40},{40,32},{48,56},{56,48},{64,72... | collective-permute-start | bytes 491528 | tf_op jit(solution)/shard_map/ppermute | solution.py:438

commit v7 on v6

--- a/solution.py
+++ b/solution.py
@@ -54,21 +54,24 @@
     return dot(jnp.concatenate([high, middle], axis=1), spread)
 
 
-def bc_kernel(chunk, hidden, weight, step_weight, out, steps, pad, joined):
-    share = weight.shape[0]
+def prepare_kernel(weight, step_weight, joined):
     joined[...] = jnp.zeros_like(joined)
     joined[: step_weight.shape[0], :] = step_weight[...]
-    joined[16 : 16 + share, :] = weight[...]
+    joined[16:, :] = weight[...]
+
+
+def bc_kernel(chunk, hidden, joined, out, steps, pad):
+    both = joined.shape[0]
     pad[...] = jnp.zeros_like(pad)
     for r in range(0, hidden.shape[0], chunk):
-        pad[:, : 16 + share] = dot_nt(hidden[r : r + chunk, :], joined[...])
+        pad[:, :both] = dot_nt(hidden[r : r + chunk, :], joined[...])
         steps[r : r + chunk, :] = pad[...]
-        out[:, r : r + chunk] = jnp.transpose(pad[...])[16 : 16 + share].astype(BF16)
+        out[:, r : r + chunk] = jnp.transpose(pad[...])[16:both].astype(BF16)
 
 
 def join_kernel(batch, halo, weight, own, out, pad):
-    share = weight.shape[0]
-    before = dot_nt(halo[...], weight[...])
+    share = out.shape[0]
+    before = dot_nt(halo[...], weight[16:, :])
     pad[...] = jnp.zeros_like(pad)
     for b in range(batch):
         pad[LANES - 8 - 64 * b : LANES - 64 * b, :share] = before[8 * b : 8 * b + 8]
@@ -152,6 +155,7 @@
             for t in range(CONV - 1):
                 total = total + tap[:, t : t + 1] * pltpu.roll(padded, CONV - 1 - t, 1)[:, LANES:]
             mixed[pl.ds(first, share), b * length : (b + 1) * length] = silu(total)
+    ended = []
     for b in range(batch):
         own = slice(b * length, (b + 1) * length)
         b_t = mixed[:STATE, own].astype(BF16)
@@ -164,14 +168,14 @@
             starts[b * blocks + k] = ready.astype(BF16)
             at = slice(k * BLOCK, (k + 1) * BLOCK)
             state = half * (ready + dot(b_t[:, at], scaled[b][at, :]))
-
-        def keep(target, state=state, b=b):
-            for g in range(STATE // 8):
-                target[g, :, :inner] = state[8 * g : 8 * g + 8].astype(BF16)
-                target[g, :, inner:] = decays[b][...]
-
-        pl.when(place[1] == b)(functools.partial(keep, mine))
-        pl.when(place[1] != b)(functools.partial(keep, other))
+        ended.append(state)
+    first = place[1] == 0
+    for target, (a, b) in ((mine, (0, 1)), (other, (1, 0))):
+        log = jnp.where(first, decays[a][...].astype(F32), decays[b][...].astype(F32)).astype(BF16)
+        for g in range(STATE // 8):
+            at = slice(8 * g, 8 * g + 8)
+            target[g, :, :inner] = jnp.where(first, ended[a][at], ended[b][at]).astype(BF16)
+            target[g, :, inner:] = log
 
 
 def log_decay(state):
@@ -355,20 +359,24 @@
     at = lax.axis_index("seq")
     place = jnp.stack([lax.axis_index("tp"), at % 2, at // 2 % WAYS, at // (2 * WAYS)])
     smem = pl.BlockSpec(memory_space=pltpu.SMEM)
+    joined = call(
+        prepare_kernel, [((16 + share, width), BF16)], flops=20 * tokens * width * share
+    )(weight, step_weight)
     tail = hidden_in[:, length - 8 :, :]
+    tail, joined, place = lax.optimization_barrier((tail, joined, place))
     halo = lax.ppermute(tail, "seq", [(i, i + 1) for i in range(seq - 1)]).reshape(8 * batch, width)
     own, step_pre = call(
         functools.partial(bc_kernel, 256),
         [((share, tokens), BF16), ((tokens, LANES), F32)],
-        scratch=[((256, LANES), F32), ((16 + share, width), BF16)],
+        scratch=[((256, LANES), F32)],
         flops=6 * tokens * width * share,
-    )(hidden, weight, step_weight)
+    )(hidden, joined)
     shard = call(
         functools.partial(join_kernel, batch),
         [((share, tokens + LANES), BF16)],
         scratch=[((LANES, LANES), F32)],
         flops=30 * tokens * width * share,
-    )(halo, weight, own)
+    )(halo, joined, own)
     work = 2 * length * width * inner
 
     def value_of(b, hidden):
@@ -404,14 +412,10 @@
             for where, part in zip((scaled, openings, rows, decays), one):
                 where.append(part)
             mark = one[3]
-        elif r < 2 * batch:
-            mark = gate_of(r - batch, hidden, openings[r - batch])
-            opened.append(mark)
-        left, right, hidden, mark = lax.optimization_barrier((to_right, to_left, hidden, mark))
-        if r < batch:
+            left, right, hidden, mark = lax.optimization_barrier((to_right, to_left, hidden, mark))
             decays[-1] = mark
         else:
-            opened[-1] = mark
+            left, right = to_right, to_left
         shards.append(left)
         places.append(tp - r - 1)
         if 2 * r + 2 < tp:
@@ -448,6 +452,9 @@
         moved = {d: along(parts[d], d, stride) for d in order}
         return [moved[d] for d in range(1, WAYS)]
 
+    def tie(x, after):
+        return lax.optimization_barrier((x, after))[0]
+
     got = to_core(other)
     leaving = call(
         chip_kernel,
@@ -457,6 +464,8 @@
         scratch=[(full, BF16)],
     )(place, mine, got)
     parts = hop(leaving, 2)
+    opened.append(gate_of(0, hidden, tie(openings[0], leaving[0])))
+    *parts, opened[0] = lax.optimization_barrier((*parts, opened[0]))
     row, before, logs = call(
         row_kernel,
         [(part, BF16), ((WAYS, quarter, 8, inner), F32), ((8, LANES), F32)],
@@ -478,6 +487,8 @@
         scratch=[((WAYS, quarter, 8, inner), BF16)],
     )(place, before, logs, *others)
     parts = hop(leaving, 2)
+    opened.append(gate_of(1, hidden, tie(openings[1], leaving[0])))
+    *parts, opened[1] = lax.optimization_barrier((*parts, opened[1]))
     own, give = call(
         arrive_kernel,
         [((STATE, inner), BF16)] * 2,

time: 88.6 us -> 88 us (level)
  local copies, waits for them, and re-layouts: 5.22 us -> 2.74 us
  starting transfers between devices: 37 us -> 38.6 us
    ppermute x4, waiting for transfers between devices: 2.78 us -> 7.51 us  [on_device(): to_right = lax.ppermute(left, 'tp', up)]
    ppermute x9, waiting for transfers between devices: 6.52 us -> 2.45 us  [along(): return lax.ppermute(x, 'seq', pairs)]
    unnamed x24 -> x20, local copies, waits for them, and re-layouts: 4.33 us -> 1.84 us
    ppermute x9, starting transfers between devices: 13.6 us -> 14.8 us  [along(): return lax.ppermute(x, 'seq', pairs)]
  transfers between devices with their start and end apart: 19 -> 19, of which waited for: 11 -> 7; matrix products, arithmetic and copies ran while one was open for 0% -> 0% of each run, Pallas kernels for 18% -> 18%
where the time goes in v7:
time: 88 us; the launch traced here: 87.8 us
  starting transfers between devices  38.6 us (44%)
  Pallas kernels  24.8 us (28%)
  waiting for transfers between devices  12.1 us (14%)
  blocking collectives  9.3 us (11%)
  local copies, waits for them, and re-layouts  2.74 us (3%)
    ppermute x9, starting transfers between devices, along(): return lax.ppermute(x, 'seq', pairs)  14.8 us
    ppermute x3, starting transfers between devices, on_device(): to_left = lax.ppermute(right, 'tp', down) if 2 * r + 2 < tp else right  11 us
    all_to_all x1, blocking collectives, on_device(): whole = lax.all_to_all(squares, 'tp', 0, 0, tiled=True)  9.3 us
    ppermute x2, starting transfers between devices, to_core(): return lax.ppermute(x, 'seq', [(i, i ^ 1) for i in range(seq)])  7.9 us
    pallas_call x2, Pallas kernels, value_of(): call(functools.partial(value_kernel, b, length, heads), [((length, inner)...  7.58 us
    ppermute x4, waiting for transfers between devices, on_device(): to_right = lax.ppermute(left, 'tp', up)  7.51 us
    pallas_call x2, Pallas kernels, gate_of(): call(functools.partial(gate_kernel, b, length), [((length, inner), BF16)]...  4.86 us
    ppermute x1, starting transfers between devices, on_device(): lax.ppermute(tail, 'seq', [(i, i + 1) for i in range(seq - 1)])  4.76 us
  transfers between devices with their start and end apart: 19, of which 7 were waited for; matrix products, arithmetic and copies ran while one was open for 0% of the time, Pallas kernels for 18%

profile of v7, /device:TPU:1, one launch (start us, length us, event | category | flops | bytes accessed | tf_op | source)
XLA Modules:
  0.0 87.8 jit_solution(9981820032577134341)
XLA Ops:
  0.0 0.9 %slice.3 = bf16[2,8,2560]{2,1,0:T(8,128)(2,1)S(1)} slice(bf16[2,512,2560]{2,1,0:T(8,128)(2,1)} %param.10), slice={[0:2], [504:512], [0:2560]} | slice | bytes 163840 | tf_op jit(solution)/shard_map/slice | solution.py:365
  0.9 0.9 %copy-done.8 = bf16[2560,32]{0,1:T(8,128)(2,1)S(1)} copy-done((bf16[2560,32]{0,1:T(8,128)(2,1)S(1)}, bf16[2560,32]{0,1:T(8,128)(2,1)}, u32[]{:S(2)}) %copy-start.8) | copy-done | bytes 163864
  1.8 0.9 %copy-done.9 = bf16[2560,10]{0,1:T(8,128)(2,1)S(1)} copy-done((bf16[2560,10]{0,1:T(8,128)(2,1)S(1)}, bf16[2560,10]{0,1:T(8,128)(2,1)}, u32[]{:S(2)}) %copy-start.9) | copy-done | bytes 51224
  2.7 0.1 pad_add_fusion.place
  2.8 4.8 %collective-permute-start = (bf16[2,8,2560]{2,1,0:T(8,128)(2,1)S(1)}, bf16[2,8,2560]{2,1,0:T(8,128)(2,1)S(1)}, u32[]{:S(2)}, u32[]{:S(2)}) collective-permute-start(bf16[2,8,2560]{2,1,0:T(8,128)(2,1)S(1)} %slice.3), channel_id=1, source_target_pairs={{0,8},{8,16},{16,24},{24,32},{32,40},{40,48},{48,56},{56,64},{64,7... | collective-permute-start | bytes 245768 | tf_op jit(solution)/shard_map/ppermute | solution.py:367
  7.6 1.6 %shard_map.101 = (bf16[32,1024]{1,0:T(8,128)(2,1)S(1)}, f32[1024,128]{1,0:T(8,128)S(1)}) custom-call(bf16[1024,2560]{1,0:T(8,128)(2,1)S(1)} %bitcast.9, bf16[48,2560]{1,0:T(8,128)(2,1)S(1)} %shard_map.100.joined.weight), custom_call_target="tpu_custom_call" | custom-call | flops 503316480 | tf_op jit(solution)/shard_map/pallas_call | solution.py:368
  9.2 0.0 copy-start.1
  9.2 0.0 copy-start.3
  9.2 0.0 copy-start.6
  9.2 0.0 copy-start.7
  9.3 0.2 shard_map.102.refs_0_
  9.5 5.6 %collective-permute-start.2 = (bf16[32,1152]{1,0:T(8,128)(2,1)S(1)}, bf16[32,1152]{1,0:T(8,128)(2,1)S(1)}, u32[]{:S(2)}, u32[]{:S(2)}) collective-permute-start(bf16[32,1152]{1,0:T(8,128)(2,1)S(1)} %shard_map.102.refs_0_), channel_id=1, source_target_pairs={{0,7},{1,0},{2,1},{3,2},{4,3},{5,4},{6,5},{7,6},{8,15},{9,8},{10,9... | collective-permute-start | bytes 221192 | tf_op jit(solution)/shard_map/ppermute | solution.py:408
  15.1 3.8 %shard_map.103 = (bf16[512,640]{1,0:T(8,128)(2,1)S(1)}, f32[512,128]{1,0:T(8,128)S(1)}, f32[8,640]{1,0:T(8,128)S(1)}, bf16[8,128]{1,0:T(8,128)(2,1)S(1)}) custom-call(f32[10]{0:T(128)S(1)} %copy-done.6, f32[10]{0:T(128)S(1)} %copy-done.7, bf16[1024,2560]{1,0:T(8,128)(2,1)S(1)} %bitcast.10, bf16[16,2560]{1,0:T(8,128)(2,1)S(1)} %bitcast.15, ...), custom_call_target="tpu_custom_call" | custom-call | flops 1677721600 | tf_op jit(solution)/shard_map/pallas_call | solution.py:383
  18.9 1.4 %collective-permute-done.1.refs_1_ = bf16[32,1152]{1,0:T(8,128)(2,1)S(1)} collective-permute-done((bf16[32,1152]{1,0:T(8,128)(2,1)S(1)}, bf16[32,1152]{1,0:T(8,128)(2,1)S(1)}, u32[]{:S(2)}, u32[]{:S(2)}) %collective-permute-start.1) | collective-permute-done | bytes 73760 | tf_op jit(solution)/shard_map/ppermute | solution.py:409
  20.3 2.7 %collective-permute-start.4 = (bf16[32,1152]{1,0:T(8,128)(2,1)S(1)}, bf16[32,1152]{1,0:T(8,128)(2,1)S(1)}, u32[]{:S(2)}, u32[]{:S(2)}) collective-permute-start(bf16[32,1152]{1,0:T(8,128)(2,1)S(1)} %collective-permute-done.2.refs_2_), channel_id=1, source_target_pairs={{0,7},{1,0},{2,1},{3,2},{4,3},{5,4},{6,5},{7,6},{8,15},{9,8},{10,9... | collective-permute-start | bytes 221192 | tf_op jit(solution)/shard_map/ppermute | solution.py:408
  23.0 3.8 %shard_map.104 = (bf16[512,640]{1,0:T(8,128)(2,1)S(1)}, f32[512,128]{1,0:T(8,128)S(1)}, f32[8,640]{1,0:T(8,128)S(1)}, bf16[8,128]{1,0:T(8,128)(2,1)S(1)}) custom-call(f32[10]{0:T(128)S(1)} %copy-done.6, f32[10]{0:T(128)S(1)} %copy-done.7, bf16[1024,2560]{1,0:T(8,128)(2,1)S(1)} %bitcast.11, bf16[16,2560]{1,0:T(8,128)(2,1)S(1)} %bitcast.16, ...), custom_call_target="tpu_custom_call" | custom-call | flops 1677721600 | tf_op jit(solution)/shard_map/pallas_call | solution.py:383
  26.8 0.1 collective-permute-start.5
  26.9 2.7 %collective-permute-start.6 = (bf16[32,1152]{1,0:T(8,128)(2,1)S(1)}, bf16[32,1152]{1,0:T(8,128)(2,1)S(1)}, u32[]{:S(2)}, u32[]{:S(2)}) collective-permute-start(bf16[32,1152]{1,0:T(8,128)(2,1)S(1)} %collective-permute-done.4.refs_4_), channel_id=1, source_target_pairs={{0,7},{1,0},{2,1},{3,2},{4,3},{5,4},{6,5},{7,6},{8,15},{9,8},{10,9... | collective-permute-start | bytes 221192 | tf_op jit(solution)/shard_map/ppermute | solution.py:408
  29.5 1.7 %collective-permute-done.5.refs_5_ = bf16[32,1152]{1,0:T(8,128)(2,1)S(1)} collective-permute-done((bf16[32,1152]{1,0:T(8,128)(2,1)S(1)}, bf16[32,1152]{1,0:T(8,128)(2,1)S(1)}, u32[]{:S(2)}, u32[]{:S(2)}) %collective-permute-start.5) | collective-permute-done | bytes 73760 | tf_op jit(solution)/shard_map/ppermute | solution.py:409
  31.3 0.0 collective-permute-start.7
  31.3 4.4 %collective-permute-done.7.refs_7_ = bf16[32,1152]{1,0:T(8,128)(2,1)S(1)} collective-permute-done((bf16[32,1152]{1,0:T(8,128)(2,1)S(1)}, bf16[32,1152]{1,0:T(8,128)(2,1)S(1)}, u32[]{:S(2)}, u32[]{:S(2)}) %collective-permute-start.7) | collective-permute-done | bytes 73760 | tf_op jit(solution)/shard_map/ppermute | solution.py:409
  35.7 2.7 %shard_map.105 = (bf16[2,128,512]{2,1,0:T(8,128)(2,1)S(1)}, bf16[1024,128]{1,0:T(8,128)(2,1)S(1)}, bf16[8,128,640]{2,1,0:T(8,128)(2,1)S(1)}, bf16[16,8,768]{2,1,0:T(8,128)(2,1)S(1)}, bf16[16,8,768]{2,1,0:T(8,128)(2,1)S(1)}) custom-call(s32[4]{0:T(128)S(1)} %pad_add_fusion.place, f32[4,256]{1,0:T(4,128)S(1)} %copy-done.4, ...), custom_call_target="tpu_custom_call" | custom-call | tf_op jit(solution)/shard_map/pallas_call | solution.py:427
  38.4 3.3 %collective-permute-start.8 = (bf16[16,8,768]{2,1,0:T(8,128)(2,1)S(1)}, bf16[16,8,768]{2,1,0:T(8,128)(2,1)S(1)}, u32[]{:S(2)}, u32[]{:S(2)}) collective-permute-start(bf16[16,8,768]{2,1,0:T(8,128)(2,1)S(1)} %get-tuple-element.81), channel_id=1, source_target_pairs={{0,8},{8,0},{16,24},{24,16},{32,40},{40,32},{48,56},{56,48},{64,72... | collective-permute-start | bytes 589832 | tf_op jit(solution)/shard_map/ppermute | solution.py:442
  41.8 1.1 %collective-permute-done.8.got = bf16[16,8,768]{2,1,0:T(8,128)(2,1)S(1)} collective-permute-done((bf16[16,8,768]{2,1,0:T(8,128)(2,1)S(1)}, bf16[16,8,768]{2,1,0:T(8,128)(2,1)S(1)}, u32[]{:S(2)}, u32[]{:S(2)}) %collective-permute-start.8) | collective-permute-done | bytes 196640 | tf_op jit(solution)/shard_map/ppermute | solution.py:442
  42.8 0.7 shard_map.106
  43.6 2.6 %collective-permute-start.9 = (bf16[4,8,768]{2,1,0:T(8,128)(2,1)S(1)}, bf16[4,8,768]{2,1,0:T(8,128)(2,1)S(1)}, u32[]{:S(2)}, u32[]{:S(2)}) collective-permute-start(bf16[4,8,768]{2,1,0:T(8,128)(2,1)S(1)} %get-tuple-element.83), channel_id=1, source_target_pairs={{0,16},{8,24},{16,32},{24,40},{32,48},{40,56},{48,0},{56,8},{64,80... | collective-permute-start | bytes 147464 | tf_op jit(solution)/shard_map/ppermute | solution.py:447
  46.2 2.5 %collective-permute-start.10 = (bf16[4,8,768]{2,1,0:T(8,128)(2,1)S(1)}, bf16[4,8,768]{2,1,0:T(8,128)(2,1)S(1)}, u32[]{:S(2)}, u32[]{:S(2)}) collective-permute-start(bf16[4,8,768]{2,1,0:T(8,128)(2,1)S(1)} %get-tuple-element.84), channel_id=1, source_target_pairs={{0,32},{8,40},{16,48},{24,56},{32,0},{40,8},{48,16},{56,24},{64,96... | collective-permute-start | bytes 147464 | tf_op jit(solution)/shard_map/ppermute | solution.py:447
  48.6 1.3 %collective-permute-start.11 = (bf16[4,8,768]{2,1,0:T(8,128)(2,1)S(1)}, bf16[4,8,768]{2,1,0:T(8,128)(2,1)S(1)}, u32[]{:S(2)}, u32[]{:S(2)}) collective-permute-start(bf16[4,8,768]{2,1,0:T(8,128)(2,1)S(1)} %get-tuple-element.85), channel_id=1, source_target_pairs={{0,48},{8,56},{16,0},{24,8},{32,16},{40,24},{48,32},{56,40},{64,11... | collective-permute-start | bytes 147464 | tf_op jit(solution)/shard_map/ppermute | solution.py:447
  50.0 2.4 %shard_map.107.refs_0_ = bf16[512,640]{1,0:T(8,128)(2,1)S(1)} custom-call(bf16[1024,2560]{1,0:T(8,128)(2,1)S(1)} %bitcast.12, bf16[2560,640]{1,0:T(8,128)(2,1)S(1)} %copy-done.2, f32[512,128]{1,0:T(8,128)S(1)} %get-tuple-element.88.opening), custom_call_target="tpu_custom_call" | custom-call | flops 1677721600 | tf_op jit(solution)/shard_map/pallas_call | solution.py:398
  52.4 0.7 shard_map.108
  53.2 3.3 %collective-permute-start.14 = (bf16[4,8,768]{2,1,0:T(8,128)(2,1)S(1)}, bf16[4,8,768]{2,1,0:T(8,128)(2,1)S(1)}, u32[]{:S(2)}, u32[]{:S(2)}) collective-permute-start(bf16[4,8,768]{2,1,0:T(8,128)(2,1)S(1)} %get-tuple-element.96), channel_id=1, source_target_pairs={{0,192},{8,200},{16,208},{24,216},{32,224},{40,232},{48,240},{56,2... | collective-permute-start | bytes 147464 | tf_op jit(solution)/shard_map/ppermute | solution.py:447
  56.5 0.4 collective-permute-start.13
  56.8 0.7 collective-permute-start.12
  57.5 1.5 %shard_map.109.within = f32[1024,640]{1,0:T(8,128)S(1)} custom-call(bf16[2,128,512]{2,1,0:T(8,128)(2,1)S(1)} %get-tuple-element.97.b_rows, bf16[1024,128]{1,0:T(8,128)(2,1)S(1)} %get-tuple-element.98.c_rows, bf16[8,128,640]{2,1,0:T(8,128)(2,1)S(1)} %get-tuple-element.99.starts, bf16[512,640]{1,0:T(8,128)(2,1)S(1)} %get-tuple-element.74.refs_8_.refs_0_, ...), custom_call_target="tpu_custom_call" | custom-call | flops 419430400 | tf_op jit(solution)/shard_map/pallas_call | solution.py:478
  59.0 1.9 %collective-permute-done.13.refs_1_ = bf16[4,8,768]{2,1,0:T(8,128)(2,1)S(1)} collective-permute-done((bf16[4,8,768]{2,1,0:T(8,128)(2,1)S(1)}, bf16[4,8,768]{2,1,0:T(8,128)(2,1)S(1)}, u32[]{:S(2)}, u32[]{:S(2)}) %collective-permute-start.13) | collective-permute-done | bytes 49184 | tf_op jit(solution)/shard_map/ppermute | solution.py:447
  60.9 0.5 collective-permute-done.12.refs_0_
  61.4 0.8 shard_map.110
  62.2 0.9 %collective-permute-start.15 = (bf16[4,8,640]{2,1,0:T(8,128)(2,1)S(1)}, bf16[4,8,640]{2,1,0:T(8,128)(2,1)S(1)}, u32[]{:S(2)}, u32[]{:S(2)}) collective-permute-start(bf16[4,8,640]{2,1,0:T(8,128)(2,1)S(1)} %get-tuple-element.104), channel_id=1, source_target_pairs={{0,16},{8,24},{16,32},{24,40},{32,48},{40,56},{48,0},{56,8},{64,80... | collective-permute-start | bytes 122888 | tf_op jit(solution)/shard_map/ppermute | solution.py:447
  63.2 2.1 %collective-permute-start.16 = (bf16[4,8,640]{2,1,0:T(8,128)(2,1)S(1)}, bf16[4,8,640]{2,1,0:T(8,128)(2,1)S(1)}, u32[]{:S(2)}, u32[]{:S(2)}) collective-permute-start(bf16[4,8,640]{2,1,0:T(8,128)(2,1)S(1)} %get-tuple-element.105), channel_id=1, source_target_pairs={{0,32},{8,40},{16,48},{24,56},{32,0},{40,8},{48,16},{56,24},{64,96... | collective-permute-start | bytes 122888 | tf_op jit(solution)/shard_map/ppermute | solution.py:447
  65.3 1.0 %collective-permute-start.17 = (bf16[4,8,640]{2,1,0:T(8,128)(2,1)S(1)}, bf16[4,8,640]{2,1,0:T(8,128)(2,1)S(1)}, u32[]{:S(2)}, u32[]{:S(2)}) collective-permute-start(bf16[4,8,640]{2,1,0:T(8,128)(2,1)S(1)} %get-tuple-element.106), channel_id=1, source_target_pairs={{0,48},{8,56},{16,0},{24,8},{32,16},{40,24},{48,32},{56,40},{64,11... | collective-permute-start | bytes 122888 | tf_op jit(solution)/shard_map/ppermute | solution.py:447
  66.3 2.4 %shard_map.111.refs_1_ = bf16[512,640]{1,0:T(8,128)(2,1)S(1)} custom-call(bf16[1024,2560]{1,0:T(8,128)(2,1)S(1)} %bitcast.13, bf16[2560,640]{1,0:T(8,128)(2,1)S(1)} %copy-done.2, f32[512,128]{1,0:T(8,128)S(1)} %get-tuple-element.108.opening), custom_call_target="tpu_custom_call" | custom-call | flops 1677721600 | tf_op jit(solution)/shard_map/pallas_call | solution.py:398
  68.8 0.0 copy-start.5
  68.8 0.8 shard_map.112
  69.6 4.6 %collective-permute-start.18 = (bf16[128,640]{1,0:T(8,128)(2,1)S(1)}, bf16[128,640]{1,0:T(8,128)(2,1)S(1)}, u32[]{:S(2)}, u32[]{:S(2)}) collective-permute-start(bf16[128,640]{1,0:T(8,128)(2,1)S(1)} %get-tuple-element.113), channel_id=1, source_target_pairs={{0,8},{8,0},{16,24},{24,16},{32,40},{40,32},{48,56},{56,48},{64,72... | collective-permute-start | bytes 491528 | tf_op jit(solution)/shard_map/ppermute | solution.py:442
  74.2 1.0 %collective-permute-done.18.taken = bf16[128,640]{1,0:T(8,128)(2,1)S(1)} collective-permute-done((bf16[128,640]{1,0:T(8,128)(2,1)S(1)}, bf16[128,640]{1,0:T(8,128)(2,1)S(1)}, u32[]{:S(2)}, u32[]{:S(2)}) %collective-permute-start.18) | collective-permute-done | bytes 163872 | tf_op jit(solution)/shard_map/ppermute | solution.py:442
  75.2 1.9 %shard_map.113 = (f32[1024,640]{1,0:T(8,128)S(1)}, f32[8,8,128]{2,1,0:T(8,128)S(1)}) custom-call(s32[4]{0:T(128)S(1)} %pad_add_fusion.place, bf16[128,640]{1,0:T(8,128)(2,1)S(1)} %get-tuple-element.112.own, bf16[128,640]{1,0:T(8,128)(2,1)S(1)} %collective-permute-done.18.taken, f32[1024,640]{1,0:T(8,128)S(1)} %shard_map.109.within, ...), custom_call_target="tpu_custom_call" | custom-call | tf_op jit(solution)/shard_map/pallas_call | solution.py:500
  77.1 9.3 %all_to_all.5.squares = f32[8,8,128]{2,1,0:T(8,128)S(1)} all-to-all(f32[8,8,128]{2,1,0:T(8,128)S(1)} %get-tuple-element.118), channel_id=1, replica_groups=mesh['seq'=32,'tp'=8] {'tp'}, dimensions={0} | all-to-all | bytes 65536 | tf_op jit(solution)/shard_map/all_to_all | solution.py:507
  86.4 1.5 %shard_map.114 = bf16[1024,640]{1,0:T(8,128)(2,1)} custom-call(f32[1024,640]{1,0:T(8,128)S(1)} %get-tuple-element.117.gated, f32[8,8,128]{2,1,0:T(8,128)S(1)} %all_to_all.5.squares, f32[640]{0:T(1024)S(1)} %copy-done.5), custom_call_target="tpu_custom_call" | custom-call | tf_op jit(solution)/shard_map/pallas_call | solution.py:508
  (28 shorter events, 0.1 us)
Async XLA Ops:
  0.9 0.9 %copy-start.8 = (bf16[2560,32]{0,1:T(8,128)(2,1)S(1)}, bf16[2560,32]{0,1:T(8,128)(2,1)}, u32[]{:S(2)}) copy-start(bf16[2560,32]{0,1:T(8,128)(2,1)} %param.13) | copy-start | bytes 491524
  1.8 0.9 %copy-start.9 = (bf16[2560,10]{0,1:T(8,128)(2,1)S(1)}, bf16[2560,10]{0,1:T(8,128)(2,1)}, u32[]{:S(2)}) copy-start(bf16[2560,10]{0,1:T(8,128)(2,1)} %param.14) | copy-start | bytes 153604
  2.7 4.9 %copy-start = (bf16[2,512,2560]{2,1,0:T(8,128)(2,1)S(1)}, bf16[2,512,2560]{2,1,0:T(8,128)(2,1)}, u32[]{:S(2)}) copy-start(bf16[2,512,2560]{2,1,0:T(8,128)(2,1)} %param.10) | copy-start | bytes 15728644
  2.8 6.4 %collective-permute-start = (bf16[2,8,2560]{2,1,0:T(8,128)(2,1)S(1)}, bf16[2,8,2560]{2,1,0:T(8,128)(2,1)S(1)}, u32[]{:S(2)}, u32[]{:S(2)}) collective-permute-start(bf16[2,8,2560]{2,1,0:T(8,128)(2,1)S(1)} %slice.3), channel_id=1, source_target_pairs={{0,8},{8,16},{16,24},{24,32},{32,40},{40,48},{48,56},{56,64},{64,7... | collective-permute-start | bytes 245768 | tf_op jit(solution)/shard_map/ppermute | solution.py:367
  9.2 5.9 %copy-start.1 = (bf16[2560,640]{1,0:T(8,128)(2,1)S(1)}, bf16[2560,640]{1,0:T(8,128)(2,1)}, u32[]{:S(2)}) copy-start(bf16[2560,640]{1,0:T(8,128)(2,1)} %weight.5) | copy-start | bytes 9830404
  9.2 5.9 %copy-start.3 = (f32[4,640]{1,0:T(4,128)S(1)}, f32[4,640]{1,0:T(4,128)}, u32[]{:S(2)}) copy-start(f32[4,640]{1,0:T(4,128)} %taps.4) | copy-start | bytes 30724
  9.2 5.9 %copy-start.6 = (f32[10]{0:T(128)S(1)}, f32[10]{0:T(128)}, u32[]{:S(2)}) copy-start(f32[10]{0:T(128)} %step_bias.3) | copy-start | bytes 124
  9.2 5.9 %copy-start.7 = (f32[10]{0:T(128)S(1)}, f32[10]{0:T(128)}, u32[]{:S(2)}) copy-start(f32[10]{0:T(128)} %log_rate.3) | copy-start | bytes 124
  9.5 9.5 %collective-permute-start.2 = (bf16[32,1152]{1,0:T(8,128)(2,1)S(1)}, bf16[32,1152]{1,0:T(8,128)(2,1)S(1)}, u32[]{:S(2)}, u32[]{:S(2)}) collective-permute-start(bf16[32,1152]{1,0:T(8,128)(2,1)S(1)} %shard_map.102.refs_0_), channel_id=1, source_target_pairs={{0,7},{1,0},{2,1},{3,2},{4,3},{5,4},{6,5},{7,6},{8,15},{9,8},{10,9... | collective-permute-start | bytes 221192 | tf_op jit(solution)/shard_map/ppermute | solution.py:408
  15.1 5.2 %collective-permute-start.1 = (bf16[32,1152]{1,0:T(8,128)(2,1)S(1)}, bf16[32,1152]{1,0:T(8,128)(2,1)S(1)}, u32[]{:S(2)}, u32[]{:S(2)}) collective-permute-start(bf16[32,1152]{1,0:T(8,128)(2,1)S(1)} %shard_map.102.refs_0_), channel_id=1, source_target_pairs={{0,1},{1,2},{2,3},{3,4},{4,5},{5,6},{6,7},{7,0},{8,9},{9,10},{10,1... | collective-permute-start | bytes 221192 | tf_op jit(solution)/shard_map/ppermute | solution.py:409
  20.3 15.4 %copy-start.4 = (f32[4,256]{1,0:T(4,128)S(1)}, f32[4,256]{1,0:T(4,128)}, u32[]{:S(2)}) copy-start(f32[4,256]{1,0:T(4,128)} %taps.5) | copy-start | bytes 12292
  20.3 6.5 %collective-permute-start.3 = (bf16[32,1152]{1,0:T(8,128)(2,1)S(1)}, bf16[32,1152]{1,0:T(8,128)(2,1)S(1)}, u32[]{:S(2)}, u32[]{:S(2)}) collective-permute-start(bf16[32,1152]{1,0:T(8,128)(2,1)S(1)} %collective-permute-done.1.refs_1_), channel_id=1, source_target_pairs={{0,1},{1,2},{2,3},{3,4},{4,5},{5,6},{6,7},{7,0},{8,9},{9,10},{10,1... | collective-permute-start | bytes 221192 | tf_op jit(solution)/shard_map/ppermute | solution.py:409
  20.3 6.5 %collective-permute-start.4 = (bf16[32,1152]{1,0:T(8,128)(2,1)S(1)}, bf16[32,1152]{1,0:T(8,128)(2,1)S(1)}, u32[]{:S(2)}, u32[]{:S(2)}) collective-permute-start(bf16[32,1152]{1,0:T(8,128)(2,1)S(1)} %collective-permute-done.2.refs_2_), channel_id=1, source_target_pairs={{0,7},{1,0},{2,1},{3,2},{4,3},{5,4},{6,5},{7,6},{8,15},{9,8},{10,9... | collective-permute-start | bytes 221192 | tf_op jit(solution)/shard_map/ppermute | solution.py:408
  23.0 27.0 %copy-start.2 = (bf16[2560,640]{1,0:T(8,128)(2,1)S(1)}, bf16[2560,640]{1,0:T(8,128)(2,1)}, u32[]{:S(2)}) copy-start(bf16[2560,640]{1,0:T(8,128)(2,1)} %weight.7) | copy-start | bytes 9830404
  26.8 4.5 %collective-permute-start.5 = (bf16[32,1152]{1,0:T(8,128)(2,1)S(1)}, bf16[32,1152]{1,0:T(8,128)(2,1)S(1)}, u32[]{:S(2)}, u32[]{:S(2)}) collective-permute-start(bf16[32,1152]{1,0:T(8,128)(2,1)S(1)} %collective-permute-done.3.refs_3_), channel_id=1, source_target_pairs={{0,1},{1,2},{2,3},{3,4},{4,5},{5,6},{6,7},{7,0},{8,9},{9,10},{10,1... | collective-permute-start | bytes 221192 | tf_op jit(solution)/shard_map/ppermute | solution.py:409
  26.9 4.4 %collective-permute-start.6 = (bf16[32,1152]{1,0:T(8,128)(2,1)S(1)}, bf16[32,1152]{1,0:T(8,128)(2,1)S(1)}, u32[]{:S(2)}, u32[]{:S(2)}) collective-permute-start(bf16[32,1152]{1,0:T(8,128)(2,1)S(1)} %collective-permute-done.4.refs_4_), channel_id=1, source_target_pairs={{0,7},{1,0},{2,1},{3,2},{4,3},{5,4},{6,5},{7,6},{8,15},{9,8},{10,9... | collective-permute-start | bytes 221192 | tf_op jit(solution)/shard_map/ppermute | solution.py:408
  31.3 4.4 %collective-permute-start.7 = (bf16[32,1152]{1,0:T(8,128)(2,1)S(1)}, bf16[32,1152]{1,0:T(8,128)(2,1)S(1)}, u32[]{:S(2)}, u32[]{:S(2)}) collective-permute-start(bf16[32,1152]{1,0:T(8,128)(2,1)S(1)} %collective-permute-done.5.refs_5_), channel_id=1, source_target_pairs={{0,1},{1,2},{2,3},{3,4},{4,5},{5,6},{6,7},{7,0},{8,9},{9,10},{10,1... | collective-permute-start | bytes 221192 | tf_op jit(solution)/shard_map/ppermute | solution.py:409
  38.4 4.4 %collective-permute-start.8 = (bf16[16,8,768]{2,1,0:T(8,128)(2,1)S(1)}, bf16[16,8,768]{2,1,0:T(8,128)(2,1)S(1)}, u32[]{:S(2)}, u32[]{:S(2)}) collective-permute-start(bf16[16,8,768]{2,1,0:T(8,128)(2,1)S(1)} %get-tuple-element.81), channel_id=1, source_target_pairs={{0,8},{8,0},{16,24},{24,16},{32,40},{40,32},{48,56},{56,48},{64,72... | collective-permute-start | bytes 589832 | tf_op jit(solution)/shard_map/ppermute | solution.py:442
  43.6 8.8 %collective-permute-start.9 = (bf16[4,8,768]{2,1,0:T(8,128)(2,1)S(1)}, bf16[4,8,768]{2,1,0:T(8,128)(2,1)S(1)}, u32[]{:S(2)}, u32[]{:S(2)}) collective-permute-start(bf16[4,8,768]{2,1,0:T(8,128)(2,1)S(1)} %get-tuple-element.83), channel_id=1, source_target_pairs={{0,16},{8,24},{16,32},{24,40},{32,48},{40,56},{48,0},{56,8},{64,80... | collective-permute-start | bytes 147464 | tf_op jit(solution)/shard_map/ppermute | solution.py:447
  46.2 6.2 %collective-permute-start.10 = (bf16[4,8,768]{2,1,0:T(8,128)(2,1)S(1)}, bf16[4,8,768]{2,1,0:T(8,128)(2,1)S(1)}, u32[]{:S(2)}, u32[]{:S(2)}) collective-permute-start(bf16[4,8,768]{2,1,0:T(8,128)(2,1)S(1)} %get-tuple-element.84), channel_id=1, source_target_pairs={{0,32},{8,40},{16,48},{24,56},{32,0},{40,8},{48,16},{56,24},{64,96... | collective-permute-start | bytes 147464 | tf_op jit(solution)/shard_map/ppermute | solution.py:447
  48.6 3.8 %collective-permute-start.11 = (bf16[4,8,768]{2,1,0:T(8,128)(2,1)S(1)}, bf16[4,8,768]{2,1,0:T(8,128)(2,1)S(1)}, u32[]{:S(2)}, u32[]{:S(2)}) collective-permute-start(bf16[4,8,768]{2,1,0:T(8,128)(2,1)S(1)} %get-tuple-element.85), channel_id=1, source_target_pairs={{0,48},{8,56},{16,0},{24,8},{32,16},{40,24},{48,32},{56,40},{64,11... | collective-permute-start | bytes 147464 | tf_op jit(solution)/shard_map/ppermute | solution.py:447
  53.2 5.8 %collective-permute-start.14 = (bf16[4,8,768]{2,1,0:T(8,128)(2,1)S(1)}, bf16[4,8,768]{2,1,0:T(8,128)(2,1)S(1)}, u32[]{:S(2)}, u32[]{:S(2)}) collective-permute-start(bf16[4,8,768]{2,1,0:T(8,128)(2,1)S(1)} %get-tuple-element.96), channel_id=1, source_target_pairs={{0,192},{8,200},{16,208},{24,216},{32,224},{40,232},{48,240},{56,2... | collective-permute-start | bytes 147464 | tf_op jit(solution)/shard_map/ppermute | solution.py:447
  56.5 4.4 %collective-permute-start.13 = (bf16[4,8,768]{2,1,0:T(8,128)(2,1)S(1)}, bf16[4,8,768]{2,1,0:T(8,128)(2,1)S(1)}, u32[]{:S(2)}, u32[]{:S(2)}) collective-permute-start(bf16[4,8,768]{2,1,0:T(8,128)(2,1)S(1)} %get-tuple-element.96), channel_id=1, source_target_pairs={{0,128},{8,136},{16,144},{24,152},{32,160},{40,168},{48,176},{56,1... | collective-permute-start | bytes 147464 | tf_op jit(solution)/shard_map/ppermute | solution.py:447
  56.8 4.6 %collective-permute-start.12 = (bf16[4,8,768]{2,1,0:T(8,128)(2,1)S(1)}, bf16[4,8,768]{2,1,0:T(8,128)(2,1)S(1)}, u32[]{:S(2)}, u32[]{:S(2)}) collective-permute-start(bf16[4,8,768]{2,1,0:T(8,128)(2,1)S(1)} %get-tuple-element.96), channel_id=1, source_target_pairs={{0,64},{8,72},{16,80},{24,88},{32,96},{40,104},{48,112},{56,120},{... | collective-permute-start | bytes 147464 | tf_op jit(solution)/shard_map/ppermute | solution.py:447
  62.2 6.6 %collective-permute-start.15 = (bf16[4,8,640]{2,1,0:T(8,128)(2,1)S(1)}, bf16[4,8,640]{2,1,0:T(8,128)(2,1)S(1)}, u32[]{:S(2)}, u32[]{:S(2)}) collective-permute-start(bf16[4,8,640]{2,1,0:T(8,128)(2,1)S(1)} %get-tuple-element.104), channel_id=1, source_target_pairs={{0,16},{8,24},{16,32},{24,40},{32,48},{40,56},{48,0},{56,8},{64,80... | collective-permute-start | bytes 122888 | tf_op jit(solution)/shard_map/ppermute | solution.py:447
  63.2 5.7 %collective-permute-start.16 = (bf16[4,8,640]{2,1,0:T(8,128)(2,1)S(1)}, bf16[4,8,640]{2,1,0:T(8,128)(2,1)S(1)}, u32[]{:S(2)}, u32[]{:S(2)}) collective-permute-start(bf16[4,8,640]{2,1,0:T(8,128)(2,1)S(1)} %get-tuple-element.105), channel_id=1, source_target_pairs={{0,32},{8,40},{16,48},{24,56},{32,0},{40,8},{48,16},{56,24},{64,96... | collective-permute-start | bytes 122888 | tf_op jit(solution)/shard_map/ppermute | solution.py:447
  65.3 3.5 %collective-permute-start.17 = (bf16[4,8,640]{2,1,0:T(8,128)(2,1)S(1)}, bf16[4,8,640]{2,1,0:T(8,128)(2,1)S(1)}, u32[]{:S(2)}, u32[]{:S(2)}) collective-permute-start(bf16[4,8,640]{2,1,0:T(8,128)(2,1)S(1)} %get-tuple-element.106), channel_id=1, source_target_pairs={{0,48},{8,56},{16,0},{24,8},{32,16},{40,24},{48,32},{56,40},{64,11... | collective-permute-start | bytes 122888 | tf_op jit(solution)/shard_map/ppermute | solution.py:447
  68.8 17.6 %copy-start.5 = (f32[640]{0:T(1024)S(1)}, f32[640]{0:T(1024)}, u32[]{:S(2)}) copy-start(f32[640]{0:T(1024)} %gain.1) | copy-start | bytes 7684
  69.6 5.6 %collective-permute-start.18 = (bf16[128,640]{1,0:T(8,128)(2,1)S(1)}, bf16[128,640]{1,0:T(8,128)(2,1)S(1)}, u32[]{:S(2)}, u32[]{:S(2)}) collective-permute-start(bf16[128,640]{1,0:T(8,128)(2,1)S(1)} %get-tuple-element.113), channel_id=1, source_target_pairs={{0,8},{8,0},{16,24},{24,16},{32,40},{40,32},{48,56},{56,48},{64,72... | collective-permute-start | bytes 491528 | tf_op jit(solution)/shard_map/ppermute | solution.py:442

commit v8 on v5

--- a/solution.py
+++ b/solution.py
@@ -51,6 +51,11 @@
 def over_channels(x, spread):
     high, middle, _ = split_in_three(x)
     return dot(jnp.concatenate([high, middle], axis=1), spread)
+
+
+def tail_kernel(batch, length, hidden, out):
+    for b in range(batch):
+        out[8 * b : 8 * b + 8, :] = hidden[(b + 1) * length - 8 : (b + 1) * length, :]
 
 
 def bc_kernel(chunk, hidden, weight, step_weight, out, steps, pad, joined):
@@ -255,8 +260,13 @@
     step_weight = step_proj.T
     place = lax.axis_index("tp").reshape(1)
     smem = pl.BlockSpec(memory_space=pltpu.SMEM)
-    tail = hidden_in[:, length - 8 :, :]
-    halo = lax.ppermute(tail, "seq", [(i, i + 1) for i in range(seq - 1)]).reshape(8 * batch, width)
+    hidden, place = lax.optimization_barrier((hidden, place))
+    tail = call(
+        functools.partial(tail_kernel, batch, length),
+        [((8 * batch, width), BF16)],
+        flops=1 * tokens * width * share,
+    )(hidden)
+    halo = lax.ppermute(tail, "seq", [(i, i + 1) for i in range(seq - 1)])
     own, step_pre = call(
         functools.partial(bc_kernel, 256),
         [((share, tokens), BF16), ((tokens, LANES), F32)],

time: 87.1 us -> 85.9 us (0.986)
  local copies, waits for them, and re-layouts: 5.23 us -> 2.55 us
  blocking collectives: 42.4 us -> 43.8 us
    unnamed x24, local copies, waits for them, and re-layouts: 4.33 us -> 2.55 us
    all_to_all x1, blocking collectives: 20.1 us -> 21.5 us  [on_device(): lax.all_to_all(sent.reshape(seq, -1, inner + LANES), 'seq', 0, 0, tiled=T...]
    slice x1 -> x0, local copies, waits for them, and re-layouts: 0.89 us -> none  [on_device(): tail = hidden_in[:, length - 8:, :]]
where the time goes in v8:
time: 85.9 us; the launch traced here: 85.6 us
  blocking collectives  43.8 us (51%)
  Pallas kernels  20.4 us (24%)
  starting transfers between devices  15.8 us (18%)
  waiting for transfers between devices  2.79 us (3%)
  local copies, waits for them, and re-layouts  2.55 us (3%)
    all_to_all x1, blocking collectives, on_device(): lax.all_to_all(sent.reshape(seq, -1, inner + LANES), 'seq', 0, 0, tiled=T...  21.5 us
    all_to_all x1, blocking collectives, on_device(): lax.all_to_all(prefix, 'seq', 0, 0, tiled=True).reshape(batch, STATE, inner)  13 us
    ppermute x3, starting transfers between devices, on_device(): to_left = lax.ppermute(right, 'tp', down) if 2 * r + 2 < tp else right  11 us
    all_to_all x1, blocking collectives, on_device(): whole = lax.all_to_all(squares, 'tp', 0, 0, tiled=True)  9.32 us
    pallas_call x2, Pallas kernels, value_of(): call(functools.partial(value_kernel, b, length, heads), [((length, inner)...  7.57 us
    pallas_call x2, Pallas kernels, gate_of(): call(functools.partial(gate_kernel, b, length), [((length, inner), BF16)]...  4.86 us
    ppermute x1, starting transfers between devices, on_device(): halo = lax.ppermute(tail, 'seq', [(i, i + 1) for i in range(seq - 1)])  4.64 us
    ppermute x4, waiting for transfers between devices, on_device(): to_right = lax.ppermute(left, 'tp', up)  2.78 us
  transfers between devices with their start and end apart: 8, of which 2 were waited for; matrix products, arithmetic and copies ran while one was open for 0% of the time, Pallas kernels for 16%

profile of v8, /device:TPU:1, one launch (start us, length us, event | category | flops | bytes accessed | tf_op | source)
XLA Modules:
  0.0 85.6 jit_solution(2424755586123104493)
XLA Ops:
  0.0 2.5 %copy-done = bf16[2,512,2560]{2,1,0:T(8,128)(2,1)S(1)} copy-done((bf16[2,512,2560]{2,1,0:T(8,128)(2,1)S(1)}, bf16[2,512,2560]{2,1,0:T(8,128)(2,1)}, u32[]{:S(2)}) %copy-start) | copy-done | bytes 5242904
  2.5 4.6 %collective-permute-start = (bf16[16,2560]{1,0:T(8,128)(2,1)S(1)}, bf16[16,2560]{1,0:T(8,128)(2,1)S(1)}, u32[]{:S(2)}, u32[]{:S(2)}) collective-permute-start(bf16[16,2560]{1,0:T(8,128)(2,1)S(1)} %shard_map.100), channel_id=1, source_target_pairs={{0,8},{8,16},{16,24},{24,32},{32,40},{40,48},{48,56},{56,64},{64,7... | collective-permute-start | bytes 245768 | tf_op jit(solution)/shard_map/ppermute | solution.py:269
  7.1 0.0 copy-done.3
  7.2 0.0 copy-done.4
  7.2 0.0 slice-start
  7.2 1.6 %shard_map.101 = (bf16[32,1024]{1,0:T(8,128)(2,1)S(1)}, f32[1024,128]{1,0:T(8,128)S(1)}) custom-call(bf16[1024,2560]{1,0:T(8,128)(2,1)S(1)} %bitcast.8, bf16[32,2560]{1,0:T(8,128)(2,1)S(1)} %bitcast.17, bf16[10,2560]{1,0:T(8,128)(2,1)S(1)} %bitcast.19), custom_call_target="tpu_custom_call" | custom-call | flops 503316480 | tf_op jit(solution)/shard_map/pallas_call | solution.py:270
  8.8 0.0 collective-permute-done.halo
  8.8 0.0 slice-start.1
  8.8 0.0 copy-start.1
  8.8 0.0 copy-start.5
  8.9 0.0 copy-start.8
  8.9 0.0 copy-start.9
  8.9 0.2 shard_map.102.refs_0_
  9.1 5.6 %collective-permute-start.2 = (bf16[32,1152]{1,0:T(8,128)(2,1)S(1)}, bf16[32,1152]{1,0:T(8,128)(2,1)S(1)}, u32[]{:S(2)}, u32[]{:S(2)}) collective-permute-start(bf16[32,1152]{1,0:T(8,128)(2,1)S(1)} %shard_map.102.refs_0_), channel_id=1, source_target_pairs={{0,7},{1,0},{2,1},{3,2},{4,3},{5,4},{6,5},{7,6},{8,15},{9,8},{10,9... | collective-permute-start | bytes 221192 | tf_op jit(solution)/shard_map/ppermute | solution.py:310
  14.7 0.0 collective-permute-start.1
  14.7 0.0 slice-done
  14.7 0.0 slice-done.1
  14.7 0.0 copy-done.1
  14.7 0.0 copy-done.5
  14.8 0.0 copy-done.8
  14.8 0.0 copy-done.9
  14.8 3.8 %shard_map.103 = (bf16[512,640]{1,0:T(8,128)(2,1)S(1)}, f32[512,128]{1,0:T(8,128)S(1)}, f32[8,640]{1,0:T(8,128)S(1)}, bf16[8,128]{1,0:T(8,128)(2,1)S(1)}) custom-call(f32[10]{0:T(128)S(1)} %copy-done.8, f32[10]{0:T(128)S(1)} %copy-done.9, bf16[1024,2560]{1,0:T(8,128)(2,1)S(1)} %bitcast.11, bf16[16,2560]{1,0:T(8,128)(2,1)S(1)} %collective-permute-done.halo, ...), custom_call_target="tpu_custom_call" | custom-call | flops 1677721600 | tf_op jit(solution)/shard_map/pallas_call | solution.py:285
  18.6 0.0 collective-permute-done.2.refs_2_
  18.6 0.8 collective-permute-done.1.refs_1_
  19.4 0.0 collective-permute-start.3
  19.4 2.7 %collective-permute-start.4 = (bf16[32,1152]{1,0:T(8,128)(2,1)S(1)}, bf16[32,1152]{1,0:T(8,128)(2,1)S(1)}, u32[]{:S(2)}, u32[]{:S(2)}) collective-permute-start(bf16[32,1152]{1,0:T(8,128)(2,1)S(1)} %collective-permute-done.2.refs_2_), channel_id=1, source_target_pairs={{0,7},{1,0},{2,1},{3,2},{4,3},{5,4},{6,5},{7,6},{8,15},{9,8},{10,9... | collective-permute-start | bytes 221192 | tf_op jit(solution)/shard_map/ppermute | solution.py:310
  22.1 3.8 %shard_map.104 = (bf16[512,640]{1,0:T(8,128)(2,1)S(1)}, f32[512,128]{1,0:T(8,128)S(1)}, f32[8,640]{1,0:T(8,128)S(1)}, bf16[8,128]{1,0:T(8,128)(2,1)S(1)}) custom-call(f32[10]{0:T(128)S(1)} %copy-done.8, f32[10]{0:T(128)S(1)} %copy-done.9, bf16[1024,2560]{1,0:T(8,128)(2,1)S(1)} %bitcast.12, bf16[16,2560]{1,0:T(8,128)(2,1)S(1)} %collective-permute-done.halo, ...), custom_call_target="tpu_custom_call" | custom-call | flops 1677721600 | tf_op jit(solution)/shard_map/pallas_call | solution.py:285
  25.9 0.0 collective-permute-done.3.refs_3_
  25.9 0.0 collective-permute-done.4.refs_4_
  25.9 0.1 collective-permute-start.5
  26.0 2.7 %collective-permute-start.6 = (bf16[32,1152]{1,0:T(8,128)(2,1)S(1)}, bf16[32,1152]{1,0:T(8,128)(2,1)S(1)}, u32[]{:S(2)}, u32[]{:S(2)}) collective-permute-start(bf16[32,1152]{1,0:T(8,128)(2,1)S(1)} %collective-permute-done.4.refs_4_), channel_id=1, source_target_pairs={{0,7},{1,0},{2,1},{3,2},{4,3},{5,4},{6,5},{7,6},{8,15},{9,8},{10,9... | collective-permute-start | bytes 221192 | tf_op jit(solution)/shard_map/ppermute | solution.py:310
  28.7 0.0 copy-done.2
  28.7 2.4 %shard_map.105.refs_2_ = bf16[512,640]{1,0:T(8,128)(2,1)S(1)} custom-call(bf16[1024,2560]{1,0:T(8,128)(2,1)S(1)} %bitcast.13, bf16[2560,640]{1,0:T(8,128)(2,1)S(1)} %copy-done.2, f32[512,128]{1,0:T(8,128)S(1)} %get-tuple-element.49.opening), custom_call_target="tpu_custom_call" | custom-call | flops 1677721600 | tf_op jit(solution)/shard_map/pallas_call | solution.py:300
  31.1 0.0 collective-permute-done.5.refs_5_
  31.1 0.0 collective-permute-done.6.refs_6_
  31.1 0.1 collective-permute-start.7
  31.2 0.0 copy-start.6
  31.2 2.4 %shard_map.106.refs_3_ = bf16[512,640]{1,0:T(8,128)(2,1)S(1)} custom-call(bf16[1024,2560]{1,0:T(8,128)(2,1)S(1)} %bitcast.14, bf16[2560,640]{1,0:T(8,128)(2,1)S(1)} %copy-done.2, f32[512,128]{1,0:T(8,128)S(1)} %get-tuple-element.53.opening), custom_call_target="tpu_custom_call" | custom-call | flops 1677721600 | tf_op jit(solution)/shard_map/pallas_call | solution.py:300
  33.7 2.0 %collective-permute-done.7.refs_7_ = bf16[32,1152]{1,0:T(8,128)(2,1)S(1)} collective-permute-done((bf16[32,1152]{1,0:T(8,128)(2,1)S(1)}, bf16[32,1152]{1,0:T(8,128)(2,1)S(1)}, u32[]{:S(2)}, u32[]{:S(2)}) %collective-permute-start.7) | collective-permute-done | bytes 73760 | tf_op jit(solution)/shard_map/ppermute | solution.py:311
  35.6 0.0 copy-done.6
  35.6 2.2 %shard_map.107 = (bf16[2,128,512]{2,1,0:T(8,128)(2,1)S(1)}, bf16[1024,128]{1,0:T(8,128)(2,1)S(1)}, bf16[8,128,640]{2,1,0:T(8,128)(2,1)S(1)}, bf16[2,16,8,768]{3,2,1,0:T(8,128)(2,1)S(1)}) custom-call(s32[1]{0:T(128)} %bitcast.1.place, f32[4,256]{1,0:T(4,128)S(1)} %copy-done.6, bf16[32,1152]{1,0:T(8,128)(2,1)S(1)} %shard_map.102.refs_0_, ...), custom_call_target="tpu_custom_call" | custom-call | tf_op jit(solution)/shard_map/pallas_call | solution.py:330
  37.8 21.5 %all_to_all.15.got = bf16[32,8,768]{2,1,0:T(8,128)(2,1)S(1)} all-to-all(bf16[32,8,768]{2,1,0:T(8,128)(2,1)S(1)} %bitcast.16), channel_id=1, replica_groups=mesh['seq'=32,'tp'=8] {'seq'}, dimensions={0} | all-to-all | bytes 786432 | tf_op jit(solution)/shard_map/all_to_all | solution.py:342
  59.3 0.3 shard_map.108
  59.6 13.0 %all_to_all.16 = bf16[32,8,640]{2,1,0:T(8,128)(2,1)S(1)} all-to-all(bf16[32,8,640]{2,1,0:T(8,128)(2,1)S(1)} %shard_map.108), channel_id=1, replica_groups=mesh['seq'=32,'tp'=8] {'seq'}, dimensions={0} | all-to-all | bytes 655360 | tf_op jit(solution)/shard_map/all_to_all | solution.py:348
  72.6 2.3 %shard_map.109 = (f32[1024,640]{1,0:T(8,128)S(1)}, f32[8,8,128]{2,1,0:T(8,128)S(1)}) custom-call(bf16[2,128,640]{2,1,0:T(8,128)(2,1)S(1)} %bitcast.15, bf16[2,128,512]{2,1,0:T(8,128)(2,1)S(1)} %get-tuple-element.62.b_rows, bf16[1024,128]{1,0:T(8,128)(2,1)S(1)} %get-tuple-element.63.c_rows, bf16[8,128,640]{2,1,0:T(8,128)(2,1)S(1)} %get-tuple-element.64.starts, ...), custom_call_target="tpu_custom_call" | custom-call | tf_op jit(solution)/shard_map/pallas_call | solution.py:349
  74.8 9.3 %all_to_all.17.squares = f32[8,8,128]{2,1,0:T(8,128)S(1)} all-to-all(f32[8,8,128]{2,1,0:T(8,128)S(1)} %get-tuple-element.68), channel_id=1, replica_groups=mesh['seq'=32,'tp'=8] {'tp'}, dimensions={0} | all-to-all | bytes 65536 | tf_op jit(solution)/shard_map/all_to_all | solution.py:353
  84.2 0.0 copy-done.7
  84.2 1.4 %shard_map.110 = bf16[1024,640]{1,0:T(8,128)(2,1)} custom-call(f32[1024,640]{1,0:T(8,128)S(1)} %get-tuple-element.67.gated, f32[8,8,128]{2,1,0:T(8,128)S(1)} %all_to_all.17.squares, f32[640]{0:T(1024)S(1)} %copy-done.7), custom_call_target="tpu_custom_call" | custom-call | tf_op jit(solution)/shard_map/pallas_call | solution.py:354
  (7 shorter events, 0.0 us)
Async XLA Ops:
  0.0 2.5 %copy-start = (bf16[2,512,2560]{2,1,0:T(8,128)(2,1)S(1)}, bf16[2,512,2560]{2,1,0:T(8,128)(2,1)}, u32[]{:S(2)}) copy-start(bf16[2,512,2560]{2,1,0:T(8,128)(2,1)} %param.10) | copy-start | bytes 15728644
  2.5 4.7 %copy-start.3 = (bf16[2560,32]{0,1:T(8,128)(2,1)S(1)}, bf16[2560,32]{0,1:T(8,128)(2,1)}, u32[]{:S(2)}) copy-start(bf16[2560,32]{0,1:T(8,128)(2,1)} %param.13) | copy-start | bytes 491524
  2.5 4.7 %copy-start.4 = (bf16[2560,10]{0,1:T(8,128)(2,1)S(1)}, bf16[2560,10]{0,1:T(8,128)(2,1)}, u32[]{:S(2)}) copy-start(bf16[2560,10]{0,1:T(8,128)(2,1)} %param.14) | copy-start | bytes 153604
  2.5 6.3 %collective-permute-start = (bf16[16,2560]{1,0:T(8,128)(2,1)S(1)}, bf16[16,2560]{1,0:T(8,128)(2,1)S(1)}, u32[]{:S(2)}, u32[]{:S(2)}) collective-permute-start(bf16[16,2560]{1,0:T(8,128)(2,1)S(1)} %shard_map.100), channel_id=1, source_target_pairs={{0,8},{8,16},{16,24},{24,32},{32,40},{40,48},{48,56},{56,64},{64,7... | collective-permute-start | bytes 245768 | tf_op jit(solution)/shard_map/ppermute | solution.py:269
  7.2 7.6 %slice-start = ((s8[5242880]{0:T(1024)(128)(4,1)}), s8[4194304]{0:T(1024)(128)(4,1)S(1)}, s32[]{:S(2)}) async-start(s8[5242880]{0:T(1024)(128)(4,1)} %bitcast.9), calls=%async_computation.3 | async-start | bytes 8388608
  8.8 5.9 %slice-start.1 = ((s8[5242880]{0:T(1024)(128)(4,1)}), s8[1048576]{0:T(1024)(128)(4,1)S(1)}, s32[]{:S(2)}) async-start(s8[5242880]{0:T(1024)(128)(4,1)} %bitcast.9), calls=%async_computation.4 | async-start | bytes 2097152
  8.8 5.9 %copy-start.1 = (bf16[2560,640]{1,0:T(8,128)(2,1)S(1)}, bf16[2560,640]{1,0:T(8,128)(2,1)}, u32[]{:S(2)}) copy-start(bf16[2560,640]{1,0:T(8,128)(2,1)} %weight.5) | copy-start | bytes 9830404
  8.8 5.9 %copy-start.5 = (f32[4,640]{1,0:T(4,128)S(1)}, f32[4,640]{1,0:T(4,128)}, u32[]{:S(2)}) copy-start(f32[4,640]{1,0:T(4,128)} %taps.4) | copy-start | bytes 30724
  8.9 5.9 %copy-start.8 = (f32[10]{0:T(128)S(1)}, f32[10]{0:T(128)}, u32[]{:S(2)}) copy-start(f32[10]{0:T(128)} %step_bias.3) | copy-start | bytes 124
  8.9 5.9 %copy-start.9 = (f32[10]{0:T(128)S(1)}, f32[10]{0:T(128)}, u32[]{:S(2)}) copy-start(f32[10]{0:T(128)} %log_rate.3) | copy-start | bytes 124
  9.1 9.5 %collective-permute-start.2 = (bf16[32,1152]{1,0:T(8,128)(2,1)S(1)}, bf16[32,1152]{1,0:T(8,128)(2,1)S(1)}, u32[]{:S(2)}, u32[]{:S(2)}) collective-permute-start(bf16[32,1152]{1,0:T(8,128)(2,1)S(1)} %shard_map.102.refs_0_), channel_id=1, source_target_pairs={{0,7},{1,0},{2,1},{3,2},{4,3},{5,4},{6,5},{7,6},{8,15},{9,8},{10,9... | collective-permute-start | bytes 221192 | tf_op jit(solution)/shard_map/ppermute | solution.py:310
  14.7 4.7 %collective-permute-start.1 = (bf16[32,1152]{1,0:T(8,128)(2,1)S(1)}, bf16[32,1152]{1,0:T(8,128)(2,1)S(1)}, u32[]{:S(2)}, u32[]{:S(2)}) collective-permute-start(bf16[32,1152]{1,0:T(8,128)(2,1)S(1)} %shard_map.102.refs_0_), channel_id=1, source_target_pairs={{0,1},{1,2},{2,3},{3,4},{4,5},{5,6},{6,7},{7,0},{8,9},{9,10},{10,1... | collective-permute-start | bytes 221192 | tf_op jit(solution)/shard_map/ppermute | solution.py:311
  19.4 9.2 %copy-start.2 = (bf16[2560,640]{1,0:T(8,128)(2,1)S(1)}, bf16[2560,640]{1,0:T(8,128)(2,1)}, u32[]{:S(2)}) copy-start(bf16[2560,640]{1,0:T(8,128)(2,1)} %weight.7) | copy-start | bytes 9830404
  19.4 6.5 %collective-permute-start.3 = (bf16[32,1152]{1,0:T(8,128)(2,1)S(1)}, bf16[32,1152]{1,0:T(8,128)(2,1)S(1)}, u32[]{:S(2)}, u32[]{:S(2)}) collective-permute-start(bf16[32,1152]{1,0:T(8,128)(2,1)S(1)} %collective-permute-done.1.refs_1_), channel_id=1, source_target_pairs={{0,1},{1,2},{2,3},{3,4},{4,5},{5,6},{6,7},{7,0},{8,9},{9,10},{10,1... | collective-permute-start | bytes 221192 | tf_op jit(solution)/shard_map/ppermute | solution.py:311
  19.4 6.5 %collective-permute-start.4 = (bf16[32,1152]{1,0:T(8,128)(2,1)S(1)}, bf16[32,1152]{1,0:T(8,128)(2,1)S(1)}, u32[]{:S(2)}, u32[]{:S(2)}) collective-permute-start(bf16[32,1152]{1,0:T(8,128)(2,1)S(1)} %collective-permute-done.2.refs_2_), channel_id=1, source_target_pairs={{0,7},{1,0},{2,1},{3,2},{4,3},{5,4},{6,5},{7,6},{8,15},{9,8},{10,9... | collective-permute-start | bytes 221192 | tf_op jit(solution)/shard_map/ppermute | solution.py:310
  25.9 5.2 %collective-permute-start.5 = (bf16[32,1152]{1,0:T(8,128)(2,1)S(1)}, bf16[32,1152]{1,0:T(8,128)(2,1)S(1)}, u32[]{:S(2)}, u32[]{:S(2)}) collective-permute-start(bf16[32,1152]{1,0:T(8,128)(2,1)S(1)} %collective-permute-done.3.refs_3_), channel_id=1, source_target_pairs={{0,1},{1,2},{2,3},{3,4},{4,5},{5,6},{6,7},{7,0},{8,9},{9,10},{10,1... | collective-permute-start | bytes 221192 | tf_op jit(solution)/shard_map/ppermute | solution.py:311
  26.0 5.1 %collective-permute-start.6 = (bf16[32,1152]{1,0:T(8,128)(2,1)S(1)}, bf16[32,1152]{1,0:T(8,128)(2,1)S(1)}, u32[]{:S(2)}, u32[]{:S(2)}) collective-permute-start(bf16[32,1152]{1,0:T(8,128)(2,1)S(1)} %collective-permute-done.4.refs_4_), channel_id=1, source_target_pairs={{0,7},{1,0},{2,1},{3,2},{4,3},{5,4},{6,5},{7,6},{8,15},{9,8},{10,9... | collective-permute-start | bytes 221192 | tf_op jit(solution)/shard_map/ppermute | solution.py:310
  31.1 4.5 %collective-permute-start.7 = (bf16[32,1152]{1,0:T(8,128)(2,1)S(1)}, bf16[32,1152]{1,0:T(8,128)(2,1)S(1)}, u32[]{:S(2)}, u32[]{:S(2)}) collective-permute-start(bf16[32,1152]{1,0:T(8,128)(2,1)S(1)} %collective-permute-done.5.refs_5_), channel_id=1, source_target_pairs={{0,1},{1,2},{2,3},{3,4},{4,5},{5,6},{6,7},{7,0},{8,9},{9,10},{10,1... | collective-permute-start | bytes 221192 | tf_op jit(solution)/shard_map/ppermute | solution.py:311
  31.2 4.4 %copy-start.6 = (f32[4,256]{1,0:T(4,128)S(1)}, f32[4,256]{1,0:T(4,128)}, u32[]{:S(2)}) copy-start(f32[4,256]{1,0:T(4,128)} %taps.5) | copy-start | bytes 12292
  59.3 24.9 %copy-start.7 = (f32[640]{0:T(1024)S(1)}, f32[640]{0:T(1024)}, u32[]{:S(2)}) copy-start(f32[640]{0:T(1024)} %gain.1) | copy-start | bytes 7684
